TPU v7x, 32 devices: a whole 2x2x4 slice. The times are simulated.
32 devices in a mesh: dp: 4 (over x, core), fsdp: 8 (over z, y).
Axes of the slice: x: 2, y: 2, z: 4, core: 2. Of those that a mesh axis runs over, the one named last changes fastest.
Arguments:
- text_rows: bfloat16 [64, 512, 768], P(('dp', 'fsdp')), may hold values from -6 to 6
- visual_matrix: bfloat16 [768, 768], P('fsdp'), may hold values from -0.21875 to 0.21875
- batch_gain: bfloat16 [768], P('fsdp'), may hold values from 0.5 to 1.5
- batch_shift: bfloat16 [768], P('fsdp'), may hold values from -2.5 to 2.5
- attend_weight: bfloat16 [768, 2304], P('fsdp'), may hold values from -0.21875 to 0.21875
- merge_weight: bfloat16 [768, 768], P('fsdp'), may hold values from -1.75 to 1.75
- first_gain: bfloat16 [768], P('fsdp'), may hold values from 0.5 to 1.5
- first_shift: bfloat16 [768], P('fsdp'), may hold values from -2.5 to 2.5
- up_matrix: bfloat16 [768, 3072], P('fsdp'), may hold values from -0.21875 to 0.21875
- down_matrix: bfloat16 [3072, 768], P('fsdp'), may hold values from -0.109375 to 0.109375
- second_gain: bfloat16 [768], P('fsdp'), may hold values from 0.5 to 1.5
- second_shift: bfloat16 [768], P('fsdp'), may hold values from -2.5 to 2.5
- segment_counts: int32 [64], P(('dp', 'fsdp')), may hold values from 5 to 128, as said below
- segment_ids: int32 [64, 512], P(('dp', 'fsdp')), may hold values from -1 to 127, as said below
- padding_mask: int32 [64, 512], P(('dp', 'fsdp')), may hold values from 0 to 1, as said below
- cotangent: bfloat16 [64, 512, 768], P(('dp', 'fsdp')), may hold values from -6 to 6
Outputs:
- layer_output: float32 [64, 512, 768], P(('dp', 'fsdp'))
- text_gradient: float32 [64, 512, 768], P(('dp', 'fsdp'))
- visual_gradient: float32 [768, 768], P('fsdp')
- batch_gain_gradient: float32 [768], P('fsdp')
- batch_shift_gradient: float32 [768], P('fsdp')
- attend_gradient: float32 [768, 2304], P('fsdp')
- merge_gradient: float32 [768, 768], P('fsdp')
- first_gain_gradient: float32 [768], P('fsdp')
- first_shift_gradient: float32 [768], P('fsdp')
- up_gradient: float32 [768, 3072], P('fsdp')
- down_gradient: float32 [3072, 768], P('fsdp')
- second_gain_gradient: float32 [768], P('fsdp')
- second_shift_gradient: float32 [768], P('fsdp')
Inputs may be any that keep to these rules, and one draw needn't show every extreme that they name: On every device of dp+fsdp one of its documents has exactly 128 segments; segment_counts[d] is one more than the largest segment_ids in document d. `segment_ids`: A document's real rows come first and form segment_counts consecutive runs of one or more rows, numbered 0, 1, ... in order; padding rows hold -1. `padding_mask`: 1 exactly on the rows whose segment id is not -1, which are the first 256 or more rows of a document.
All inputs are finite; a program needn't handle non-finite values.
Results may differ from a plain program's by a relative error of at most 0.023.
The roundings to bfloat16 on the way count: a program that leaves them out, or rounds other values in their place, can miss the bound.
Values may be sent and summed in bfloat16 or wider, within the bound.
No kernel may reach another device: no remote copies, remote signals or barrier semaphores. Data moves between devices by JAX's collectives and lax.ppermute only.
A program may use at most 192 MiB of HBM per device.

v0:
```python
import jax
import jax.numpy as jnp
from jax import lax
from jax.sharding import PartitionSpec as P

HEADS = 12
SEGMAX = 128


eps_norm = 1e-05
eps_batch = 1e-05
masked_score = -1e30
highest_precision = lax.Precision.HIGHEST


def layer_norm(values, gain, shift):
    center = values - jnp.mean(values, axis=-1, keepdims=True)
    variance = jnp.mean(center * center, axis=-1, keepdims=True)
    return center * lax.rsqrt(variance + eps_norm) * gain + shift


def exact_gelu(values):
    return jax.nn.gelu(values, approximate=False)


def split_heads(packed):
    length = packed.shape[0]
    features = packed.shape[1] // 3
    head_size = features // HEADS
    queries = packed[:, :features].reshape(length, HEADS, head_size)
    keys_part = packed[:, features : 2 * features].reshape(length, HEADS, head_size)
    values_part = packed[:, 2 * features :].reshape(length, HEADS, head_size)
    return (queries, keys_part, values_part, head_size ** (-0.5))


def masked_scores(queries, keys_part, key_mask, scaling):
    scores = (
        jnp.einsum("qhe,khe->hqk", queries, keys_part, preferred_element_type=jnp.float32) * scaling
    )
    return jnp.where(key_mask[None, None, :] > 0, scores, masked_score)


def attend_doc(operands):
    packed, key_mask = operands
    queries, keys_part, values_part, scaling = split_heads(packed)
    scores = masked_scores(queries, keys_part, key_mask, scaling)
    top_score = jnp.max(scores, axis=-1, keepdims=True)
    unnormed = jnp.exp(scores - top_score)
    totals = jnp.sum(unnormed, axis=-1, keepdims=True)
    attention = unnormed / totals
    mixed = jnp.einsum(
        "hqk,khe->qhe",
        attention.astype(jnp.bfloat16),
        values_part,
        preferred_element_type=jnp.float32,
    )
    log_total = (top_score + jnp.log(totals))[..., 0]
    return (mixed.reshape(packed.shape[0], packed.shape[1] // 3).astype(jnp.bfloat16), log_total)


def attend_back(operands):
    packed, key_mask, log_total, delta_attended = operands
    queries, keys_part, values_part, scaling = split_heads(packed)
    length = packed.shape[0]
    features = packed.shape[1] // 3
    scores = masked_scores(queries, keys_part, key_mask, scaling)
    attention = jnp.exp(scores - log_total[..., None])
    delta_heads = delta_attended.reshape(length, HEADS, features // HEADS)
    delta_attention = jnp.einsum(
        "qhe,khe->hqk", delta_heads, values_part, preferred_element_type=jnp.float32
    )
    delta_scores = attention * (
        delta_attention - jnp.sum(attention * delta_attention, axis=-1, keepdims=True)
    )
    delta_low = delta_scores.astype(jnp.bfloat16)
    delta_queries = (
        jnp.einsum("hqk,khe->qhe", delta_low, keys_part, preferred_element_type=jnp.float32)
        * scaling
    )
    delta_keys = (
        jnp.einsum("hqk,qhe->khe", delta_low, queries, preferred_element_type=jnp.float32) * scaling
    )
    delta_values = jnp.einsum(
        "hqk,qhe->khe",
        attention.astype(jnp.bfloat16),
        delta_heads,
        preferred_element_type=jnp.float32,
    )
    merged = jnp.concatenate(
        [
            delta_queries.reshape(length, features),
            delta_keys.reshape(length, features),
            delta_values.reshape(length, features),
        ],
        axis=1,
    )
    return merged.astype(jnp.bfloat16)


def shards(
    text_rows,
    visual_matrix,
    batch_gain,
    batch_shift,
    attend_weight,
    merge_weight,
    first_gain,
    first_shift,
    up_matrix,
    down_matrix,
    second_gain,
    second_shift,
    segment_counts,
    segment_ids,
    padding_mask,
    cotangent,
):
    gathered = (
        lax.all_gather(visual_matrix, "fsdp", axis=0, tiled=True),
        lax.all_gather(batch_gain, "fsdp", axis=0, tiled=True),
        lax.all_gather(batch_shift, "fsdp", axis=0, tiled=True),
        lax.all_gather(attend_weight, "fsdp", axis=0, tiled=True),
        lax.all_gather(merge_weight, "fsdp", axis=0, tiled=True),
        lax.all_gather(first_gain, "fsdp", axis=0, tiled=True),
        lax.all_gather(first_shift, "fsdp", axis=0, tiled=True),
        lax.all_gather(up_matrix, "fsdp", axis=0, tiled=True),
        lax.all_gather(down_matrix, "fsdp", axis=0, tiled=True),
        lax.all_gather(second_gain, "fsdp", axis=0, tiled=True),
        lax.all_gather(second_shift, "fsdp", axis=0, tiled=True),
    )
    (
        gathered_visual_weight,
        full_batch_gain,
        full_batch_shift,
        full_attend,
        full_merge,
        full_first_gain,
        full_first_shift,
        gathered_up_weight,
        gathered_down_weight,
        full_second_gain,
        full_second_shift,
    ) = gathered
    features = text_rows.shape[2]
    slot_index = jnp.arange(SEGMAX)
    matches = segment_ids[:, :, None] == slot_index[None, None, :]
    onehot = matches.astype(jnp.bfloat16)
    onehot_wide = matches.astype(jnp.float32)
    divisor = jnp.maximum(jnp.sum(onehot_wide, axis=1), 1.0)[..., None]
    pooled_segments = (
        jnp.einsum("drs,drc->dsc", onehot, text_rows, preferred_element_type=jnp.float32) / divisor
    ).astype(jnp.bfloat16)
    visual_rows = jnp.einsum(
        "bil,ly->biy", pooled_segments, gathered_visual_weight, preferred_element_type=jnp.float32
    )
    valid_slot = (slot_index[None, :] < segment_counts[:, None]).astype(jnp.float32)[..., None]
    local_count = jnp.sum(segment_counts).astype(jnp.float32)
    masked_visual = valid_slot * visual_rows
    segment_total, visual_sum = lax.psum(
        (local_count, jnp.sum(masked_visual, axis=(0, 1))), ("dp", "fsdp")
    )
    batch_center = visual_sum / segment_total
    center = visual_rows - batch_center
    variance = (
        lax.psum(jnp.sum(valid_slot * center * center, axis=(0, 1)), ("dp", "fsdp")) / segment_total
    )
    inverse_spread = lax.rsqrt(variance + eps_batch)
    normed = center * inverse_spread
    embedded = (
        normed * full_batch_gain.astype(jnp.float32) + full_batch_shift.astype(jnp.float32)
    ).astype(jnp.bfloat16)
    joined = text_rows.astype(jnp.float32) + jnp.einsum(
        "drs,dsc->drc", onehot, embedded, preferred_element_type=jnp.float32
    )
    joined_low = joined.astype(jnp.bfloat16)
    packed = jnp.einsum(
        "drc,ce->dre", joined_low, full_attend, preferred_element_type=jnp.float32
    ).astype(jnp.bfloat16)
    attended, log_total = lax.map(attend_doc, (packed, padding_mask))
    projected = jnp.einsum("drc,ce->dre", attended, full_merge, preferred_element_type=jnp.float32)
    pre_one = joined + projected
    hidden_state = layer_norm(
        pre_one, full_first_gain.astype(jnp.float32), full_first_shift.astype(jnp.float32)
    )
    hidden_reduced_precision = hidden_state.astype(jnp.bfloat16)
    inner_hidden = jnp.einsum(
        "sjq,qy->sjy",
        hidden_reduced_precision,
        gathered_up_weight,
        preferred_element_type=jnp.float32,
    )
    gelu_activated = exact_gelu(inner_hidden).astype(jnp.bfloat16)
    residual_branch = jnp.einsum(
        "zya,av->zyv", gelu_activated, gathered_down_weight, preferred_element_type=jnp.float32
    )
    pre_two = hidden_state + residual_branch
    layer_output = layer_norm(
        pre_two, full_second_gain.astype(jnp.float32), full_second_shift.astype(jnp.float32)
    )
    again = (
        lax.all_gather(visual_matrix, "fsdp", axis=0, tiled=True),
        lax.all_gather(batch_gain, "fsdp", axis=0, tiled=True),
        lax.all_gather(attend_weight, "fsdp", axis=0, tiled=True),
        lax.all_gather(merge_weight, "fsdp", axis=0, tiled=True),
        lax.all_gather(first_gain, "fsdp", axis=0, tiled=True),
        lax.all_gather(up_matrix, "fsdp", axis=0, tiled=True),
        lax.all_gather(down_matrix, "fsdp", axis=0, tiled=True),
        lax.all_gather(second_gain, "fsdp", axis=0, tiled=True),
    )
    (
        visual_pullback,
        back_batch_gain,
        back_attend,
        back_merge,
        back_first_gain,
        up_pullback,
        down_pullback,
        back_second_gain,
    ) = again
    second_back = jax.vjp(
        layer_norm,
        pre_two,
        back_second_gain.astype(jnp.float32),
        full_second_shift.astype(jnp.float32),
    )[1]
    delta_two, second_gain_local, second_shift_local = second_back(cotangent.astype(jnp.float32))
    branch_gradient = delta_two.astype(jnp.bfloat16)
    down_local = jnp.einsum(
        "omt,oms->ts", gelu_activated, branch_gradient, preferred_element_type=jnp.float32
    )
    delta_activated = jnp.einsum(
        "ivj,hj->ivh", branch_gradient, down_pullback, preferred_element_type=jnp.float32
    )
    gelu_back = jax.vjp(exact_gelu, inner_hidden)[1]
    inner_gradient = gelu_back(delta_activated)[0].astype(jnp.bfloat16)
    up_local = jnp.einsum(
        "oih,oiu->hu", hidden_reduced_precision, inner_gradient, preferred_element_type=jnp.float32
    )
    delta_hidden = delta_two + jnp.einsum(
        "wmx,ix->wmi", inner_gradient, up_pullback, preferred_element_type=jnp.float32
    )
    first_back = jax.vjp(
        layer_norm,
        pre_one,
        back_first_gain.astype(jnp.float32),
        full_first_shift.astype(jnp.float32),
    )[1]
    delta_one, first_gain_local, first_shift_local = first_back(delta_hidden)
    delta_projected = delta_one.astype(jnp.bfloat16)
    merge_local = jnp.einsum(
        "drc,dre->ce", attended, delta_projected, preferred_element_type=jnp.float32
    )
    delta_attended = jnp.einsum(
        "dre,ce->drc", delta_projected, back_merge, preferred_element_type=jnp.float32
    ).astype(jnp.bfloat16)
    delta_packed = lax.map(attend_back, (packed, padding_mask, log_total, delta_attended))
    attend_local = jnp.einsum(
        "drc,dre->ce", joined_low, delta_packed, preferred_element_type=jnp.float32
    )
    delta_joined = delta_one + jnp.einsum(
        "dre,ce->drc", delta_packed, back_attend, preferred_element_type=jnp.float32
    )
    delta_embedded = jnp.einsum(
        "drs,drc->dsc",
        onehot_wide,
        delta_joined,
        precision=highest_precision,
        preferred_element_type=jnp.float32,
    )
    shift_total, gain_total = lax.psum(
        (jnp.sum(delta_embedded, axis=(0, 1)), jnp.sum(delta_embedded * normed, axis=(0, 1))),
        ("dp", "fsdp"),
    )
    visual_delta_rows = (
        valid_slot
        * back_batch_gain.astype(jnp.float32)
        * inverse_spread
        * (delta_embedded - shift_total / segment_total - normed * gain_total / segment_total)
    ).astype(jnp.bfloat16)
    visual_local = jnp.einsum(
        "bli,blz->iz", pooled_segments, visual_delta_rows, preferred_element_type=jnp.float32
    )
    delta_pooled = (
        jnp.einsum(
            "zbl,wl->zbw", visual_delta_rows, visual_pullback, preferred_element_type=jnp.float32
        )
        / divisor
    )
    text_gradient = delta_joined + jnp.einsum(
        "drs,dsc->drc",
        onehot_wide,
        delta_pooled,
        precision=highest_precision,
        preferred_element_type=jnp.float32,
    )
    (
        visual_shard,
        attend_shard,
        merge_shard,
        first_gain_shard,
        first_shift_shard,
        up_shard,
        down_shard,
        second_gain_shard,
        second_shift_shard,
    ) = (
        lax.psum_scatter(
            visual_local.astype(jnp.bfloat16), "fsdp", scatter_dimension=0, tiled=True
        ).astype(jnp.float32),
        lax.psum_scatter(
            attend_local.astype(jnp.bfloat16), "fsdp", scatter_dimension=0, tiled=True
        ).astype(jnp.float32),
        lax.psum_scatter(
            merge_local.astype(jnp.bfloat16), "fsdp", scatter_dimension=0, tiled=True
        ).astype(jnp.float32),
        lax.psum_scatter(
            first_gain_local.astype(jnp.bfloat16), "fsdp", scatter_dimension=0, tiled=True
        ).astype(jnp.float32),
        lax.psum_scatter(
            first_shift_local.astype(jnp.bfloat16), "fsdp", scatter_dimension=0, tiled=True
        ).astype(jnp.float32),
        lax.psum_scatter(
            up_local.astype(jnp.bfloat16), "fsdp", scatter_dimension=0, tiled=True
        ).astype(jnp.float32),
        lax.psum_scatter(
            down_local.astype(jnp.bfloat16), "fsdp", scatter_dimension=0, tiled=True
        ).astype(jnp.float32),
        lax.psum_scatter(
            second_gain_local.astype(jnp.bfloat16), "fsdp", scatter_dimension=0, tiled=True
        ).astype(jnp.float32),
        lax.psum_scatter(
            second_shift_local.astype(jnp.bfloat16), "fsdp", scatter_dimension=0, tiled=True
        ).astype(jnp.float32),
    )
    summed = (
        lax.psum(visual_shard.astype(jnp.bfloat16), "dp").astype(jnp.float32),
        lax.psum(attend_shard.astype(jnp.bfloat16), "dp").astype(jnp.float32),
        lax.psum(merge_shard.astype(jnp.bfloat16), "dp").astype(jnp.float32),
        lax.psum(first_gain_shard.astype(jnp.bfloat16), "dp").astype(jnp.float32),
        lax.psum(first_shift_shard.astype(jnp.bfloat16), "dp").astype(jnp.float32),
        lax.psum(up_shard.astype(jnp.bfloat16), "dp").astype(jnp.float32),
        lax.psum(down_shard.astype(jnp.bfloat16), "dp").astype(jnp.float32),
        lax.psum(second_gain_shard.astype(jnp.bfloat16), "dp").astype(jnp.float32),
        lax.psum(second_shift_shard.astype(jnp.bfloat16), "dp").astype(jnp.float32),
    )
    (
        visual_gradient,
        attend_gradient,
        merge_gradient,
        first_gain_gradient,
        first_shift_gradient,
        up_gradient,
        down_gradient,
        second_gain_gradient,
        second_shift_gradient,
    ) = summed
    piece = features // lax.axis_size("fsdp")
    start = lax.axis_index("fsdp") * piece
    batch_gain_gradient = lax.dynamic_slice_in_dim(gain_total, start, piece, 0)
    batch_shift_gradient = lax.dynamic_slice_in_dim(shift_total, start, piece, 0)
    return (
        layer_output,
        text_gradient,
        visual_gradient,
        batch_gain_gradient,
        batch_shift_gradient,
        attend_gradient,
        merge_gradient,
        first_gain_gradient,
        first_shift_gradient,
        up_gradient,
        down_gradient,
        second_gain_gradient,
        second_shift_gradient,
    )


def solution(mesh):
    in_specs = (
        P(("dp", "fsdp"), None, None),
        P("fsdp", None),
        P("fsdp"),
        P("fsdp"),
        P("fsdp", None),
        P("fsdp", None),
        P("fsdp"),
        P("fsdp"),
        P("fsdp", None),
        P("fsdp", None),
        P("fsdp"),
        P("fsdp"),
        P(("dp", "fsdp")),
        P(("dp", "fsdp"), None),
        P(("dp", "fsdp"), None),
        P(("dp", "fsdp"), None, None),
    )
    out_specs = (
        P(("dp", "fsdp"), None, None),
        P(("dp", "fsdp"), None, None),
        P("fsdp", None),
        P("fsdp"),
        P("fsdp"),
        P("fsdp", None),
        P("fsdp", None),
        P("fsdp"),
        P("fsdp"),
        P("fsdp", None),
        P("fsdp", None),
        P("fsdp"),
        P("fsdp"),
    )
    return jax.shard_map(shards, mesh=mesh, in_specs=in_specs, out_specs=out_specs, check_vma=False)
```

profile of v0, /device:TPU:0, one launch (start us, length us, event | category | flops | bytes accessed | tf_op | source)
XLA Modules:
  0.0 913.8 jit_solution(14838720792702939342)
XLA Ops:
  20.4 39.1 %all-reduce.13 = (bf16[768]{0:T(1024)(128)(2,1)S(1)}, bf16[768]{0:T(1024)(128)(2,1)S(1)}, bf16[768]{0:T(1024)(128)(2,1)S(1)}, bf16[768]{0:T(1024)(128)(2,1)S(1)}, bf16[768]{0:T(1024)(128)(2,1)S(1)}) all-reduce(bf16[768]{0:T(1024)(128)(2,1)S(1)} %dynamic-update-slice.1, ...), channel_id=1, replica_groups=mesh['dp'=4,'fsdp'=8] {'fsdp'}, use_global_device_ids=true, to_apply=%add.1 | all-reduce | flops 3840 | bytes 15360
  61.3 2.1 fusion.47
  63.5 2.0 multiply_reduce_fusion.6
  65.5 38.1 %all-reduce.11 = (f32[768]{0:T(1024)S(1)}, f32[]{:T(128)}) all-reduce(f32[768]{0:T(1024)S(1)} %get-tuple-element.172, f32[]{:T(128)S(6)} %convert_element_type.181), channel_id=1, replica_groups=mesh['dp'=4,'fsdp'=8] {'dp','fsdp'}, use_global_device_ids=true, to_apply=%region_2.0 | all-reduce | flops 769 | bytes 6152 | tf_op jit(solution)/shard_map/psum | solution.py:159
  104.5 42.7 %psum.100 = f32[768]{0:T(1024)S(1)} all-reduce(f32[768]{0:T(1024)S(1)} %fusion.53), channel_id=1, replica_groups=mesh['dp'=4,'fsdp'=8] {'dp','fsdp'}, use_global_device_ids=true, to_apply=%region_6.0 | all-reduce | flops 768 | bytes 6144 | tf_op jit(solution)/shard_map/psum | solution.py:165
  147.8 2.3 fusion.55
  150.1 9.0 convolution_convert_fusion
  159.1 6.8 copy.50
  165.9 22.5 %while.22 = (s32[]{:T(128)}, bf16[2,512,768]{1,2,0:T(8,128)(2,1)S(1)}, f32[2,12,512]{2,1,0:T(8,128)S(1)}, bf16[2,512,2304]{1,2,0:T(8,128)(2,1)}, s32[2,512]{1,0:T(2,128)S(1)}, /*index=5*/s32[]{:T(128)}) while((s32[]{:T(128)}, bf16[2,512,768]{1,2,0:T(8,128)(2,1)S(1)}, f32[2,12,512]{2,1,0:T(8,128)S(1)}, bf16[2,512,2304]{1,2,0:T(8,128)(2,1)}, ...), condition=%wide.region_10.11_spmd, body=%wide.region_7.10_spmd.sunk | while | flops 843442688 | bytes 52129876 | solution.py:179
  166.0 1.8 dynamic-slice_bitcast_fusion.6
  168.1 3.1 fusion.131
  171.1 2.6 fusion.132
  173.8 3.3 fusion.133
  177.1 1.8 dynamic-slice_bitcast_fusion.6
  179.1 3.1 fusion.131
  182.2 2.6 fusion.132
  184.9 3.3 fusion.133
  189.6 4.8 fusion.77
  194.9 49.1 %all-gather.12.cloned.1.call-done = bf16[768,3072]{1,0:T(8,128)(2,1)} async-done(((bf16[96,3072]{1,0:T(8,128)(2,1)}), bf16[768,3072]{1,0:T(8,128)(2,1)}) %all-gather.12.cloned.1.call-update) | async-done | bytes 4718608 | tf_op jit(solution)/shard_map/all_gather | solution.py:126
  244.0 14.9 %fusion.36 = (u8[512,3072]{1,0:T(8,128)(4,1)S(1)}, u8[512,3072]{1,0:T(8,128)(4,1)S(1)}, f32[2,512,3072]{2,1,0:T(8,128)}) fusion(bf16[768,3072]{1,0:T(8,128)(2,1)} %all-gather.12.cloned.1.call-done, f32[2,512,768]{2,1,0:T(8,128)S(1)} %get-tuple-element.175, f32[768]{0:T(1024)S(1)} %copy-done.50, f32[768]{0:T(1024)S(1)} %copy-done.40, ...), kind=kOutput, calls=%fused_computation.80 | convolution fusion | flops 4873519104 | bytes 23607296 | tf_op jit(solution)/shard_map/sjq,qy->sjy/dot_general | solution.py:186
  258.9 31.0 %multiply_convert_fusion.3 = (bf16[2,512,3072]{2,1,0:T(8,128)(2,1)}, f32[2,512,3072]{2,1,0:T(8,128)}) fusion(f32[2,512,3072]{2,1,0:T(8,128)} %get-tuple-element.176, u8[512,3072]{1,0:T(8,128)(4,1)S(1)} %get-tuple-element.99, u8[512,3072]{1,0:T(8,128)(4,1)S(1)} %get-tuple-element.98), kind=kLoop, calls=%fused_computation.37 | loop fusion | flops 220200960 | bytes 34603008 | tf_op jit(solution)/shard_map/convert_element_type | solution.py:192
  289.9 34.1 %all-gather.14.cloned.1.call-done = bf16[3072,768]{1,0:T(8,128)(2,1)} async-done(((bf16[384,768]{1,0:T(8,128)(2,1)}), bf16[3072,768]{1,0:T(8,128)(2,1)}) %all-gather.14.cloned.1.call-update) | async-done | bytes 4718608 | tf_op jit(solution)/shard_map/all_gather | solution.py:127
  324.1 9.7 %fusion.78 = (f32[2,512]{1,0:T(2,128)S(1)}, f32[2,512,768]{2,1,0:T(8,128)S(1)}) fusion(bf16[2,512,3072]{2,1,0:T(8,128)(2,1)} %get-tuple-element.156, bf16[3072,768]{1,0:T(8,128)(2,1)} %all-gather.14.cloned.1.call-done, f32[768]{0:T(1024)S(1)} %copy-done.50, f32[768]{0:T(1024)S(1)} %copy-done.40, f32[2,512]{1,0:T(2,128)S(1)} %fusion.66, ...), kind=kOutput, calls=%fused_computation.142 | convolution fusion | flops 4836555776 | bytes 17319936 | tf_op jit(solution)/shard_map/zya,av->zyv/dot_general | solution.py:193
  334.9 2.4 fusion.34
  337.3 16.4 %add_convert_fusion = bf16[2,512,3072]{2,1,0:T(8,128)(2,1)} fusion(f32[2,512,3072]{2,1,0:T(8,128)} %get-tuple-element.157, f32[2,512,3072]{2,1,0:T(8,128)} %get-tuple-element.176, bf16[3072,768]{1,0:T(8,128)(2,1)} %all-gather.14.cloned.1.call-done, f32[2,512]{1,0:T(2,128)S(1)} %negate_multiply_fusion.2, bf16[2,512,768]{2,1,0:T(8,128)(2,1)} %param.35, ...), kind=kOutput, calls=%fused_computation.36 | convolution fusion | flops 4882956288 | bytes 40913920 | tf_op jit(solution)/shard_map/ivj,hj->ivh/dot_general | solution.py:231
  353.7 11.2 %multiply_reduce_fusion.1 = (bf16[768]{0:T(1024)(128)(2,1)}, f32[2,512]{1,0:T(2,128)S(1)}, bf16[768]{0:T(1024)(128)(2,1)}, f32[2,512,768]{2,1,0:T(8,128)S(1)}) fusion(f32[2,512,768]{2,1,0:T(8,128)} %copy-done.2, f32[2,512]{1,0:T(2,128)S(1)} %fusion.66, f32[2,512]{1,0:T(2,128)S(1)} %broadcast_multiply_fusion.1, f32[768]{0:T(1024)S(1)} %copy-done.40, ...), kind=kOutput, calls=%fused_computation.72 | convolution fusion | flops 4845204480 | bytes 22057984 | tf_op jit(solution)/shard_map/wmx,ix->wmi/dot_general | solution.py:239
  366.3 2.5 bitcast_convert_fusion.3
  369.0 3.9 convolution_convert_fusion.1
  372.8 77.4 %while.23 = (s32[]{:T(128)}, bf16[2,512,2304]{1,2,0:T(8,128)(2,1)}, bf16[2,512,2304]{1,2,0:T(8,128)(2,1)}, s32[2,512]{1,0:T(2,128)S(1)}, f32[2,12,512]{2,1,0:T(8...) while((s32[]{:T(128)}, bf16[2,512,2304]{1,2,0:T(8,128)(2,1)}, bf16[2,512,2304]{1,2,0:T(8,128)(2,1)}, ...), condition=%wide.region_21.22_spmd, body=%wide.region_19.21_spmd.sunk | while | flops 2069490176 | bytes 163754704 | solution.py:256
  373.0 1.9 dynamic-slice_bitcast_fusion.7
  375.1 6.4 fusion.145
  383.9 11.5 %multiply_reduce_fusion.8 = (f32[12,512]{1,0:T(8,128)S(1)}, f32[12,512,512]{1,2,0:T(8,128)}) fusion(f32[12,512,512]{1,2,0:T(8,128)} %fusion.145, f32[12,512]{1,0:T(8,128)S(1)} %dynamic-slice_bitcast_fusion.8, pred[512]{0:T(512)(128)(4,1)S(1)} %compare_reduce_fusion.5, bf16[512,12,64]{0,2,1:T(8,128)(2,1)S(1)} %bitcast.169, ...), kind=kOutput, calls=%fused_computation.14.clone.1 | convolution fusion | flops 418375680 | bytes 26788352 | tf_op jit(solution)/shard_map/while/body/eval_jaxpr/qhe,khe->hqk/dot_general | solution.py:69
  396.7 7.1 multiply_convert_fusion.8
  404.9 2.0 multiply_convert_fusion.9
  407.0 3.1 fusion.146
  410.0 1.6 maximum_dynamic-update-slice_fusion.2
  411.6 1.8 dynamic-slice_bitcast_fusion.7
  413.6 6.4 fusion.145
  422.4 11.5 %multiply_reduce_fusion.8 = (f32[12,512]{1,0:T(8,128)S(1)}, f32[12,512,512]{1,2,0:T(8,128)}) fusion(f32[12,512,512]{1,2,0:T(8,128)} %fusion.145, f32[12,512]{1,0:T(8,128)S(1)} %dynamic-slice_bitcast_fusion.8, pred[512]{0:T(512)(128)(4,1)S(1)} %compare_reduce_fusion.5, bf16[512,12,64]{0,2,1:T(8,128)(2,1)S(1)} %bitcast.169, ...), kind=kOutput, calls=%fused_computation.14.clone.1 | convolution fusion | flops 418375680 | bytes 26788352 | tf_op jit(solution)/shard_map/while/body/eval_jaxpr/qhe,khe->hqk/dot_general | solution.py:69
  435.1 7.1 multiply_convert_fusion.8
  443.3 2.0 multiply_convert_fusion.9
  445.3 3.1 fusion.146
  448.4 1.6 maximum_dynamic-update-slice_fusion.2
  450.3 8.5 add_add_fusion.2
  458.8 1.6 copy-done.8
  460.4 1.5 fusion.71
  461.9 38.4 %all-reduce.10 = (f32[768]{0:T(1024)S(1)}, f32[768]{0:T(1024)S(1)}) all-reduce(f32[768]{0:T(1024)S(1)} %get-tuple-element.108, f32[768]{0:T(1024)S(1)} %get-tuple-element.107), channel_id=1, replica_groups=mesh['dp'=4,'fsdp'=8] {'dp','fsdp'}, use_global_device_ids=true, to_apply=%region_25.26 | all-reduce | flops 1536 | bytes 12288 | tf_op jit(solution)/shard_map/psum | solution.py:270
  502.7 1.5 bitcast_convert_fusion.4
  505.0 8.5 bitcast_convert_fusion.2
  513.9 1.5 copy-done.1
  515.4 11.2 %bitcast_convert_fusion = bf16[3072,768]{1,0:T(8,128)(2,1)} fusion(bf16[2,512,3072]{2,1,0:T(8,128)(2,1)} %get-tuple-element.156, f32[2,512]{1,0:T(2,128)S(1)} %copy-done.53, bf16[2,512,768]{2,1,0:T(8,128)(2,1)} %param.35, f32[2,512,768]{2,1,0:T(8,128)S(1)} %copy-done.1, f32[2,512]{1,0:T(2,128)S(1)} %copy-done.46, f32[768]{0:T(1024)S(1)} %copy-done.27, ...), kind=kOutput, calls=%fused_computation.50 | convolution fusion | flops 4841275392 | bytes 15748096 | tf_op jit(solution)/shard_map/omt,oms->ts/dot_general | solution.py:228
  527.3 10.5 %bitcast_convert_fusion.1 = bf16[768,3072]{1,0:T(8,128)(2,1)} fusion(bf16[2,512,3072]{2,1,0:T(8,128)(2,1)} %add_convert_fusion, f32[2,512,768]{2,1,0:T(8,128)} %copy-done.2, f32[768]{0:T(1024)S(1)} %copy-done.51, f32[768]{0:T(1024)S(1)} %copy-done.41, f32[2,512]{1,0:T(2,128)S(1)} %copy-done.43, f32[2,512]{1,0:T(2,128)S(1)} %copy-done.37), kind=kOutput, calls=%fused_computation.51 | convolution fusion | flops 4838129664 | bytes 14170112 | tf_op jit(solution)/shard_map/oih,oiu->hu/dot_general | solution.py:236
  537.9 2.3 reduce_sum.212
  545.3 37.1 %all-reduce.12 = (bf16[768]{0:T(1024)(128)(2,1)}, bf16[768]{0:T(1024)(128)(2,1)}, bf16[768]{0:T(1024)(128)(2,1)}, bf16[768]{0:T(1024)(128)(2,1)}, bf16[768]{0:T(1024)(128)(2,1)}) all-reduce(bf16[768]{0:T(1024)(128)(2,1)} %dynamic-update-slice.5, bf16[768]{0:T(1024)(128)(2,1)} %get-tuple-element.100, ...), channel_id=1, replica_groups=mesh['dp'=4,'fsdp'=8] {'fsdp'}, use_global_device_ids=true, to_apply=%add.5 | all-reduce | flops 3840 | bytes 15360
  587.4 7.0 all-reduce.14
  600.4 50.5 %reduce-scatter.8.cloned.1.call-done = bf16[96,2304]{1,0:T(8,128)(2,1)} async-done(((bf16[768,2304]{1,0:T(8,128)(2,1)}), bf16[96,2304]{1,0:T(8,128)(2,1)}) %reduce-scatter.8.cloned.1.call-update) | async-done | bytes 442384 | tf_op jit(solution)/shard_map/reduce_scatter | solution.py:310
  650.9 98.5 %reduce-scatter.14.cloned.1.call-done = bf16[384,768]{1,0:T(8,128)(2,1)} async-done(((bf16[3072,768]{1,0:T(8,128)(2,1)}), bf16[384,768]{1,0:T(8,128)(2,1)}) %reduce-scatter.14.cloned.1.call-update) | async-done | bytes 589840 | tf_op jit(solution)/shard_map/reduce_scatter | solution.py:325
  749.4 98.5 %reduce-scatter.12.cloned.1.call-done = bf16[96,3072]{1,0:T(8,128)(2,1)} async-done(((bf16[768,3072]{1,0:T(8,128)(2,1)}), bf16[96,3072]{1,0:T(8,128)(2,1)}) %reduce-scatter.12.cloned.1.call-update) | async-done | bytes 589840 | tf_op jit(solution)/shard_map/reduce_scatter | solution.py:322
  848.0 1.8 convolution_divide_fusion
  849.8 2.2 multiply_add_fusion
  852.7 3.2 convolution_add_fusion
  855.9 44.0 %all-reduce.18.cloned.1.call-done = (bf16[96,768]{1,0:T(8,128)(2,1)}, bf16[96,2304]{1,0:T(8,128)(2,1)}, bf16[96,768]{1,0:T(8,128)(2,1)}, bf16[96,3072]{1,0:T(8,128)(2,1)}, bf16[384,768]{1,0:T(8,128)(2,1)}) async-done(((bf16[96,768]{1,0:T(8,128)(2,1)}, bf16[96,2304]{1,0:T(8,128)(2,1)}, bf16[96,768]{1,0:T(8,128)(2,1)}, bf16[96,3072]{1,0:T(8,128)(2,1)}, bf16[384,768]{1,0:T(8,128)(2,1)}), ...) | async-done | bytes 1916944 | tf_op jit(solution)/shard_map/psum | solution.py:336
  899.9 2.2 convert_element_type.210
  902.1 2.2 convert_element_type.212
  (231 shorter events, 52.4 us)
Async XLA Ops:
  7.2 56.3 %all-gather.6.cloned.1.call-start = ((), (), s32[]{:S(2)}) async-start(), calls=%async_computation.5 | async-start | bytes 1327104 | tf_op jit(solution)/shard_map/all_gather | solution.py:119
  7.9 142.2 %all-gather.8.cloned.1.call-start = ((), (), s32[]{:S(2)}) async-start(), calls=%async_computation.6 | async-start | bytes 3981312 | tf_op jit(solution)/shard_map/all_gather | solution.py:122
  8.7 179.8 %all-gather.10.cloned.1.call-start = ((), (), s32[]{:S(2)}) async-start(), calls=%async_computation.7 | async-start | bytes 1327104 | tf_op jit(solution)/shard_map/all_gather | solution.py:123
  9.4 234.6 %all-gather.12.cloned.1.call-start = ((), (), s32[]{:S(2)}) async-start(), calls=%async_computation.8 | async-start | bytes 5308416 | tf_op jit(solution)/shard_map/all_gather | solution.py:126
  10.0 314.1 %all-gather.14.cloned.1.call-start = ((), (), s32[]{:S(2)}) async-start(), calls=%async_computation.9 | async-start | bytes 5308416 | tf_op jit(solution)/shard_map/all_gather | solution.py:127
  10.6 589.8 %reduce-scatter.10.cloned.1.call-start = ((), (), s32[]{:S(2)}) async-start(), calls=%async_computation.12 | async-start | bytes 1327104 | tf_op jit(solution)/shard_map/reduce_scatter | solution.py:313
  11.4 92.9 %copy-start.47 = (f32[2,128]{1,0:T(2,128)}, f32[2,128]{1,0:T(2,128)S(1)}, u32[]{:S(2)}) copy-start(f32[2,128]{1,0:T(2,128)S(1)} %compare_convert_fusion) | copy-start | bytes 3076
  13.6 49.9 %copy-start.57 = (f32[2,128]{1,0:T(2,128)}, f32[2,128]{1,0:T(2,128)S(1)}, u32[]{:S(2)}) copy-start(f32[2,128]{1,0:T(2,128)S(1)} %broadcast_maximum_fusion) | copy-start | bytes 3076
  59.5 88.3 %copy-start.34 = (f32[768]{0:T(1024)}, f32[768]{0:T(1024)S(1)}, u32[]{:S(2)}) copy-start(f32[768]{0:T(1024)S(1)} %convert_element_type.182) | copy-start | bytes 9220
  61.3 86.5 %copy-start.30 = (s32[2,512]{1,0:T(2,128)S(1)}, s32[2,512]{1,0:T(2,128)}, u32[]{:S(2)}) copy-start(s32[2,512]{1,0:T(2,128)} %param.33) | copy-start | bytes 12292
  63.4 86.7 %copy-start.16 = (bf16[2,128,768]{2,1,0:T(8,128)(2,1)}, bf16[2,128,768]{2,1,0:T(8,128)(2,1)S(1)}, u32[]{:S(2)}) copy-start(bf16[2,128,768]{2,1,0:T(8,128)(2,1)S(1)} %fusion.47) | copy-start | bytes 1179652
  63.5 86.6 %copy-start.12 = (bf16[2,512,768]{2,1,0:T(8,128)(2,1)S(1)}, bf16[2,512,768]{2,1,0:T(8,128)(2,1)}, u32[]{:S(2)}) copy-start(bf16[2,512,768]{2,1,0:T(8,128)(2,1)} %param.20) | copy-start | bytes 4718596
  65.5 93.5 %copy-start.4 = (f32[2,128,768]{2,1,0:T(8,128)}, f32[2,128,768]{2,1,0:T(8,128)S(1)}, u32[]{:S(2)}) copy-start(f32[2,128,768]{2,1,0:T(8,128)S(1)} %get-tuple-element.173) | copy-start | bytes 2359300
  104.3 54.8 %copy-start.24 = (f32[768]{0:T(1024)}, f32[768]{0:T(1024)S(1)}, u32[]{:S(2)}) copy-start(f32[768]{0:T(1024)S(1)} %broadcast_divide_fusion.1) | copy-start | bytes 9220
  147.8 11.3 %copy-start.32 = (f32[768]{0:T(1024)}, f32[768]{0:T(1024)S(1)}, u32[]{:S(2)}) copy-start(f32[768]{0:T(1024)S(1)} %add_rsqrt_fusion) | copy-start | bytes 9220
  159.1 6.8 copy-start.13
  159.1 6.8 copy-start.23
  194.3 64.5 %copy-start.2 = (f32[2,512,768]{2,1,0:T(8,128)}, f32[2,512,768]{2,1,0:T(8,128)S(1)}, u32[]{:S(2)}) copy-start(f32[2,512,768]{2,1,0:T(8,128)S(1)} %get-tuple-element.175) | copy-start | bytes 9437188
  194.3 49.6 %copy-start.40 = (f32[768]{0:T(1024)S(1)}, f32[768]{0:T(1024)}, u32[]{:S(2)}) copy-start(f32[768]{0:T(1024)} %convert_element_type.187) | copy-start | bytes 9220
  194.4 49.6 %copy-start.50 = (f32[768]{0:T(1024)S(1)}, f32[768]{0:T(1024)}, u32[]{:S(2)}) copy-start(f32[768]{0:T(1024)} %convert_element_type.188) | copy-start | bytes 9220
  194.4 170.5 %copy-start.36 = (f32[2,512]{1,0:T(2,128)}, f32[2,512]{1,0:T(2,128)S(1)}, u32[]{:S(2)}) copy-start(f32[2,512]{1,0:T(2,128)S(1)} %broadcast_multiply_fusion.1) | copy-start | bytes 12292
  194.9 170.0 %copy-start.42 = (f32[2,512]{1,0:T(2,128)}, f32[2,512]{1,0:T(2,128)S(1)}, u32[]{:S(2)}) copy-start(f32[2,512]{1,0:T(2,128)S(1)} %fusion.66) | copy-start | bytes 12292
  324.1 9.8 %copy-start.6 = (bf16[2,512,768]{2,1,0:T(8,128)(2,1)S(1)}, bf16[2,512,768]{2,1,0:T(8,128)(2,1)}, u32[]{:S(2)}) copy-start(bf16[2,512,768]{2,1,0:T(8,128)(2,1)} %param.35) | copy-start | bytes 4718596
  324.1 9.8 %copy-start.26 = (f32[768]{0:T(1024)S(1)}, f32[768]{0:T(1024)}, u32[]{:S(2)}) copy-start(f32[768]{0:T(1024)} %convert_element_type.191) | copy-start | bytes 9220
  333.8 19.9 %copy-start = (f32[2,512,768]{2,1,0:T(8,128)}, f32[2,512,768]{2,1,0:T(8,128)S(1)}, u32[]{:S(2)}) copy-start(f32[2,512,768]{2,1,0:T(8,128)S(1)} %get-tuple-element.178) | copy-start | bytes 9437188
  333.8 19.8 %copy-start.28 = (f32[2,512]{1,0:T(2,128)}, f32[2,512]{1,0:T(2,128)S(1)}, u32[]{:S(2)}) copy-start(f32[2,512]{1,0:T(2,128)S(1)} %broadcast_multiply_fusion) | copy-start | bytes 12292
  334.9 18.8 %copy-start.38 = (f32[2,512]{1,0:T(2,128)}, f32[2,512]{1,0:T(2,128)S(1)}, u32[]{:S(2)}) copy-start(f32[2,512]{1,0:T(2,128)S(1)} %get-tuple-element.169) | copy-start | bytes 12292
  334.9 18.8 %copy-start.45 = (f32[2,512]{1,0:T(2,128)}, f32[2,512]{1,0:T(2,128)S(1)}, u32[]{:S(2)}) copy-start(f32[2,512]{1,0:T(2,128)S(1)} %get-tuple-element.168) | copy-start | bytes 12292
  337.3 16.4 %copy-start.52 = (f32[2,512]{1,0:T(2,128)}, f32[2,512]{1,0:T(2,128)S(1)}, u32[]{:S(2)}) copy-start(f32[2,512]{1,0:T(2,128)S(1)} %negate_multiply_fusion.2) | copy-start | bytes 12292
  353.7 11.2 %copy-start.3 = (f32[2,512,768]{2,1,0:T(8,128)S(1)}, f32[2,512,768]{2,1,0:T(8,128)}, u32[]{:S(2)}) copy-start(f32[2,512,768]{2,1,0:T(8,128)} %copy-done.2) | copy-start | bytes 9437188
  366.2 2.8 copy-start.11
  366.2 2.8 copy-start.55
  368.9 231.5 %reduce-scatter.6.cloned.1.call-start = ((), (), s32[]{:S(2)}) async-start(), calls=%async_computation.10 | async-start | bytes 1327104 | tf_op jit(solution)/shard_map/reduce_scatter | solution.py:307
  372.8 77.4 %copy-start.56 = (f32[2,512]{1,0:T(2,128)S(1)}, f32[2,512]{1,0:T(2,128)}, u32[]{:S(2)}) copy-start(f32[2,512]{1,0:T(2,128)} %copy-done.55) | copy-start | bytes 12292
  375.1 6.4 copy-start.10
  383.8 11.5 %slice-start = ((s8[12582912]{0:T(1024)(128)(4,1)}), s8[4194304]{0:T(1024)(128)(4,1)S(1)}, s32[]{:S(2)}) async-start(s8[12582912]{0:T(1024)(128)(4,1)} %bitcast.161), calls=%async_computation.16 | async-start | bytes 8388608 | tf_op jit(solution)/shard_map/while
  383.8 11.5 %slice-start.1 = ((s8[12582912]{0:T(1024)(128)(4,1)}), s8[4194304]{0:T(1024)(128)(4,1)S(1)}, s32[]{:S(2)}) async-start(s8[12582912]{0:T(1024)(128)(4,1)} %bitcast.161), calls=%async_computation.17 | async-start | bytes 8388608 | tf_op jit(solution)/shard_map/while
  383.9 12.8 %slice-start.2 = ((s8[12582912]{0:T(1024)(128)(4,1)}), s8[4194304]{0:T(1024)(128)(4,1)S(1)}, s32[]{:S(2)}) async-start(s8[12582912]{0:T(1024)(128)(4,1)} %bitcast.161), calls=%async_computation.18 | async-start | bytes 8388608 | tf_op jit(solution)/shard_map/while
  413.6 6.4 copy-start.10
  422.3 11.5 %slice-start = ((s8[12582912]{0:T(1024)(128)(4,1)}), s8[4194304]{0:T(1024)(128)(4,1)S(1)}, s32[]{:S(2)}) async-start(s8[12582912]{0:T(1024)(128)(4,1)} %bitcast.161), calls=%async_computation.16 | async-start | bytes 8388608 | tf_op jit(solution)/shard_map/while
  422.4 11.5 %slice-start.1 = ((s8[12582912]{0:T(1024)(128)(4,1)}), s8[4194304]{0:T(1024)(128)(4,1)S(1)}, s32[]{:S(2)}) async-start(s8[12582912]{0:T(1024)(128)(4,1)} %bitcast.161), calls=%async_computation.17 | async-start | bytes 8388608 | tf_op jit(solution)/shard_map/while
  422.4 12.7 %slice-start.2 = ((s8[12582912]{0:T(1024)(128)(4,1)}), s8[4194304]{0:T(1024)(128)(4,1)S(1)}, s32[]{:S(2)}) async-start(s8[12582912]{0:T(1024)(128)(4,1)} %bitcast.161), calls=%async_computation.18 | async-start | bytes 8388608 | tf_op jit(solution)/shard_map/while
  450.2 10.2 %copy-start.5 = (f32[2,128,768]{2,1,0:T(8,128)S(1)}, f32[2,128,768]{2,1,0:T(8,128)}, u32[]{:S(2)}) copy-start(f32[2,128,768]{2,1,0:T(8,128)} %copy-done.4) | copy-start | bytes 2359300
  450.2 10.2 %copy-start.25 = (f32[768]{0:T(1024)S(1)}, f32[768]{0:T(1024)}, u32[]{:S(2)}) copy-start(f32[768]{0:T(1024)} %copy-done.24) | copy-start | bytes 9220
  450.2 10.2 %copy-start.31 = (s32[2,512]{1,0:T(2,128)S(1)}, s32[2,512]{1,0:T(2,128)}, u32[]{:S(2)}) copy-start(s32[2,512]{1,0:T(2,128)} %param.33) | copy-start | bytes 12292
  450.3 10.1 %copy-start.33 = (f32[768]{0:T(1024)S(1)}, f32[768]{0:T(1024)}, u32[]{:S(2)}) copy-start(f32[768]{0:T(1024)} %copy-done.32) | copy-start | bytes 9220
  460.4 40.6 %copy-start.35 = (f32[768]{0:T(1024)S(1)}, f32[768]{0:T(1024)}, u32[]{:S(2)}) copy-start(f32[768]{0:T(1024)} %copy-done.34) | copy-start | bytes 9220
  460.4 40.6 %copy-start.48 = (f32[2,128]{1,0:T(2,128)S(1)}, f32[2,128]{1,0:T(2,128)}, u32[]{:S(2)}) copy-start(f32[2,128]{1,0:T(2,128)} %copy-done.47) | copy-start | bytes 3076
  460.4 42.3 %copy-start.17 = (bf16[2,128,768]{2,1,0:T(8,128)(2,1)S(1)}, bf16[2,128,768]{2,1,0:T(8,128)(2,1)}, u32[]{:S(2)}) copy-start(bf16[2,128,768]{2,1,0:T(8,128)(2,1)} %copy-done.16) | copy-start | bytes 1179652
  502.7 2.3 copy-start.7
  504.3 146.6 %reduce-scatter.8.cloned.1.call-start = ((), (), s32[]{:S(2)}) async-start(), calls=%async_computation.11 | async-start | bytes 3981312 | tf_op jit(solution)/shard_map/reduce_scatter | solution.py:310
  513.5 1.9 copy-start.1
  513.5 1.9 copy-start.27
  513.5 1.9 copy-start.29
  513.5 1.9 copy-start.39
  513.5 1.9 copy-start.46
  513.6 235.9 %reduce-scatter.14.cloned.1.call-start = ((), (), s32[]{:S(2)}) async-start(), calls=%async_computation.14 | async-start | bytes 5308416 | tf_op jit(solution)/shard_map/reduce_scatter | solution.py:325
  526.6 321.4 %reduce-scatter.12.cloned.1.call-start = ((), (), s32[]{:S(2)}) async-start(), calls=%async_computation.13 | async-start | bytes 5308416 | tf_op jit(solution)/shard_map/reduce_scatter | solution.py:322
  537.8 310.2 %copy-start.19 = (bf16[2,128,768]{2,1,0:T(8,128)(2,1)S(1)}, bf16[2,128,768]{2,1,0:T(8,128)(2,1)}, u32[]{:S(2)}) copy-start(bf16[2,128,768]{2,1,0:T(8,128)(2,1)} %copy-done.18) | copy-start | bytes 1179652
  537.8 362.1 %all-reduce.18.cloned.1.call-start = ((), (), s32[]{:S(2)}) async-start(), calls=%async_computation.15 | async-start | bytes 3833856 | tf_op jit(solution)/shard_map/psum | solution.py:336
  849.8 2.9 copy-start.9
  899.9 4.4 copy-start.20
  899.9 5.4 copy-start.22
  899.9 6.1 copy-start.21
  (12 other events, 12.7 us)
Sparse Core Ops, SparseCore 0:
  10.2 44.0 all-gather.5
  56.5 64.8 all-gather.7
  123.5 39.6 all-gather.9
  165.3 78.6 all-gather.11
  246.0 78.0 all-gather.13
  369.0 62.1 reduce-scatter.9
  504.4 64.6 reduce-scatter.5
  572.7 78.1 reduce-scatter.7
  654.6 94.8 reduce-scatter.13
  752.9 95.0 reduce-scatter.11
  850.7 49.1 all-reduce.17
where the time goes:
time: 922 us; the launch traced here: 914 us
  waiting for transfers between devices  378 us (41%)
  blocking collectives  202 us (22%)
  matrix products  186 us (20%)
  other arithmetic  84 us (9%)
  local copies, waits for them, and re-layouts  44.5 us (5%)
  between operations  17.1 us (2%)
    reduce_scatter x1, waiting for transfers between devices, shards(): lax.psum_scatter(up_local.astype(jnp.bfloat16), 'fsdp', scatter_dimension...  98.5 us
    reduce_scatter x1, waiting for transfers between devices, shards(): lax.psum_scatter(down_local.astype(jnp.bfloat16), 'fsdp', scatter_dimensi...  98.5 us
    unnamed x2, blocking collectives  76.2 us
    reduce_scatter x1, waiting for transfers between devices, shards(): lax.psum_scatter(attend_local.astype(jnp.bfloat16), 'fsdp', scatter_dimen...  50.5 us
    all_gather x1, waiting for transfers between devices, shards(): lax.all_gather(up_matrix, 'fsdp', axis=0, tiled=True)  49.1 us
    psum x1, waiting for transfers between devices, shards(): lax.psum(visual_shard.astype(jnp.bfloat16), 'dp').astype(jnp.float32)  44 us
    psum x1, blocking collectives, shards(): lax.psum(jnp.sum(valid_slot * center * center, axis=(0, 1)), ('dp', 'fsdp'))  42.7 us
    psum x1, blocking collectives, shards(): lax.psum((jnp.sum(delta_embedded, axis=(0, 1)), jnp.sum(delta_embedded *...  38.4 us
  transfers between devices with their start and end apart: 11, of which 6 were waited for; matrix products, arithmetic and copies ran while one was open for 28% of the time, Pallas kernels for 0%

commit v1 on v0

--- a/solution.py
+++ b/solution.py
@@ -5,7 +5,83 @@
 
 HEADS = 12
 SEGMAX = 128
-
+low = jnp.bfloat16
+
+
+def pair_groups(size):
+    return [[i, i + 1] for i in range(0, size, 2)]
+
+
+def line_groups(size):
+    return [list(range(0, size, 2)), list(range(1, size, 2))]
+
+
+def spread(value, axis, groups, count):
+    copies = jnp.broadcast_to(value[None], (count,) + value.shape)
+    return lax.all_to_all(copies, axis, 0, 0, axis_index_groups=groups)
+
+
+def gather_weight(shard):
+    rows, columns = shard.shape
+    dp, fsdp = lax.axis_size("dp"), lax.axis_size("fsdp")
+    half = columns // 2
+    core = lax.axis_index("dp") % 2
+    mine = lax.dynamic_slice_in_dim(shard, core * half, half, 1)
+    line = spread(mine, "fsdp", line_groups(fsdp), fsdp // 2)
+    both = spread(line, "fsdp", pair_groups(fsdp), 2)
+    full = spread(both, "dp", pair_groups(dp), 2)
+    full = full.transpose(2, 1, 3, 0, 4)
+    return full.reshape(fsdp * rows, columns)
+
+
+def gather_first(shard):
+    rows, columns = shard.shape
+    dp, fsdp = lax.axis_size("dp"), lax.axis_size("fsdp")
+    half = columns // 2
+    core = lax.axis_index("dp") % 2
+    mine = lax.dynamic_slice_in_dim(shard, core * half, half, 1)
+    line = spread(mine, "fsdp", None, fsdp)
+    full = spread(line, "dp", pair_groups(dp), 2)
+    return full.transpose(1, 2, 0, 3).reshape(fsdp * rows, columns)
+
+
+def swap(value, axis, bit):
+    size = lax.axis_size(axis)
+    return lax.ppermute(value, axis, [(i, i ^ bit) for i in range(size)])
+
+
+def add_low(left, right):
+    return (left.astype(jnp.float32) + right.astype(jnp.float32)).astype(low)
+
+
+def scatter_gradient(local):
+    rows, columns = local.shape
+    dp, fsdp = lax.axis_size("dp"), lax.axis_size("fsdp")
+    half = columns // 2
+    piece = rows // fsdp
+    core = lax.axis_index("dp") % 2
+    side = lax.axis_index("fsdp") % 2
+    local = local.astype(low)
+    keep = lax.dynamic_slice_in_dim(local, core * half, half, 1)
+    give = lax.dynamic_slice_in_dim(local, (1 - core) * half, half, 1)
+    chip = add_low(keep, swap(give, "dp", 1)).reshape(fsdp // 2, 2, piece, half)
+    keep = lax.dynamic_index_in_dim(chip, side, 1, False)
+    give = lax.dynamic_index_in_dim(chip, 1 - side, 1, False)
+    pair = add_low(keep, swap(give, "fsdp", 1))
+    parts = lax.all_to_all(pair, "fsdp", 0, 0, axis_index_groups=line_groups(fsdp))
+    total = jnp.sum(parts.astype(jnp.float32), axis=0).astype(low)
+    bit = 2
+    while bit < dp:
+        total = add_low(total, swap(total, "dp", bit))
+        bit *= 2
+    both = spread(total, "dp", pair_groups(dp), 2)
+    return both.transpose(1, 0, 2).reshape(piece, columns).astype(jnp.float32)
+
+
+def sum_all(value):
+    dp, fsdp = lax.axis_size("dp"), lax.axis_size("fsdp")
+    value = jnp.sum(spread(value, "fsdp", None, fsdp), axis=0)
+    return jnp.sum(spread(value, "dp", None, dp), axis=0)
 
 eps_norm = 1e-05
 eps_batch = 1e-05
@@ -115,32 +191,17 @@
     padding_mask,
     cotangent,
 ):
-    gathered = (
-        lax.all_gather(visual_matrix, "fsdp", axis=0, tiled=True),
-        lax.all_gather(batch_gain, "fsdp", axis=0, tiled=True),
-        lax.all_gather(batch_shift, "fsdp", axis=0, tiled=True),
-        lax.all_gather(attend_weight, "fsdp", axis=0, tiled=True),
-        lax.all_gather(merge_weight, "fsdp", axis=0, tiled=True),
-        lax.all_gather(first_gain, "fsdp", axis=0, tiled=True),
-        lax.all_gather(first_shift, "fsdp", axis=0, tiled=True),
-        lax.all_gather(up_matrix, "fsdp", axis=0, tiled=True),
-        lax.all_gather(down_matrix, "fsdp", axis=0, tiled=True),
-        lax.all_gather(second_gain, "fsdp", axis=0, tiled=True),
-        lax.all_gather(second_shift, "fsdp", axis=0, tiled=True),
-    )
-    (
-        gathered_visual_weight,
-        full_batch_gain,
-        full_batch_shift,
-        full_attend,
-        full_merge,
-        full_first_gain,
-        full_first_shift,
-        gathered_up_weight,
-        gathered_down_weight,
-        full_second_gain,
-        full_second_shift,
-    ) = gathered
+    small = jnp.stack([batch_gain, batch_shift, first_gain, first_shift, second_gain, second_shift])
+    small = spread(small, "fsdp", None, lax.axis_size("fsdp"))
+    small = small.transpose(1, 0, 2).reshape(6, -1)
+    full_batch_gain, full_batch_shift, full_first_gain, full_first_shift, full_second_gain, full_second_shift = (
+        small[i] for i in range(6)
+    )
+    gathered_visual_weight = gather_first(visual_matrix)
+    full_attend = gather_weight(attend_weight)
+    full_merge = gather_weight(merge_weight)
+    gathered_up_weight = gather_weight(up_matrix)
+    gathered_down_weight = gather_weight(down_matrix)
     features = text_rows.shape[2]
     slot_index = jnp.arange(SEGMAX)
     matches = segment_ids[:, :, None] == slot_index[None, None, :]
@@ -155,14 +216,18 @@
     )
     valid_slot = (slot_index[None, :] < segment_counts[:, None]).astype(jnp.float32)[..., None]
     local_count = jnp.sum(segment_counts).astype(jnp.float32)
-    masked_visual = valid_slot * visual_rows
-    segment_total, visual_sum = lax.psum(
-        (local_count, jnp.sum(masked_visual, axis=(0, 1))), ("dp", "fsdp")
-    )
-    batch_center = visual_sum / segment_total
+    local_sum = jnp.sum(valid_slot * visual_rows, axis=(0, 1))
+    local_center = visual_rows - local_sum / local_count
+    local_square = jnp.sum(valid_slot * local_center * local_center, axis=(0, 1))
+    stats = jnp.stack([local_sum, local_square, jnp.full_like(local_sum, local_count)])
+    stats = spread(stats, "fsdp", None, lax.axis_size("fsdp"))
+    stats = spread(stats, "dp", None, lax.axis_size("dp")).reshape(-1, 3, stats.shape[-1])
+    sums, squares, sizes = stats[:, 0], stats[:, 1], stats[:, 2]
+    segment_total = jnp.sum(sizes, axis=0)
+    batch_center = jnp.sum(sums, axis=0) / segment_total
     center = visual_rows - batch_center
     variance = (
-        lax.psum(jnp.sum(valid_slot * center * center, axis=(0, 1)), ("dp", "fsdp")) / segment_total
+        jnp.sum(squares + sizes * jnp.square(sums / sizes - batch_center), axis=0) / segment_total
     )
     inverse_spread = lax.rsqrt(variance + eps_batch)
     normed = center * inverse_spread
@@ -197,26 +262,14 @@
     layer_output = layer_norm(
         pre_two, full_second_gain.astype(jnp.float32), full_second_shift.astype(jnp.float32)
     )
-    again = (
-        lax.all_gather(visual_matrix, "fsdp", axis=0, tiled=True),
-        lax.all_gather(batch_gain, "fsdp", axis=0, tiled=True),
-        lax.all_gather(attend_weight, "fsdp", axis=0, tiled=True),
-        lax.all_gather(merge_weight, "fsdp", axis=0, tiled=True),
-        lax.all_gather(first_gain, "fsdp", axis=0, tiled=True),
-        lax.all_gather(up_matrix, "fsdp", axis=0, tiled=True),
-        lax.all_gather(down_matrix, "fsdp", axis=0, tiled=True),
-        lax.all_gather(second_gain, "fsdp", axis=0, tiled=True),
-    )
-    (
-        visual_pullback,
-        back_batch_gain,
-        back_attend,
-        back_merge,
-        back_first_gain,
-        up_pullback,
-        down_pullback,
-        back_second_gain,
-    ) = again
+    visual_pullback = gathered_visual_weight
+    back_batch_gain = full_batch_gain
+    back_attend = full_attend
+    back_merge = full_merge
+    back_first_gain = full_first_gain
+    up_pullback = gathered_up_weight
+    down_pullback = gathered_down_weight
+    back_second_gain = full_second_gain
     second_back = jax.vjp(
         layer_norm,
         pre_two,
@@ -267,10 +320,19 @@
         precision=highest_precision,
         preferred_element_type=jnp.float32,
     )
-    shift_total, gain_total = lax.psum(
-        (jnp.sum(delta_embedded, axis=(0, 1)), jnp.sum(delta_embedded * normed, axis=(0, 1))),
-        ("dp", "fsdp"),
-    )
+    vectors = sum_all(
+        jnp.stack(
+            [
+                jnp.sum(delta_embedded, axis=(0, 1)),
+                jnp.sum(delta_embedded * normed, axis=(0, 1)),
+                first_gain_local,
+                first_shift_local,
+                second_gain_local,
+                second_shift_local,
+            ]
+        )
+    )
+    shift_total, gain_total = vectors[0], vectors[1]
     visual_delta_rows = (
         valid_slot
         * back_batch_gain.astype(jnp.float32)
@@ -293,71 +355,17 @@
         precision=highest_precision,
         preferred_element_type=jnp.float32,
     )
-    (
-        visual_shard,
-        attend_shard,
-        merge_shard,
-        first_gain_shard,
-        first_shift_shard,
-        up_shard,
-        down_shard,
-        second_gain_shard,
-        second_shift_shard,
-    ) = (
-        lax.psum_scatter(
-            visual_local.astype(jnp.bfloat16), "fsdp", scatter_dimension=0, tiled=True
-        ).astype(jnp.float32),
-        lax.psum_scatter(
-            attend_local.astype(jnp.bfloat16), "fsdp", scatter_dimension=0, tiled=True
-        ).astype(jnp.float32),
-        lax.psum_scatter(
-            merge_local.astype(jnp.bfloat16), "fsdp", scatter_dimension=0, tiled=True
-        ).astype(jnp.float32),
-        lax.psum_scatter(
-            first_gain_local.astype(jnp.bfloat16), "fsdp", scatter_dimension=0, tiled=True
-        ).astype(jnp.float32),
-        lax.psum_scatter(
-            first_shift_local.astype(jnp.bfloat16), "fsdp", scatter_dimension=0, tiled=True
-        ).astype(jnp.float32),
-        lax.psum_scatter(
-            up_local.astype(jnp.bfloat16), "fsdp", scatter_dimension=0, tiled=True
-        ).astype(jnp.float32),
-        lax.psum_scatter(
-            down_local.astype(jnp.bfloat16), "fsdp", scatter_dimension=0, tiled=True
-        ).astype(jnp.float32),
-        lax.psum_scatter(
-            second_gain_local.astype(jnp.bfloat16), "fsdp", scatter_dimension=0, tiled=True
-        ).astype(jnp.float32),
-        lax.psum_scatter(
-            second_shift_local.astype(jnp.bfloat16), "fsdp", scatter_dimension=0, tiled=True
-        ).astype(jnp.float32),
-    )
-    summed = (
-        lax.psum(visual_shard.astype(jnp.bfloat16), "dp").astype(jnp.float32),
-        lax.psum(attend_shard.astype(jnp.bfloat16), "dp").astype(jnp.float32),
-        lax.psum(merge_shard.astype(jnp.bfloat16), "dp").astype(jnp.float32),
-        lax.psum(first_gain_shard.astype(jnp.bfloat16), "dp").astype(jnp.float32),
-        lax.psum(first_shift_shard.astype(jnp.bfloat16), "dp").astype(jnp.float32),
-        lax.psum(up_shard.astype(jnp.bfloat16), "dp").astype(jnp.float32),
-        lax.psum(down_shard.astype(jnp.bfloat16), "dp").astype(jnp.float32),
-        lax.psum(second_gain_shard.astype(jnp.bfloat16), "dp").astype(jnp.float32),
-        lax.psum(second_shift_shard.astype(jnp.bfloat16), "dp").astype(jnp.float32),
-    )
-    (
-        visual_gradient,
-        attend_gradient,
-        merge_gradient,
-        first_gain_gradient,
-        first_shift_gradient,
-        up_gradient,
-        down_gradient,
-        second_gain_gradient,
-        second_shift_gradient,
-    ) = summed
+    down_gradient = scatter_gradient(down_local)
+    up_gradient = scatter_gradient(up_local)
+    merge_gradient = scatter_gradient(merge_local)
+    attend_gradient = scatter_gradient(attend_local)
+    visual_gradient = scatter_gradient(visual_local)
     piece = features // lax.axis_size("fsdp")
     start = lax.axis_index("fsdp") * piece
-    batch_gain_gradient = lax.dynamic_slice_in_dim(gain_total, start, piece, 0)
-    batch_shift_gradient = lax.dynamic_slice_in_dim(shift_total, start, piece, 0)
+    own = lax.dynamic_slice_in_dim(vectors, start, piece, 1)
+    batch_shift_gradient, batch_gain_gradient = own[0], own[1]
+    first_gain_gradient, first_shift_gradient = own[2], own[3]
+    second_gain_gradient, second_shift_gradient = own[4], own[5]
     return (
         layer_output,
         text_gradient,

time: 922 us -> 764 us (0.83)
  waiting for transfers between devices: 378 us -> 171 us
  blocking collectives: 202 us -> 72.4 us
  local copies, waits for them, and re-layouts: 44.5 us -> 149 us
  starting transfers between devices: 0.69 us -> 90.9 us
  between operations: 17.1 us -> 2.94 us
    reduce_scatter x5 -> x0, waiting for transfers between devices: 248 us -> none  [the longest x1 98.5 us: shards(): lax.psum_scatter(up_local.astype(jnp.bfloat16), 'fsdp', scatter_dimension...]
    psum x4 -> x0, blocking collectives: 126 us -> none  [the longest x1 42.7 us: shards(): lax.psum(jnp.sum(valid_slot * center * center, axis=(0, 1)), ('dp', 'fsdp'))]
    all_to_all x0 -> x19, waiting for transfers between devices: none -> 108 us  [the longest x14 91.4 us: spread(): return lax.all_to_all(copies, axis, 0, 0, axis_index_groups=groups)]
    all_gather x5 -> x0, waiting for transfers between devices: 83.3 us -> none  [the longest x1 49.1 us: shards(): lax.all_gather(up_matrix, 'fsdp', axis=0, tiled=True)]
    all_to_all x0 -> x19, starting transfers between devices: none -> 78.9 us  [the longest x14 56.9 us: spread(): return lax.all_to_all(copies, axis, 0, 0, axis_index_groups=groups)]
    unnamed x2 -> x0, blocking collectives: 76.2 us -> none
    all_to_all x0 -> x10, blocking collectives: none -> 72.4 us  [spread(): return lax.all_to_all(copies, axis, 0, 0, axis_index_groups=groups)]
    ppermute x0 -> x15, waiting for transfers between devices: none -> 63.3 us  [swap(): return lax.ppermute(value, axis, [(i, i ^ bit) for i in range(size)])]
  transfers between devices with their start and end apart: 11 -> 34, of which waited for: 6 -> 20; matrix products, arithmetic and copies ran while one was open for 28% -> 24% of each run, Pallas kernels for 0% -> 0%
where the time goes in v1:
time: 764 us; the launch traced here: 753 us
  matrix products  179 us (23%)
  waiting for transfers between devices  171 us (22%)
  local copies, waits for them, and re-layouts  149 us (20%)
  starting transfers between devices  90.9 us (12%)
  other arithmetic  86.5 us (11%)
  blocking collectives  72.4 us (9%)
    all_to_all x14, waiting for transfers between devices, spread(): return lax.all_to_all(copies, axis, 0, 0, axis_index_groups=groups)  91.4 us
    all_to_all x10, blocking collectives, spread(): return lax.all_to_all(copies, axis, 0, 0, axis_index_groups=groups)  72.4 us
    ppermute x15, waiting for transfers between devices, swap(): return lax.ppermute(value, axis, [(i, i ^ bit) for i in range(size)])  63.3 us
    all_to_all x14, starting transfers between devices, spread(): return lax.all_to_all(copies, axis, 0, 0, axis_index_groups=groups)  56.9 us
    reshape x4, local copies, waits for them, and re-layouts, gather_weight(): return full.reshape(fsdp * rows, columns)  35.6 us
    convert_element_type x1, other arithmetic, shards(): gelu_activated = exact_gelu(inner_hidden).astype(jnp.bfloat16)  31 us
    transpose x4, local copies, waits for them, and re-layouts, gather_weight(): full = full.transpose(2, 1, 3, 0, 4)  27.6 us
    dot_general x2, matrix products, attend_back(): jnp.einsum('qhe,khe->hqk', delta_heads, values_part, preferred_element_ty...  23.4 us
  transfers between devices with their start and end apart: 34, of which 20 were waited for; matrix products, arithmetic and copies ran while one was open for 24% of the time, Pallas kernels for 0%

profile of v1, /device:TPU:0, one launch (start us, length us, event | category | flops | bytes accessed | tf_op | source)
XLA Modules:
  0.0 752.8 jit_solution(8537943716839339825)
XLA Ops:
  1.9 15.7 %all_to_all.145 = bf16[4,96,384]{2,1,0:T(8,128)(2,1)S(1)} all-to-all(bf16[4,96,384]{2,1,0:T(8,128)(2,1)S(1)} %broadcast_in_dim.96), channel_id=1, replica_groups={{0,2,4,6},{1,3,5,7},{8,10,12,14},{9,11,13,15},{16,18,20,22},{17,19,21,2..., dimensions={0} | all-to-all | bytes 589824 | tf_op jit(solution)/shard_map/all_to_all | solution.py:21
  22.0 6.9 all-to-all-done.9
  29.7 4.0 all-to-all-start
  38.0 10.0 %all-to-all-done = bf16[8,96,384]{2,1,0:T(8,128)(2,1)S(1)} async-done(((bf16[8,96,384]{2,1,0:T(8,128)(2,1)}), bf16[8,96,384]{2,1,0:T(8,128)(2,1)S(1)}, u32[]{:S(2)}, u32[]{:S(2)}) %all-to-all-start) | async-done | bytes 589856 | tf_op jit(solution)/shard_map/all_to_all | solution.py:21
  48.1 4.8 all_to_all.146
  64.9 5.5 all_to_all.147
  71.1 6.0 all-to-all-start.2
  78.0 6.2 all-to-all-done.2
  88.7 21.3 %all-to-all-done.5 = bf16[4,96,1152]{2,1,0:T(8,128)(2,1)S(1)} async-done(((bf16[4,96,1152]{2,1,0:T(8,128)(2,1)}), bf16[4,96,1152]{2,1,0:T(8,128)(2,1)S(1)}, u32[]{:S(2)}, u32[]{:S(2)}) %all-to-all-start.5) | async-done | bytes 884768 | tf_op jit(solution)/shard_map/all_to_all | solution.py:21
  110.0 9.0 %all_to_all.148 = f32[4,8,3,768]{3,1,2,0:T(8,128)S(1)} all-to-all(f32[4,8,3,768]{3,1,2,0:T(8,128)S(1)} %broadcast_in_dim.84), channel_id=1, replica_groups=mesh['dp'=4,'fsdp'=8] {'dp'}, dimensions={0} | all-to-all | bytes 589824 | tf_op jit(solution)/shard_map/all_to_all | solution.py:21
  124.8 20.9 %all-to-all-done.6 = bf16[2,4,96,1152]{3,2,1,0:T(8,128)(2,1)S(1)} async-done(((bf16[2,4,96,1152]{3,2,1,0:T(8,128)(2,1)}), bf16[2,4,96,1152]{3,2,1,0:T(8,128)(2,1)S(1)}, u32[]{:S(2)}, u32[]{:S(2)}) %all-to-all-start.6) | async-done | bytes 1769504 | tf_op jit(solution)/shard_map/all_to_all | solution.py:21
  147.8 4.3 all-to-all-start.11
  159.5 3.9 reshape.442
  164.9 15.3 %all-to-all-done.11 = bf16[4,96,1536]{2,1,0:T(8,128)(2,1)} async-done(((bf16[4,96,1536]{2,1,0:T(8,128)(2,1)}), bf16[4,96,1536]{2,1,0:T(8,128)(2,1)}, u32[]{:S(2)}, u32[]{:S(2)}) %all-to-all-start.11) | async-done | bytes 1179680 | tf_op jit(solution)/shard_map/all_to_all | solution.py:21
  182.0 7.6 %all_to_all.149 = bf16[2,2,4,96,1152]{4,3,1,2,0:T(8,128)(2,1)} all-to-all(bf16[2,2,4,96,1152]{4,3,1,2,0:T(8,128)(2,1)S(1)} %broadcast_in_dim.94), channel_id=1, replica_groups={{0,8},{16,24},{1,9},{17,25},{2,10},{18,26},{3,11},{19,27},{4,12},{20,28..., dimensions={0} | all-to-all | bytes 7077888 | tf_op jit(solution)/shard_map/all_to_all | solution.py:21
  192.5 5.3 all-to-all-start.12
  200.8 5.4 copy.181
  206.3 8.8 %reshape.441 = bf16[768,2304,1]{1,0,2:T(8,128)(2,1)} reshape(bf16[4,2,96,2,1152]{4,3,2,1,0:T(2,128)(2,1)} %copy.181) | data formatting | bytes 7077888 | tf_op jit(solution)/shard_map/reshape | solution.py:34
  215.1 8.9 %convolution_convert_fusion = bf16[2,512,2304]{2,1,0:T(8,128)(2,1)} fusion(bf16[768,2304,1]{1,0,2:T(8,128)(2,1)} %reshape.441, f32[2,512,768]{2,1,0:T(8,128)} %fusion.39, bf16[2,512,768]{2,1,0:T(8,128)(2,1)S(1)} %copy-done.22), kind=kOutput, calls=%fused_computation.53 | convolution fusion | flops 3628597248 | bytes 12976128 | tf_op jit(solution)/shard_map/drc,ce->dre/dot_general | solution.py:241
  224.0 6.7 copy.182
  231.8 4.7 all-to-all-start.14
  236.5 24.0 %while.22 = (s32[]{:T(128)}, bf16[2,512,768]{1,2,0:T(8,128)(2,1)}, f32[2,12,512]{2,1,0:T(8,128)S(1)}, bf16[2,512,2304]{1,2,0:T(8,128)(2,1)}, s32[2,512]{1,0:T(2,128)S(1)}, /*index=5*/s32[]{:T(128)}) while((s32[]{:T(128)}, bf16[2,512,768]{1,2,0:T(8,128)(2,1)}, f32[2,12,512]{2,1,0:T(8,128)S(1)}, bf16[2,512,2304]{1,2,0:T(8,128)(2,1)}, ...), condition=%wide.region_10.11_spmd, body=%wide.region_7.10_spmd.sunk | while | flops 843442688 | bytes 52130384 | solution.py:244
  266.1 8.6 %all_to_all.150 = bf16[2,2,4,96,1536]{4,3,1,2,0:T(8,128)(2,1)} all-to-all(bf16[2,2,4,96,1536]{4,3,1,2,0:T(8,128)(2,1)S(1)} %broadcast_in_dim.105), channel_id=1, replica_groups={{0,8},{16,24},{1,9},{17,25},{2,10},{18,26},{3,11},{19,27},{4,12},{20,28..., dimensions={0} | all-to-all | bytes 9437184 | tf_op jit(solution)/shard_map/all_to_all | solution.py:21
  277.7 4.0 all-to-all-start.15
  281.7 4.9 fusion.71
  288.7 9.4 %copy.187 = bf16[4,2,96,2,1536]{4,3,2,1,0:T(2,128)(2,1)} copy(bf16[4,2,96,2,1536]{4,2,1,0,3:T(8,128)(2,1)} %bitcast.239) | data formatting | bytes 9437184 | tf_op jit(solution)/shard_map/transpose | solution.py:33
  298.1 11.5 %reshape.443 = bf16[768,3072,1]{1,0,2:T(8,128)(2,1)} reshape(bf16[4,2,96,2,1536]{4,3,2,1,0:T(2,128)(2,1)} %copy.187) | data formatting | bytes 9437184 | tf_op jit(solution)/shard_map/reshape | solution.py:34
  310.7 8.8 %all_to_all.151 = bf16[2,2,4,384,384]{4,3,1,2,0:T(8,128)(2,1)} all-to-all(bf16[2,2,4,384,384]{4,3,1,2,0:T(8,128)(2,1)S(1)} %broadcast_in_dim.108), channel_id=1, replica_groups={{0,8},{16,24},{1,9},{17,25},{2,10},{18,26},{3,11},{19,27},{4,12},{20,28..., dimensions={0} | all-to-all | bytes 9437184 | tf_op jit(solution)/shard_map/all_to_all | solution.py:21
  319.5 9.3 %copy.189 = bf16[4,2,384,2,384]{4,3,2,1,0:T(2,128)(2,1)} copy(bf16[4,2,384,2,384]{4,2,1,0,3:T(8,128)(2,1)} %bitcast.240) | data formatting | bytes 9437184 | tf_op jit(solution)/shard_map/transpose | solution.py:33
  328.9 11.4 %reshape.444 = bf16[3072,768,1]{1,0,2:T(8,128)(2,1)} reshape(bf16[4,2,384,2,384]{4,3,2,1,0:T(2,128)(2,1)} %copy.189) | data formatting | bytes 9437184 | tf_op jit(solution)/shard_map/reshape | solution.py:34
  340.2 14.4 %fusion.26 = (u8[512,3072]{1,0:T(8,128)(4,1)}, u8[512,3072]{1,0:T(8,128)(4,1)}, f32[2,512,3072]{2,1,0:T(8,128)S(1)}) fusion(bf16[768,3072,1]{1,0,2:T(8,128)(2,1)} %reshape.443, f32[2,512,768]{2,1,0:T(8,128)} %copy-done.3, f32[768]{0:T(1024)S(1)} %copy-done.53, f32[768]{0:T(1024)S(1)} %copy-done.44, f32[2,512]{1,0:T(2,128)S(1)} %fusion.62, ...), kind=kOutput, calls=%fused_computation.74 | convolution fusion | flops 4873519104 | bytes 23607296 | tf_op jit(solution)/shard_map/sjq,qy->sjy/dot_general | solution.py:251
  354.6 31.0 %multiply_convert_fusion.3 = (bf16[2,512,3072]{2,1,0:T(8,128)(2,1)S(1)}, f32[2,512,3072]{2,1,0:T(8,128)}) fusion(f32[2,512,3072]{2,1,0:T(8,128)S(1)} %get-tuple-element.265, u8[512,3072]{1,0:T(8,128)(4,1)} %get-tuple-element.195, u8[512,3072]{1,0:T(8,128)(4,1)} %get-tuple-element.194), kind=kLoop, calls=%fused_computation.37 | loop fusion | flops 220200960 | bytes 34603008 | tf_op jit(solution)/shard_map/convert_element_type | solution.py:257
  385.7 5.4 fusion.72
  396.7 8.3 %bitcast_convert_fusion = bf16[3072,768]{1,0:T(8,128)(2,1)} fusion(bf16[2,512,3072]{2,1,0:T(8,128)(2,1)S(1)} %get-tuple-element.240, f32[2,512]{1,0:T(2,128)S(1)} %negate_multiply_fusion.2, bf16[2,512,768]{2,1,0:T(8,128)(2,1)S(1)} %copy-done.16, f32[2,512,768]{2,1,0:T(8,128)S(1)} %get-tuple-element.267, f32[2,512]{1,0:T(2,128)S(1)} %get-tuple-element.259, ...), kind=kOutput, calls=%fused_computation.50 | convolution fusion | flops 4841275392 | bytes 15748096 | tf_op jit(solution)/shard_map/omt,oms->ts/dot_general | solution.py:281
  405.1 16.6 %add_convert_fusion = bf16[2,512,3072]{2,1,0:T(8,128)(2,1)} fusion(f32[2,512,3072]{2,1,0:T(8,128)} %get-tuple-element.241, f32[2,512,3072]{2,1,0:T(8,128)} %copy-done.9, bf16[3072,768,1]{1,0,2:T(8,128)(2,1)} %reshape.444, f32[2,512]{1,0:T(2,128)S(1)} %negate_multiply_fusion.2, bf16[2,512,768]{2,1,0:T(8,128)(2,1)S(1)} %copy-done.16, ...), kind=kOutput, calls=%fused_computation.36 | convolution fusion | flops 4882956288 | bytes 40913920 | tf_op jit(solution)/shard_map/ivj,hj->ivh/dot_general | solution.py:284
  421.7 11.4 %multiply_reduce_fusion.1 = (f32[768]{0:T(1024)}, f32[2,512]{1,0:T(2,128)S(1)}, f32[768]{0:T(1024)}, f32[2,512,768]{2,1,0:T(8,128)S(1)}) fusion(f32[2,512,768]{2,1,0:T(8,128)} %copy-done.3, f32[2,512]{1,0:T(2,128)S(1)} %fusion.62, f32[2,512]{1,0:T(2,128)S(1)} %broadcast_multiply_fusion.1, f32[768]{0:T(1024)S(1)} %copy-done.44, ...), kind=kOutput, calls=%fused_computation.66 | convolution fusion | flops 4845204480 | bytes 22061056 | tf_op jit(solution)/shard_map/wmx,ix->wmi/dot_general | solution.py:292
  437.1 79.1 %while.23 = (s32[]{:T(128)}, bf16[2,512,2304]{1,2,0:T(8,128)(2,1)}, bf16[2,512,2304]{1,2,0:T(8,128)(2,1)}, s32[2,512]{1,0:T(2,128)S(1)}, f32[2,12,512]{2,1,0:T(8...) while((s32[]{:T(128)}, bf16[2,512,2304]{1,2,0:T(8,128)(2,1)}, bf16[2,512,2304]{1,2,0:T(8,128)(2,1)}, ...), condition=%wide.region_21.22_spmd, body=%wide.region_19.21_spmd.sunk | while | flops 2069490176 | bytes 166900464 | solution.py:309
  439.5 6.4 fusion.149
  449.1 11.7 %multiply_reduce_fusion.8 = (f32[12,512]{1,0:T(8,128)S(1)}, f32[12,512,512]{1,2,0:T(8,128)}) fusion(f32[12,512,512]{1,2,0:T(8,128)} %fusion.149, f32[12,512]{1,0:T(8,128)S(1)} %dynamic-slice_bitcast_fusion.13, pred[512]{0:T(512)(128)(4,1)S(1)} %compare_reduce_fusion.5, bf16[512,12,64]{0,2,1:T(8,128)(2,1)} %bitcast.231, ...), kind=kOutput, calls=%fused_computation.14.clone.1 | convolution fusion | flops 418375680 | bytes 26788352 | tf_op jit(solution)/shard_map/while/body/eval_jaxpr/qhe,khe->hqk/dot_general | solution.py:145
  461.9 7.1 multiply_convert_fusion.8
  478.9 6.4 fusion.149
  488.5 11.7 %multiply_reduce_fusion.8 = (f32[12,512]{1,0:T(8,128)S(1)}, f32[12,512,512]{1,2,0:T(8,128)}) fusion(f32[12,512,512]{1,2,0:T(8,128)} %fusion.149, f32[12,512]{1,0:T(8,128)S(1)} %dynamic-slice_bitcast_fusion.13, pred[512]{0:T(512)(128)(4,1)S(1)} %compare_reduce_fusion.5, bf16[512,12,64]{0,2,1:T(8,128)(2,1)} %bitcast.231, ...), kind=kOutput, calls=%fused_computation.14.clone.1 | convolution fusion | flops 418375680 | bytes 26788352 | tf_op jit(solution)/shard_map/while/body/eval_jaxpr/qhe,khe->hqk/dot_general | solution.py:145
  501.3 7.1 multiply_convert_fusion.8
  516.2 8.5 %add_add_fusion.2 = f32[2,512,768]{2,1,0:T(8,128)S(1)} fusion(f32[2,512,768]{2,1,0:T(8,128)} %copy-done.20, bf16[2,512,2304]{1,2,0:T(8,128)(2,1)} %get-tuple-element.75, bf16[768,2304,1]{1,0,2:T(8,128)(2,1)} %reshape.441, f32[2,512]{1,0:T(2,128)S(1)} %copy-done.56), kind=kOutput, calls=%fused_computation.75 | convolution fusion | flops 3625451520 | bytes 14553088 | tf_op jit(solution)/shard_map/dre,ce->drc/dot_general | solution.py:313
  528.9 3.9 all-to-all-start.17
  532.8 3.9 bitcast_convert_fusion.3
  536.7 4.3 all-to-all-done.17
  551.4 9.0 %bitcast_convert_fusion.2 = bf16[768,2304]{1,0:T(8,128)(2,1)} fusion(bf16[2,512,2304]{1,2,0:T(8,128)(2,1)} %get-tuple-element.75, f32[2,512,768]{2,1,0:T(8,128)S(1)} %copy-done.10, bf16[2,512,768]{2,1,0:T(8,128)(2,1)} %param.20), kind=kOutput, calls=%fused_computation.52 | convolution fusion | flops 3628007424 | bytes 12976128 | tf_op jit(solution)/shard_map/drc,dre->ce/dot_general | solution.py:310
  566.4 5.3 collective-permute-done.7
  572.5 4.1 all-to-all-start.23
  587.3 10.5 %bitcast_convert_fusion.1 = bf16[768,3072]{1,0:T(8,128)(2,1)} fusion(bf16[2,512,3072]{2,1,0:T(8,128)(2,1)} %add_convert_fusion, f32[2,512,768]{2,1,0:T(8,128)} %copy-done.3, f32[768]{0:T(1024)S(1)} %copy-done.54, f32[768]{0:T(1024)S(1)} %copy-done.45, f32[2,512]{1,0:T(2,128)S(1)} %copy-done.47, f32[2,512]{1,0:T(2,128)S(1)} %copy-done.40), kind=kOutput, calls=%fused_computation.51 | convolution fusion | flops 4838129664 | bytes 14170112 | tf_op jit(solution)/shard_map/oih,oiu->hu/dot_general | solution.py:289
  617.9 15.5 %collective-permute-done.4 = bf16[4,96,1152]{2,1,0:T(8,128)(2,1)S(1)} collective-permute-done((bf16[4,96,1152]{2,1,0:T(8,128)(2,1)S(1)}, bf16[4,96,1152]{2,1,0:T(8,128)(2,1)S(1)}, u32[]{:S(2)}, u32[]{:S(2)}) %collective-permute-start.4) | collective-permute-done | bytes 884768 | tf_op jit(solution)/shard_map/ppermute | solution.py:50
  634.5 3.8 all_to_all.152
  638.4 5.3 all-to-all-start.21
  646.8 11.6 %collective-permute-done.13 = bf16[4,384,384]{2,1,0:T(8,128)(2,1)} collective-permute-done((bf16[4,384,384]{2,1,0:T(8,128)(2,1)}, bf16[4,384,384]{2,1,0:T(8,128)(2,1)}, u32[]{:S(2)}, u32[]{:S(2)}) %collective-permute-start.13) | collective-permute-done | bytes 1179680 | tf_op jit(solution)/shard_map/ppermute | solution.py:50
  660.9 5.4 all-to-all-done.21
  666.3 4.3 all-to-all-start.27
  672.8 26.2 %collective-permute-done.10 = bf16[4,96,1536]{2,1,0:T(8,128)(2,1)} collective-permute-done((bf16[4,96,1536]{2,1,0:T(8,128)(2,1)}, bf16[4,96,1536]{2,1,0:T(8,128)(2,1)}, u32[]{:S(2)}, u32[]{:S(2)}) %collective-permute-start.10) | collective-permute-done | bytes 1179680 | tf_op jit(solution)/shard_map/ppermute | solution.py:50
  701.6 4.8 all-to-all-start.25
  708.6 5.0 convolution_add_fusion
  717.8 3.9 collective-permute-done.5
  724.7 8.2 %all-to-all-done.25 = bf16[4,96,1536]{2,1,0:T(8,128)(2,1)S(1)} async-done(((bf16[4,96,1536]{2,1,0:T(8,128)(2,1)}), bf16[4,96,1536]{2,1,0:T(8,128)(2,1)S(1)}, u32[]{:S(2)}, u32[]{:S(2)}) %all-to-all-start.25) | async-done | bytes 1179680 | tf_op jit(solution)/shard_map/all_to_all | solution.py:71
  740.0 4.2 all_to_all.153
  747.0 4.3 all_to_all.154
  (371 shorter events, 210.9 us)
Async XLA Ops:
  0.6 123.4 %copy-start = (bf16[96,3072]{1,0:T(8,128)(2,1)S(1)}, bf16[96,3072]{1,0:T(8,128)(2,1)}, u32[]{:S(2)}) copy-start(bf16[96,3072]{1,0:T(8,128)(2,1)} %param.28) | copy-start | bytes 1769476
  0.7 21.3 %copy-start.41 = (bf16[96,768]{1,0:T(8,128)(2,1)S(1)}, bf16[96,768]{1,0:T(8,128)(2,1)}, u32[]{:S(2)}) copy-start(bf16[96,768]{1,0:T(8,128)(2,1)} %param.21) | copy-start | bytes 442372
  0.7 33.1 %copy-start.66 = (s32[2]{0:T(128)S(1)}, s32[2]{0:T(128)}, u32[]{:S(2)}) copy-start(s32[2]{0:T(128)} %param.32) | copy-start | bytes 28
  0.7 35.0 %copy-start.59 = (bf16[96]{0:T(256)(128)(2,1)S(1)}, bf16[96]{0:T(256)(128)(2,1)}, u32[]{:S(2)}) copy-start(bf16[96]{0:T(256)(128)(2,1)} %param.22) | copy-start | bytes 580
  0.7 34.9 %copy-start.60 = (bf16[96]{0:T(256)(128)(2,1)S(1)}, bf16[96]{0:T(256)(128)(2,1)}, u32[]{:S(2)}) copy-start(bf16[96]{0:T(256)(128)(2,1)} %param.23) | copy-start | bytes 580
  0.7 34.9 %copy-start.61 = (bf16[96]{0:T(256)(128)(2,1)S(1)}, bf16[96]{0:T(256)(128)(2,1)}, u32[]{:S(2)}) copy-start(bf16[96]{0:T(256)(128)(2,1)} %param.26) | copy-start | bytes 580
  0.7 34.9 %copy-start.62 = (bf16[96]{0:T(256)(128)(2,1)S(1)}, bf16[96]{0:T(256)(128)(2,1)}, u32[]{:S(2)}) copy-start(bf16[96]{0:T(256)(128)(2,1)} %param.27) | copy-start | bytes 580
  0.7 34.9 %copy-start.63 = (bf16[96]{0:T(256)(128)(2,1)S(1)}, bf16[96]{0:T(256)(128)(2,1)}, u32[]{:S(2)}) copy-start(bf16[96]{0:T(256)(128)(2,1)} %param.30) | copy-start | bytes 580
  0.7 34.9 %copy-start.64 = (bf16[96]{0:T(256)(128)(2,1)S(1)}, bf16[96]{0:T(256)(128)(2,1)}, u32[]{:S(2)}) copy-start(bf16[96]{0:T(256)(128)(2,1)} %param.31) | copy-start | bytes 580
  0.7 35.0 %copy-start.32 = (s32[2,512]{1,0:T(2,128)S(1)}, s32[2,512]{1,0:T(2,128)}, u32[]{:S(2)}) copy-start(s32[2,512]{1,0:T(2,128)} %param.33) | copy-start | bytes 12292
  0.8 35.8 %copy-start.21 = (bf16[2,512,768]{2,1,0:T(8,128)(2,1)S(1)}, bf16[2,512,768]{2,1,0:T(8,128)(2,1)}, u32[]{:S(2)}) copy-start(bf16[2,512,768]{2,1,0:T(8,128)(2,1)} %param.20) | copy-start | bytes 4718596
  18.4 10.4 %all-to-all-start.9 = ((bf16[2,4,96,384]{3,2,1,0:T(8,128)(2,1)}), bf16[2,4,96,384]{3,2,1,0:T(8,128)(2,1)S(1)}, u32[]{:S(2)}, u32[]{:S(2)}) async-start(bf16[2,4,96,384]{3,2,1,0:T(8,128)(2,1)} %broadcast_in_dim.101), calls=%async_computation.9 | async-start | bytes 1179648 | tf_op jit(solution)/shard_map/all_to_all | solution.py:21
  29.7 18.3 %all-to-all-start = ((bf16[8,96,384]{2,1,0:T(8,128)(2,1)}), bf16[8,96,384]{2,1,0:T(8,128)(2,1)S(1)}, u32[]{:S(2)}, u32[]{:S(2)}) async-start(bf16[8,96,384]{2,1,0:T(8,128)(2,1)} %broadcast_in_dim.81), calls=%async_computation | async-start | bytes 1179648 | tf_op jit(solution)/shard_map/all_to_all | solution.py:21
  53.5 11.2 %all-to-all-start.4 = ((bf16[8,6,96]{2,1,0:T(8,128)(2,1)}), bf16[8,6,96]{2,1,0:T(8,128)(2,1)S(1)}, u32[]{:S(2)}, u32[]{:S(2)}) async-start(bf16[8,6,96]{2,1,0:T(8,128)(2,1)} %broadcast_in_dim.85), calls=%async_computation.4 | async-start | bytes 32768 | tf_op jit(solution)/shard_map/all_to_all | solution.py:21
  63.8 133.9 %copy-start.6 = (f32[2,128,768]{2,1,0:T(8,128)}, f32[2,128,768]{2,1,0:T(8,128)S(1)}, u32[]{:S(2)}) copy-start(f32[2,128,768]{2,1,0:T(8,128)S(1)} %get-tuple-element.262) | copy-start | bytes 2359300
  71.1 13.1 %all-to-all-start.2 = ((f32[8,3,768]{2,1,0:T(4,128)}), f32[8,3,768]{2,1,0:T(4,128)S(1)}, u32[]{:S(2)}, u32[]{:S(2)}) async-start(f32[8,3,768]{2,1,0:T(4,128)} %broadcast_in_dim.83), calls=%async_computation.2 | async-start | bytes 196608 | tf_op jit(solution)/shard_map/all_to_all | solution.py:21
  85.2 24.9 %all-to-all-start.5 = ((bf16[4,96,1152]{2,1,0:T(8,128)(2,1)}), bf16[4,96,1152]{2,1,0:T(8,128)(2,1)S(1)}, u32[]{:S(2)}, u32[]{:S(2)}) async-start(bf16[4,96,1152]{2,1,0:T(8,128)(2,1)} %broadcast_in_dim.92), calls=%async_computation.5 | async-start | bytes 1769472 | tf_op jit(solution)/shard_map/all_to_all | solution.py:21
  120.3 25.4 %all-to-all-start.6 = ((bf16[2,4,96,1152]{3,2,1,0:T(8,128)(2,1)}), bf16[2,4,96,1152]{3,2,1,0:T(8,128)(2,1)S(1)}, u32[]{:S(2)}, u32[]{:S(2)}) async-start(bf16[2,4,96,1152]{3,2,1,0:T(8,128)(2,1)} %broadcast_in_dim.93), calls=%async_computation.6 | async-start | bytes 3538944 | tf_op jit(solution)/shard_map/all_to_all | solution.py:21
  147.8 32.4 %all-to-all-start.11 = ((bf16[4,96,1536]{2,1,0:T(8,128)(2,1)}), bf16[4,96,1536]{2,1,0:T(8,128)(2,1)}, u32[]{:S(2)}, u32[]{:S(2)}) async-start(bf16[4,96,1536]{2,1,0:T(8,128)(2,1)} %broadcast_in_dim.103), calls=%async_computation.11 | async-start | bytes 2359296 | tf_op jit(solution)/shard_map/all_to_all | solution.py:21
  153.3 44.4 %copy-start.37 = (f32[768]{0:T(1024)}, f32[768]{0:T(1024)S(1)}, u32[]{:S(2)}) copy-start(f32[768]{0:T(1024)S(1)} %reshape.424) | copy-start | bytes 9220
  163.5 18.5 %copy-start.27 = (f32[768]{0:T(1024)}, f32[768]{0:T(1024)S(1)}, u32[]{:S(2)}) copy-start(f32[768]{0:T(1024)S(1)} %get-tuple-element.206) | copy-start | bytes 9220
  163.5 34.3 %copy-start.30 = (f32[768]{0:T(1024)}, f32[768]{0:T(1024)S(1)}, u32[]{:S(2)}) copy-start(f32[768]{0:T(1024)S(1)} %div.112) | copy-start | bytes 9220
  163.6 34.2 %copy-start.35 = (f32[768]{0:T(1024)}, f32[768]{0:T(1024)S(1)}, u32[]{:S(2)}) copy-start(f32[768]{0:T(1024)S(1)} %add_rsqrt_fusion) | copy-start | bytes 9220
  192.5 38.2 %all-to-all-start.12 = ((bf16[2,4,96,1536]{3,2,1,0:T(8,128)(2,1)}), bf16[2,4,96,1536]{3,2,1,0:T(8,128)(2,1)}, u32[]{:S(2)}, u32[]{:S(2)}) async-start(bf16[2,4,96,1536]{3,2,1,0:T(8,128)(2,1)} %broadcast_in_dim.104), calls=%async_computation.12 | async-start | bytes 4718592 | tf_op jit(solution)/shard_map/all_to_all | solution.py:21
  231.8 33.9 %all-to-all-start.14 = ((bf16[4,384,384]{2,1,0:T(8,128)(2,1)}), bf16[4,384,384]{2,1,0:T(8,128)(2,1)}, u32[]{:S(2)}, u32[]{:S(2)}) async-start(bf16[4,384,384]{2,1,0:T(8,128)(2,1)} %broadcast_in_dim.106), calls=%async_computation.14 | async-start | bytes 2359296 | tf_op jit(solution)/shard_map/all_to_all | solution.py:21
  277.7 32.2 %all-to-all-start.15 = ((bf16[2,4,384,384]{3,2,1,0:T(8,128)(2,1)}), bf16[2,4,384,384]{3,2,1,0:T(8,128)(2,1)S(1)}, u32[]{:S(2)}, u32[]{:S(2)}) async-start(bf16[2,4,384,384]{3,2,1,0:T(8,128)(2,1)} %broadcast_in_dim.107), calls=%async_computation.15 | async-start | bytes 4718592 | tf_op jit(solution)/shard_map/all_to_all | solution.py:21
  286.5 146.6 %copy-start.39 = (f32[2,512]{1,0:T(2,128)}, f32[2,512]{1,0:T(2,128)S(1)}, u32[]{:S(2)}) copy-start(f32[2,512]{1,0:T(2,128)S(1)} %broadcast_multiply_fusion.1) | copy-start | bytes 12292
  288.7 144.5 %copy-start.46 = (f32[2,512]{1,0:T(2,128)}, f32[2,512]{1,0:T(2,128)S(1)}, u32[]{:S(2)}) copy-start(f32[2,512]{1,0:T(2,128)S(1)} %fusion.62) | copy-start | bytes 12292
  354.6 31.0 %copy-start.9 = (f32[2,512,3072]{2,1,0:T(8,128)}, f32[2,512,3072]{2,1,0:T(8,128)S(1)}, u32[]{:S(2)}) copy-start(f32[2,512,3072]{2,1,0:T(8,128)S(1)} %get-tuple-element.265) | copy-start | bytes 37748740
  354.6 31.0 %copy-start.4 = (f32[2,512,768]{2,1,0:T(8,128)S(1)}, f32[2,512,768]{2,1,0:T(8,128)}, u32[]{:S(2)}) copy-start(f32[2,512,768]{2,1,0:T(8,128)} %copy-done.3) | copy-start | bytes 9437188
  354.6 31.1 %copy-start.18 = (bf16[3072,768,1]{1,0,2:T(8,128)(2,1)S(1)}, bf16[3072,768,1]{1,0,2:T(8,128)(2,1)}, u32[]{:S(2)}) copy-start(bf16[3072,768,1]{1,0,2:T(8,128)(2,1)} %reshape.444) | copy-start | bytes 14155780
  437.1 79.1 %copy-start.56 = (f32[2,512]{1,0:T(2,128)S(1)}, f32[2,512]{1,0:T(2,128)}, u32[]{:S(2)}) copy-start(f32[2,512]{1,0:T(2,128)} %copy-done.55) | copy-start | bytes 12292
  528.9 12.2 %all-to-all-start.17 = ((f32[8,6,768]{2,1,0:T(8,128)}), f32[8,6,768]{2,1,0:T(8,128)S(1)}, u32[]{:S(2)}, u32[]{:S(2)}) async-start(f32[8,6,768]{2,1,0:T(8,128)} %broadcast_in_dim.114), calls=%async_computation.17 | async-start | bytes 393216 | tf_op jit(solution)/shard_map/all_to_all | solution.py:21
  532.8 16.7 %copy-start.28 = (f32[768]{0:T(1024)S(1)}, f32[768]{0:T(1024)}, u32[]{:S(2)}) copy-start(f32[768]{0:T(1024)} %copy-done.27) | copy-start | bytes 9220
  532.8 16.7 %copy-start.38 = (f32[768]{0:T(1024)S(1)}, f32[768]{0:T(1024)}, u32[]{:S(2)}) copy-start(f32[768]{0:T(1024)} %copy-done.37) | copy-start | bytes 9220
  532.8 16.7 %copy-start.50 = (f32[2,128]{1,0:T(2,128)S(1)}, f32[2,128]{1,0:T(2,128)}, u32[]{:S(2)}) copy-start(f32[2,128]{1,0:T(2,128)} %compare_convert_fusion) | copy-start | bytes 3076
  541.7 7.7 %all-to-all-start.18 = ((f32[4,6,768]{2,1,0:T(8,128)}), f32[4,6,768]{2,1,0:T(8,128)S(1)}, u32[]{:S(2)}, u32[]{:S(2)}) async-start(f32[4,6,768]{2,1,0:T(8,128)} %broadcast_in_dim.115), calls=%async_computation.18 | async-start | bytes 196608 | tf_op jit(solution)/shard_map/all_to_all | solution.py:21
  546.1 14.3 %collective-permute-start.6 = (bf16[768,384]{1,0:T(8,128)(2,1)}, bf16[768,384]{1,0:T(8,128)(2,1)}, u32[]{:S(2)}, u32[]{:S(2)}) collective-permute-start(bf16[768,384]{1,0:T(8,128)(2,1)} %constant_dynamic-slice_fusion.3), channel_id=1, source_target_pairs={{0,8},{8,0},{16,24},{24,16},{1,9},{9,1},{17,25},{25,17},{2,10},{10... | collective-permute-start | bytes 1769480 | tf_op jit(solution)/shard_map/ppermute | solution.py:50
  550.5 9.9 %collective-permute-start = (bf16[768,384]{1,0:T(8,128)(2,1)S(1)}, bf16[768,384]{1,0:T(8,128)(2,1)S(1)}, u32[]{:S(2)}, u32[]{:S(2)}) collective-permute-start(bf16[768,384]{1,0:T(8,128)(2,1)S(1)} %constant_dynamic-slice_fusion.6), channel_id=1, source_target_pairs={{0,8},{8,0},{16,24},{24,16},{1,9},{9,1},{17,25},{25,17},{2,10},{10... | collective-permute-start | bytes 1769480 | tf_op jit(solution)/shard_map/ppermute | solution.py:50
  561.8 10.0 %collective-permute-start.7 = (bf16[4,96,384]{2,1,0:T(8,128)(2,1)S(1)}, bf16[4,96,384]{2,1,0:T(8,128)(2,1)S(1)}, u32[]{:S(2)}, u32[]{:S(2)}) collective-permute-start(bf16[4,96,384]{2,1,0:T(8,128)(2,1)S(1)} %dynamic-slice_bitcast_fusion.6), channel_id=1, source_target_pairs={{0,1},{1,0},{2,3},{3,2},{4,5},{5,4},{6,7},{7,6},{8,9},{9,8},{10,11... | collective-permute-start | bytes 884744 | tf_op jit(solution)/shard_map/ppermute | solution.py:50
  564.5 47.4 %collective-permute-start.12 = (bf16[3072,384]{1,0:T(8,128)(2,1)}, bf16[3072,384]{1,0:T(8,128)(2,1)S(1)}, u32[]{:S(2)}, u32[]{:S(2)}) collective-permute-start(bf16[3072,384]{1,0:T(8,128)(2,1)} %constant_dynamic-slice_fusion.1), channel_id=1, source_target_pairs={{0,8},{8,0},{16,24},{24,16},{1,9},{9,1},{17,25},{25,17},{2,10},{10... | collective-permute-start | bytes 7077896 | tf_op jit(solution)/shard_map/ppermute | solution.py:50
  565.3 21.9 %copy-start.40 = (f32[2,512]{1,0:T(2,128)S(1)}, f32[2,512]{1,0:T(2,128)}, u32[]{:S(2)}) copy-start(f32[2,512]{1,0:T(2,128)} %copy-done.39) | copy-start | bytes 12292
  565.3 21.9 %copy-start.45 = (f32[768]{0:T(1024)S(1)}, f32[768]{0:T(1024)}, u32[]{:S(2)}) copy-start(f32[768]{0:T(1024)} %reshape.426) | copy-start | bytes 9220
  565.3 21.9 %copy-start.47 = (f32[2,512]{1,0:T(2,128)S(1)}, f32[2,512]{1,0:T(2,128)}, u32[]{:S(2)}) copy-start(f32[2,512]{1,0:T(2,128)} %copy-done.46) | copy-start | bytes 12292
  565.3 22.0 %copy-start.54 = (f32[768]{0:T(1024)S(1)}, f32[768]{0:T(1024)}, u32[]{:S(2)}) copy-start(f32[768]{0:T(1024)} %reshape.427) | copy-start | bytes 9220
  565.3 14.2 %collective-permute-start.1 = (bf16[4,96,384]{2,1,0:T(8,128)(2,1)}, bf16[4,96,384]{2,1,0:T(8,128)(2,1)}, u32[]{:S(2)}, u32[]{:S(2)}) collective-permute-start(bf16[4,96,384]{2,1,0:T(8,128)(2,1)} %dynamic-slice_bitcast_fusion.7), channel_id=1, source_target_pairs={{0,1},{1,0},{2,3},{3,2},{4,5},{5,4},{6,7},{7,6},{8,9},{9,8},{10,11... | collective-permute-start | bytes 884744 | tf_op jit(solution)/shard_map/ppermute | solution.py:50
  572.5 11.2 %all-to-all-start.23 = ((bf16[4,96,384]{2,1,0:T(8,128)(2,1)}), bf16[4,96,384]{2,1,0:T(8,128)(2,1)}, u32[]{:S(2)}, u32[]{:S(2)}) async-start(bf16[4,96,384]{2,1,0:T(8,128)(2,1)} %fusion.36), calls=%async_computation.23 | async-start | bytes 589824 | tf_op jit(solution)/shard_map/all_to_all | solution.py:71
  579.5 28.9 %collective-permute-start.3 = (bf16[768,1152]{1,0:T(8,128)(2,1)}, bf16[768,1152]{1,0:T(8,128)(2,1)}, u32[]{:S(2)}, u32[]{:S(2)}) collective-permute-start(bf16[768,1152]{1,0:T(8,128)(2,1)} %constant_dynamic-slice_fusion.4), channel_id=1, source_target_pairs={{0,8},{8,0},{16,24},{24,16},{1,9},{9,1},{17,25},{25,17},{2,10},{10... | collective-permute-start | bytes 5308424 | tf_op jit(solution)/shard_map/ppermute | solution.py:50
  583.7 19.6 %all-to-all-start.19 = ((bf16[4,96,384]{2,1,0:T(8,128)(2,1)}), bf16[4,96,384]{2,1,0:T(8,128)(2,1)S(1)}, u32[]{:S(2)}, u32[]{:S(2)}) async-start(bf16[4,96,384]{2,1,0:T(8,128)(2,1)} %fusion.37), calls=%async_computation.19 | async-start | bytes 589824 | tf_op jit(solution)/shard_map/all_to_all | solution.py:71
  598.7 5.4 collective-permute-start.8
  603.4 40.3 %collective-permute-start.9 = (bf16[768,1536]{1,0:T(8,128)(2,1)}, bf16[768,1536]{1,0:T(8,128)(2,1)}, u32[]{:S(2)}, u32[]{:S(2)}) collective-permute-start(bf16[768,1536]{1,0:T(8,128)(2,1)} %constant_dynamic-slice_fusion.2), channel_id=1, source_target_pairs={{0,8},{8,0},{16,24},{24,16},{1,9},{9,1},{17,25},{25,17},{2,10},{10... | collective-permute-start | bytes 7077896 | tf_op jit(solution)/shard_map/ppermute | solution.py:50
  603.4 4.9 collective-permute-start.2
  604.9 29.6 %all-to-all-start.24 = ((bf16[2,96,384]{2,1,0:T(8,128)(2,1)}), bf16[2,96,384]{2,1,0:T(8,128)(2,1)S(1)}, u32[]{:S(2)}, u32[]{:S(2)}) async-start(bf16[2,96,384]{2,1,0:T(8,128)(2,1)} %broadcast_in_dim.118), calls=%async_computation.24 | async-start | bytes 294912 | tf_op jit(solution)/shard_map/all_to_all | solution.py:21
  610.9 22.5 %collective-permute-start.4 = (bf16[4,96,1152]{2,1,0:T(8,128)(2,1)S(1)}, bf16[4,96,1152]{2,1,0:T(8,128)(2,1)S(1)}, u32[]{:S(2)}, u32[]{:S(2)}) collective-permute-start(bf16[4,96,1152]{2,1,0:T(8,128)(2,1)S(1)} %dynamic-slice_bitcast_fusion.5), channel_id=1, source_target_pairs={{0,1},{1,0},{2,3},{3,2},{4,5},{5,4},{6,7},{7,6},{8,9},{9,8},{10,11... | collective-permute-start | bytes 2654216 | tf_op jit(solution)/shard_map/ppermute | solution.py:50
  616.8 41.5 %collective-permute-start.13 = (bf16[4,384,384]{2,1,0:T(8,128)(2,1)}, bf16[4,384,384]{2,1,0:T(8,128)(2,1)}, u32[]{:S(2)}, u32[]{:S(2)}) collective-permute-start(bf16[4,384,384]{2,1,0:T(8,128)(2,1)} %dynamic-slice_bitcast_fusion.3), channel_id=1, source_target_pairs={{0,1},{1,0},{2,3},{3,2},{4,5},{5,4},{6,7},{7,6},{8,9},{9,8},{10,11... | collective-permute-start | bytes 3538952 | tf_op jit(solution)/shard_map/ppermute | solution.py:50
  638.4 27.9 %all-to-all-start.21 = ((bf16[4,96,1152]{2,1,0:T(8,128)(2,1)}), bf16[4,96,1152]{2,1,0:T(8,128)(2,1)}, u32[]{:S(2)}, u32[]{:S(2)}) async-start(bf16[4,96,1152]{2,1,0:T(8,128)(2,1)} %fusion.33), calls=%async_computation.21 | async-start | bytes 1769472 | tf_op jit(solution)/shard_map/all_to_all | solution.py:71
  666.3 35.3 %all-to-all-start.27 = ((bf16[4,384,384]{2,1,0:T(8,128)(2,1)}), bf16[4,384,384]{2,1,0:T(8,128)(2,1)}, u32[]{:S(2)}, u32[]{:S(2)}) async-start(bf16[4,384,384]{2,1,0:T(8,128)(2,1)} %fusion.29), calls=%async_computation.27 | async-start | bytes 2359296 | tf_op jit(solution)/shard_map/all_to_all | solution.py:71
  671.7 35.2 %copy-start.58 = (f32[2,128]{1,0:T(2,128)S(1)}, f32[2,128]{1,0:T(2,128)}, u32[]{:S(2)}) copy-start(f32[2,128]{1,0:T(2,128)} %copy-done.57) | copy-start | bytes 3076
  671.7 27.3 %collective-permute-start.10 = (bf16[4,96,1536]{2,1,0:T(8,128)(2,1)}, bf16[4,96,1536]{2,1,0:T(8,128)(2,1)}, u32[]{:S(2)}, u32[]{:S(2)}) collective-permute-start(bf16[4,96,1536]{2,1,0:T(8,128)(2,1)} %dynamic-slice_bitcast_fusion.4), channel_id=1, source_target_pairs={{0,1},{1,0},{2,3},{3,2},{4,5},{5,4},{6,7},{7,6},{8,9},{9,8},{10,11... | collective-permute-start | bytes 3538952 | tf_op jit(solution)/shard_map/ppermute | solution.py:50
  701.6 31.4 %all-to-all-start.25 = ((bf16[4,96,1536]{2,1,0:T(8,128)(2,1)}), bf16[4,96,1536]{2,1,0:T(8,128)(2,1)S(1)}, u32[]{:S(2)}, u32[]{:S(2)}) async-start(bf16[4,96,1536]{2,1,0:T(8,128)(2,1)} %fusion.30), calls=%async_computation.25 | async-start | bytes 2359296 | tf_op jit(solution)/shard_map/all_to_all | solution.py:71
  715.7 6.0 collective-permute-start.5
  723.3 16.6 %collective-permute-start.14 = (bf16[384,384]{1,0:T(8,128)(2,1)S(1)}, bf16[384,384]{1,0:T(8,128)(2,1)S(1)}, u32[]{:S(2)}, u32[]{:S(2)}) collective-permute-start(bf16[384,384]{1,0:T(8,128)(2,1)S(1)} %reduce_sum.360), channel_id=1, source_target_pairs={{0,16},{8,24},{16,0},{24,8},{1,17},{9,25},{17,1},{25,9},{2,18},{10... | collective-permute-start | bytes 884744 | tf_op jit(solution)/shard_map/ppermute | solution.py:50
  733.7 5.2 all-to-all-start.22
  737.4 9.5 %collective-permute-start.11 = (bf16[96,1536]{1,0:T(8,128)(2,1)S(1)}, bf16[96,1536]{1,0:T(8,128)(2,1)S(1)}, u32[]{:S(2)}, u32[]{:S(2)}) collective-permute-start(bf16[96,1536]{1,0:T(8,128)(2,1)S(1)} %reduce_sum.359), channel_id=1, source_target_pairs={{0,16},{8,24},{16,0},{24,8},{1,17},{9,25},{17,1},{25,9},{2,18},{10... | collective-permute-start | bytes 884744 | tf_op jit(solution)/shard_map/ppermute | solution.py:50
  (47 other events, 342.4 us)

commit v2 on v1

v2 whole, which is shorter than its diff:
```python
import functools

import jax
import jax.numpy as jnp
from jax import lax
from jax.experimental import pallas as pl
from jax.experimental.pallas import tpu as pltpu
from jax.sharding import PartitionSpec as P

HEADS = 12
SEGMAX = 128
low = jnp.bfloat16
wide = jnp.float32
eps_norm = 1e-05
eps_batch = 1e-05
masked_score = -1e30
highest_precision = lax.Precision.HIGHEST

NN = (((1,), (0,)), ((), ()))
NT = (((1,), (1,)), ((), ()))
TN = (((0,), (0,)), ((), ()))

tail_spread = 0.39 * 2**-0.5
tail_poly = [
    0.5 * value
    for value in (
        0.22003657898400666,
        0.21993814342134163,
        0.20469834418114297,
        0.1590209501745049,
        0.17253866336379592,
        -0.06413901990527864,
        0.25209925299909935,
        -0.21837884731666118,
        0.05418596701413587,
    )
]


def dot(left, right, dims=NN):
    return lax.dot_general(left, right, dims, preferred_element_type=wide)


def shape(dims, dtype=low):
    return jax.ShapeDtypeStruct(dims, dtype)


def call(kernel, name, grid, in_specs, out_specs, out_shape, scratch=(), aliases=None, cost=None):
    return pl.pallas_call(
        kernel,
        name=name,
        grid_spec=pltpu.PrefetchScalarGridSpec(
            num_scalar_prefetch=1,
            grid=grid,
            in_specs=in_specs,
            out_specs=out_specs,
            scratch_shapes=list(scratch),
        ),
        out_shape=out_shape,
        input_output_aliases=aliases or {},
        cost_estimate=cost,
        compiler_params=pltpu.CompilerParams(vmem_limit_bytes=56 * 2**20),
    )


def cost(flops, moved):
    return pl.CostEstimate(flops=int(flops), bytes_accessed=int(moved), transcendentals=0)


def pair_groups(size):
    return [[i, i + 1] for i in range(0, size, 2)]


def line_groups(size):
    return [list(range(0, size, 2)), list(range(1, size, 2))]


def spread(value, axis, groups, count):
    copies = jnp.broadcast_to(value[None], (count,) + value.shape)
    return lax.all_to_all(copies, axis, 0, 0, axis_index_groups=groups)


def swap(value, axis, bit):
    size = lax.axis_size(axis)
    return lax.ppermute(value, axis, [(i, i ^ bit) for i in range(size)])


def half_of(value, index):
    half = value.shape[-1] // 2
    return lax.dynamic_slice_in_dim(value, index * half, half, value.ndim - 1)


def gather_quick(mine):
    fsdp = lax.axis_size("fsdp")
    own = spread(mine, "fsdp", None, fsdp).reshape((fsdp * mine.shape[0],) + mine.shape[1:])
    return own, swap(own, "dp", 1)


def gather_bulk(mine):
    own = lax.all_gather(mine, "fsdp", axis=0, tiled=True)
    return own, swap(own, "dp", 1)


def join(own, other, core):
    return jnp.where(
        core == 0,
        jnp.concatenate([own, other], axis=-1),
        jnp.concatenate([other, own], axis=-1),
    )


def add_low(left, right):
    return (left.astype(wide) + right.astype(wide)).astype(low)


def finish(total, core):
    bit = 2
    while bit < lax.axis_size("dp"):
        total = add_low(total, swap(total, "dp", bit))
        bit *= 2
    return total, swap(total, "dp", 1)


def scatter_bulk(keep, give, core):
    chip = add_low(keep, swap(give, "dp", 1))
    return finish(lax.psum_scatter(chip, "fsdp", scatter_dimension=0, tiled=True), core)


def scatter_quick(keep, give, core):
    rows, half = keep.shape
    fsdp = lax.axis_size("fsdp")
    side = lax.axis_index("fsdp") % 2
    chip = add_low(keep, swap(give, "dp", 1)).reshape(fsdp // 2, 2, rows // fsdp, half)
    keep = lax.dynamic_index_in_dim(chip, side, 1, False)
    give = lax.dynamic_index_in_dim(chip, 1 - side, 1, False)
    pair = add_low(keep, swap(give, "fsdp", 1))
    parts = lax.all_to_all(pair, "fsdp", 0, 0, axis_index_groups=line_groups(fsdp))
    return finish(jnp.sum(parts.astype(wide), axis=0).astype(low), core)


def project_kernel(core_ref, x_ref, own_ref, other_ref, out_ref):
    @pl.when(pl.program_id(0) == 0)
    def _():
        out_ref[...] = dot(x_ref[...], own_ref[...]).astype(low)

    @pl.when(pl.program_id(0) == 1)
    def _():
        out_ref[...] = dot(x_ref[...], other_ref[...]).astype(low)


def project(x, own, other, core):
    rows, features = x.shape
    half = features // 2
    parts = own.shape[1] // half
    return call(
        project_kernel,
        "project",
        (2, parts),
        [
            pl.BlockSpec((rows, features), lambda s, j, c: (0, 0)),
            pl.BlockSpec((features, half), lambda s, j, c: (0, jnp.where(s == 0, j, parts - 1))),
            pl.BlockSpec((features, half), lambda s, j, c: (0, jnp.where(s == 1, j, 0))),
        ],
        pl.BlockSpec((rows, half), lambda s, j, c: (0, 2 * j + jnp.where(s == 0, c[0], 1 - c[0]))),
        shape((rows, 2 * own.shape[1])),
        cost=cost(4 * rows * features * own.shape[1], 2 * (rows * features + 2 * own.size * 3)),
    )(core, x, own, other)


def attend_kernel(core_ref, q_ref, k_ref, v_ref, mask_ref, out_ref, share_ref):
    queries, keys, values = q_ref[...], k_ref[...], v_ref[...]
    first = lax.broadcasted_iota(jnp.int32, queries.shape, 1) < queries.shape[1] // 2
    real = mask_ref[...] > 0
    mixed = []
    for head in range(2):
        mine = first if head == 0 else jnp.logical_not(first)
        scaled = jnp.where(mine, queries, jnp.zeros_like(queries)) * jnp.asarray(0.125, low)
        scores = jnp.where(real, dot(scaled, keys, NT), masked_score)
        raised = jnp.exp(scores - jnp.max(scores, axis=-1, keepdims=True))
        share = (raised * (1.0 / jnp.sum(raised, axis=-1, keepdims=True))).astype(low)
        share_ref[head] = share
        mixed.append(dot(share, values))
    out_ref[...] = jnp.where(first, mixed[0], mixed[1]).astype(low)


def column_spec(length, offset):
    return pl.BlockSpec((None, length, 128), lambda d, h, c: (d, 0, h + offset))


def attend(packed, mask, core):
    docs, length, columns = packed.shape
    pairs = columns // 3 // 128
    return call(
        attend_kernel,
        "attend",
        (docs, pairs),
        [
            column_spec(length, 0),
            column_spec(length, pairs),
            column_spec(length, 2 * pairs),
            pl.BlockSpec((None, 1, length), lambda d, h, c: (d, 0, 0)),
        ],
        [
            column_spec(length, 0),
            pl.BlockSpec((None, 2, length, length), lambda d, h, c: (d, h, 0, 0)),
        ],
        [
            shape((docs, length, columns // 3)),
            shape((docs, 2 * pairs, length, length)),
        ],
        cost=cost(docs * pairs * 8 * length * length * 256, docs * pairs * 4 * length * length),
    )(core, packed, packed, packed, mask[:, None, :])


def attend_back_kernel(core_ref, q_ref, k_ref, v_ref, share_ref, delta_ref, mixed_ref, out_ref):
    queries, keys, values, delta = q_ref[...], k_ref[...], v_ref[...], delta_ref[...]
    half = queries.shape[1] // 2
    first = lax.broadcasted_iota(jnp.int32, queries.shape, 1) < half
    product = delta.astype(wide) * mixed_ref[...].astype(wide)
    queries_t, delta_t = queries.T, delta.T
    for_queries, for_keys, for_values = [], [], []
    for head in range(2):
        mine = first if head == 0 else jnp.logical_not(first)
        delta_share = dot(jnp.where(mine, delta, jnp.zeros_like(delta)), values, NT)
        row = jnp.sum(jnp.where(mine, product, 0.0), axis=-1, keepdims=True)
        share = share_ref[head]
        delta_scores = (share.astype(wide) * (delta_share - row)).astype(low)
        for_queries.append(dot(delta_scores, keys))
        for_keys.append(dot(queries_t[half * head : half * (head + 1)], delta_scores))
        for_values.append(dot(delta_t[half * head : half * (head + 1)], share))
    out_ref[0] = (jnp.where(first, for_queries[0], for_queries[1]) * 0.125).astype(low)
    out_ref[1] = (jnp.concatenate(for_keys, 0) * 0.125).astype(low).T
    out_ref[2] = jnp.concatenate(for_values, 0).astype(low).T


def attend_back(packed, share, delta, mixed, core):
    docs, length, columns = packed.shape
    pairs = columns // 3 // 128
    return call(
        attend_back_kernel,
        "attend_back",
        (docs, pairs),
        [
            column_spec(length, 0),
            column_spec(length, pairs),
            column_spec(length, 2 * pairs),
            pl.BlockSpec((None, 2, length, length), lambda d, h, c: (d, h, 0, 0)),
            column_spec(length, 0),
            column_spec(length, 0),
        ],
        pl.BlockSpec((3, None, length, 128), lambda d, h, c: (0, d, 0, h)),
        shape((3, docs, length, columns // 3)),
        cost=cost(docs * pairs * 20 * length * length * 128, docs * pairs * 4 * length * length),
    )(core, packed, packed, packed, share, delta, mixed)


def gelu_parts(value):
    ratio = 1.0 / (1.0 + tail_spread * jnp.abs(value))
    poly = tail_poly[-1]
    for coefficient in tail_poly[-2::-1]:
        poly = poly * ratio + coefficient
    bell = jnp.exp(-0.5 * value * value)
    tail = poly * ratio * bell
    below = jnp.where(value < 0, tail, 1.0 - tail)
    return value * below, below + value * (bell * 0.3989422804014327)


def up_kernel(core_ref, x_ref, own_ref, other_ref, out_ref, slope_ref):
    def block(weight):
        value, slope = gelu_parts(dot(x_ref[...], weight))
        out_ref[...] = value.astype(low)
        slope_ref[...] = slope.astype(low)

    @pl.when(pl.program_id(0) == 0)
    def _():
        block(own_ref[...])

    @pl.when(pl.program_id(0) == 1)
    def _():
        block(other_ref[...])


def up(x, own, other, core, columns=512, rows=512):
    count, features = x.shape
    half = own.shape[1]
    steps = half // columns
    out = pl.BlockSpec(
        (rows, columns), lambda s, j, i, c: (i, j + steps * jnp.where(s == 0, c[0], 1 - c[0]))
    )
    return call(
        up_kernel,
        "up",
        (2, steps, count // rows),
        [
            pl.BlockSpec((rows, features), lambda s, j, i, c: (i, 0)),
            pl.BlockSpec((features, columns), lambda s, j, i, c: (0, jnp.where(s == 0, j, steps - 1))),
            pl.BlockSpec((features, columns), lambda s, j, i, c: (0, jnp.where(s == 1, j, 0))),
        ],
        [out, out],
        [shape((count, 2 * half))] * 2,
        cost=cost(4 * count * features * half, 4 * (features * half + 2 * count * half)),
    )(core, x, own, other)


def normalize(value):
    center = value - jnp.mean(value, axis=-1, keepdims=True)
    scale = lax.rsqrt(jnp.mean(center * center, axis=-1, keepdims=True) + eps_norm)
    return center * scale, scale


def normalize_back(scale, unit, delta):
    return scale * (
        delta
        - jnp.mean(delta, axis=-1, keepdims=True)
        - unit * jnp.mean(delta * unit, axis=-1, keepdims=True)
    )


def merge_kernel(core_ref, x_ref, joined_ref, weight_ref, vectors_ref, sum_ref, low_ref):
    total = joined_ref[...] + dot(x_ref[...], weight_ref[...])
    sum_ref[...] = total
    unit, _ = normalize(total)
    low_ref[...] = (unit * vectors_ref[0:1, :] + vectors_ref[1:2, :]).astype(low)


def merge(x, joined, weight, vectors, core, rows=256):
    count, features = x.shape
    block = pl.BlockSpec((rows, features), lambda i, c: (i, 0))
    return call(
        merge_kernel,
        "merge",
        (count // rows,),
        [
            block,
            block,
            pl.BlockSpec(weight.shape, lambda i, c: (0, 0)),
            pl.BlockSpec(vectors.shape, lambda i, c: (0, 0)),
        ],
        [block, block],
        [shape((count, features), wide), shape((count, features))],
        cost=cost(2 * count * features * features, 14 * count * features),
    )(core, x, joined, weight, vectors)


def fetch(own, other, target, sems, core):
    half = own.shape[1]
    mine = pl.multiple_of(core * half, 128)
    theirs = pl.multiple_of((1 - core) * half, 128)
    return (
        pltpu.make_async_copy(own, target.at[:, pl.ds(mine, half)], sems.at[0]),
        pltpu.make_async_copy(other, target.at[:, pl.ds(theirs, half)], sems.at[1]),
    )


def down_kernel(
    core_ref,
    x_ref,
    sum_ref,
    cotangent_ref,
    vectors_ref,
    own_ref,
    other_ref,
    out_ref,
    delta_ref,
    low_ref,
    sums_ref,
    weight,
    sems,
):
    @pl.when(pl.program_id(0) == 0)
    def _():
        copies = fetch(own_ref, other_ref, weight, sems, core_ref[0])
        for copy in copies:
            copy.start()
        sums_ref[...] = jnp.zeros_like(sums_ref)
        for copy in copies:
            copy.wait()

    unit, _ = normalize(sum_ref[...])
    hidden = unit * vectors_ref[0:1, :] + vectors_ref[1:2, :]
    unit, scale = normalize(hidden + dot(x_ref[...], weight[...]))
    out_ref[...] = unit * vectors_ref[2:3, :] + vectors_ref[3:4, :]
    given = cotangent_ref[...].astype(wide)
    delta = normalize_back(scale, unit, given * vectors_ref[2:3, :])
    delta_ref[...] = delta
    low_ref[...] = delta.astype(low)
    sums_ref[0:1, :] += jnp.sum(given * unit, axis=0, keepdims=True)
    sums_ref[1:2, :] += jnp.sum(given, axis=0, keepdims=True)


def down(x, total, cotangent, vectors, own, other, core, rows=256):
    count, hidden = x.shape
    features = total.shape[1]
    block = pl.BlockSpec((rows, features), lambda i, c: (i, 0))
    return call(
        down_kernel,
        "down",
        (count // rows,),
        [
            pl.BlockSpec((rows, hidden), lambda i, c: (i, 0)),
            block,
            block,
            pl.BlockSpec(vectors.shape, lambda i, c: (0, 0)),
            pl.BlockSpec(memory_space=pl.ANY),
            pl.BlockSpec(memory_space=pl.ANY),
        ],
        [block, block, block, pl.BlockSpec((8, features), lambda i, c: (0, 0))],
        [
            shape((count, features), wide),
            shape((count, features), wide),
            shape((count, features)),
            shape((8, features), wide),
        ],
        [pltpu.VMEM((hidden, features), low), pltpu.SemaphoreType.DMA((2,))],
        cost=cost(2 * count * features * hidden, 12 * count * features + 4 * count * hidden),
    )(core, x, total, cotangent, vectors, own, other)


def inner_kernel(
    core_ref,
    low_ref,
    delta_ref,
    slope_ref,
    sum_ref,
    vectors_ref,
    merge_ref,
    down_own_ref,
    down_other_ref,
    up_own_ref,
    up_other_ref,
    inner_ref,
    one_ref,
    one_low_ref,
    mixed_ref,
    sums_ref,
    down_weight,
    up_weight,
    sems,
):
    core = core_ref[0]

    def copies():
        return (
            *fetch(down_own_ref, down_other_ref, down_weight, sems.at[0], core),
            *fetch(up_own_ref, up_other_ref, up_weight, sems.at[1], core),
        )

    @pl.when(pl.program_id(0) == 0)
    def _():
        started = copies()
        for copy in started:
            copy.start()
        sums_ref[...] = jnp.zeros_like(sums_ref)
        for copy in started:
            copy.wait()

    inner = (dot(low_ref[...], down_weight[...], NT) * slope_ref[...].astype(wide)).astype(low)
    inner_ref[...] = inner
    delta = delta_ref[...] + dot(inner, up_weight[...], NT)
    unit, scale = normalize(sum_ref[...])
    one = normalize_back(scale, unit, delta * vectors_ref[0:1, :])
    one_ref[...] = one
    one_low = one.astype(low)
    one_low_ref[...] = one_low
    mixed_ref[...] = dot(one_low, merge_ref[...], NT).astype(low)
    sums_ref[0:1, :] += jnp.sum(delta * unit, axis=0, keepdims=True)
    sums_ref[1:2, :] += jnp.sum(delta, axis=0, keepdims=True)


def inner_back(branch, delta, slope, total, vectors, weight, downs, ups, core, rows=256):
    count, hidden = slope.shape
    features = total.shape[1]
    block = pl.BlockSpec((rows, features), lambda i, c: (i, 0))
    tall = pl.BlockSpec((rows, hidden), lambda i, c: (i, 0))
    anywhere = pl.BlockSpec(memory_space=pl.ANY)
    return call(
        inner_kernel,
        "inner_back",
        (count // rows,),
        [
            block,
            block,
            tall,
            block,
            pl.BlockSpec(vectors.shape, lambda i, c: (0, 0)),
            pl.BlockSpec(weight.shape, lambda i, c: (0, 0)),
            anywhere,
            anywhere,
            anywhere,
            anywhere,
        ],
        [tall, block, block, block, pl.BlockSpec((8, features), lambda i, c: (0, 0))],
        [
            shape((count, hidden)),
            shape((count, features), wide),
            shape((count, features)),
            shape((count, features)),
            shape((8, features), wide),
        ],
        [
            pltpu.VMEM((hidden, features), low),
            pltpu.VMEM((features, hidden), low),
            pltpu.SemaphoreType.DMA((2, 2)),
        ],
        cost=cost(4 * count * features * hidden, 16 * count * features + 8 * count * hidden),
    )(core, branch, delta, slope, total, vectors, weight, *downs, *ups)


def columns_kernel(core_ref, left_ref, own_ref, other_ref, keep_ref, give_ref):
    half = own_ref.shape[-1]
    both = jnp.concatenate([own_ref[...], other_ref[...]], axis=1)
    total = dot(left_ref[...], both, TN)
    keep_ref[...] = total[:, :half].astype(low)
    give_ref[...] = total[:, half:].astype(low)


def weight_columns(left, right, core, rows=768):
    count, height = left.shape
    parts, _, width = right.shape
    half = width // 2
    steps = height // rows
    out = pl.BlockSpec((rows, half), lambda p, j, c: (j, p))
    return call(
        columns_kernel,
        "weight_columns",
        (parts, steps),
        [
            pl.BlockSpec((count, rows), lambda p, j, c: (0, j)),
            pl.BlockSpec((None, count, half), lambda p, j, c: (p, 0, c[0])),
            pl.BlockSpec((None, count, half), lambda p, j, c: (p, 0, 1 - c[0])),
        ],
        [out, out],
        [shape((height, parts * half))] * 2,
        cost=cost(
            2 * parts * count * height * width, 2 * (count * height + parts * width * (count + height))
        ),
    )(core, left, right, right)


def wide_kernel(core_ref, left_ref, right_ref, keep_ref, give_ref):
    total = dot(left_ref[...], right_ref[...], TN).astype(low)

    @pl.when(pl.program_id(0) == 0)
    def _():
        give_ref[...] = total

    @pl.when(pl.program_id(0) == 1)
    def _():
        keep_ref[...] = total


def weight_wide(left, right, core, columns=768):
    count, height = left.shape
    steps = right.shape[1] // 2 // columns
    return call(
        wide_kernel,
        "weight_wide",
        (2, steps),
        [
            pl.BlockSpec((count, height), lambda s, j, c: (0, 0)),
            pl.BlockSpec(
                (count, columns), lambda s, j, c: (0, j + steps * jnp.where(s == 0, 1 - c[0], c[0]))
            ),
        ],
        [
            pl.BlockSpec((height, columns), lambda s, j, c: (0, jnp.where(s == 1, j, 0))),
            pl.BlockSpec((height, columns), lambda s, j, c: (0, jnp.where(s == 0, j, steps - 1))),
        ],
        [shape((height, right.shape[1] // 2))] * 2,
        cost=cost(2 * count * height * right.shape[1], 2 * (count + height) * right.shape[1]),
    )(core, left, right)


def joined_kernel(core_ref, one_ref, left_ref, right_ref, own_ref, other_ref, out_ref, total):
    part = pl.program_id(1)

    @pl.when(part == 0)
    def _():
        total[...] = one_ref[...]

    both = jnp.concatenate([left_ref[...], right_ref[...]], axis=1)
    weight = jnp.concatenate([own_ref[...], other_ref[...]], axis=1)
    total[...] += dot(both, weight, NT)

    @pl.when(part == pl.num_programs(1) - 1)
    def _():
        out_ref[...] = total[...]


def joined_back(one, packed, own, other, core, rows=1024):
    count, features = one.shape
    parts = packed.shape[0]
    half = features // 2
    block = pl.BlockSpec((rows, features), lambda i, p, c: (i, 0))
    weight = pl.BlockSpec((features, half), lambda i, p, c: (0, p))
    return call(
        joined_kernel,
        "joined_back",
        (count // rows, parts),
        [
            block,
            pl.BlockSpec((None, rows, half), lambda i, p, c: (p, i, c[0])),
            pl.BlockSpec((None, rows, half), lambda i, p, c: (p, i, 1 - c[0])),
            weight,
            weight,
        ],
        block,
        shape((count, features), wide),
        [pltpu.VMEM((rows, features), wide)],
        cost=cost(2 * parts * count * features * features, 14 * count * features),
    )(core, one, packed, packed, own, other)


def shards(
    text_rows,
    visual_matrix,
    batch_gain,
    batch_shift,
    attend_weight,
    merge_weight,
    first_gain,
    first_shift,
    up_matrix,
    down_matrix,
    second_gain,
    second_shift,
    segment_counts,
    segment_ids,
    padding_mask,
    cotangent,
):
    docs, length, features = text_rows.shape
    count = docs * length
    half = features // 2
    dp, fsdp = lax.axis_size("dp"), lax.axis_size("fsdp")
    core = lax.axis_index("dp") % 2
    which = core.reshape(1).astype(jnp.int32)
    piece = features // fsdp

    small = jnp.stack(
        [first_gain, first_shift, second_gain, second_shift, batch_gain, batch_shift]
    )
    visual_own, visual_other = gather_quick(half_of(visual_matrix, core))
    small = spread(small, "fsdp", None, fsdp).transpose(1, 0, 2).reshape(6, features)
    vectors = jnp.pad(small.astype(wide), ((0, 2), (0, 0)))
    full_batch_gain, full_batch_shift = vectors[4], vectors[5]
    mine = half_of(attend_weight.reshape(piece, 3, features), core).reshape(piece, 3 * half)
    attend_own, attend_other = gather_quick(mine)
    merge_own, merge_other = gather_quick(half_of(merge_weight, core))
    ups = gather_bulk(half_of(up_matrix, core))
    downs = gather_bulk(half_of(down_matrix, core))
    full_visual = join(visual_own, visual_other, core)
    full_merge = join(merge_own, merge_other, core)

    slot_index = jnp.arange(SEGMAX)
    matches = segment_ids[:, :, None] == slot_index[None, None, :]
    onehot = matches.astype(low)
    onehot_wide = matches.astype(wide)
    divisor = jnp.maximum(jnp.sum(onehot_wide, axis=1), 1.0)[..., None]
    pooled_segments = (
        jnp.einsum("drs,drc->dsc", onehot, text_rows, preferred_element_type=wide) / divisor
    ).astype(low)
    visual_rows = jnp.einsum(
        "bil,ly->biy", pooled_segments, full_visual, preferred_element_type=wide
    )
    valid_slot = (slot_index[None, :] < segment_counts[:, None]).astype(wide)[..., None]
    local_count = jnp.sum(segment_counts).astype(wide)
    local_sum = jnp.sum(valid_slot * visual_rows, axis=(0, 1))
    local_center = visual_rows - local_sum / local_count
    local_square = jnp.sum(valid_slot * local_center * local_center, axis=(0, 1))
    stats = jnp.stack([local_sum, local_square, jnp.full_like(local_sum, local_count)])
    stats = spread(stats, "fsdp", None, fsdp)
    stats = spread(stats, "dp", None, dp).reshape(-1, 3, features)
    sums, squares, sizes = stats[:, 0], stats[:, 1], stats[:, 2]
    segment_total = jnp.sum(sizes, axis=0)
    batch_center = jnp.sum(sums, axis=0) / segment_total
    center = visual_rows - batch_center
    variance = (
        jnp.sum(squares + sizes * jnp.square(sums / sizes - batch_center), axis=0) / segment_total
    )
    inverse_spread = lax.rsqrt(variance + eps_batch)
    normed = center * inverse_spread
    embedded = (normed * full_batch_gain + full_batch_shift).astype(low)
    joined = text_rows.astype(wide) + jnp.einsum(
        "drs,dsc->drc", onehot, embedded, preferred_element_type=wide
    )
    joined = joined.reshape(count, features)
    joined_low = joined.astype(low)

    packed = project(joined_low, attend_own, attend_other, which).reshape(docs, length, -1)
    attended, share = attend(packed, padding_mask, which)
    flat_attended = attended.reshape(count, features)
    total_one, hidden_low = merge(flat_attended, joined, full_merge, vectors, which)
    activated, slope = up(hidden_low, *ups, which)
    layer_output, delta_two, branch_low, sums_two = down(
        activated, total_one, cotangent.reshape(count, features), vectors, *downs, which
    )

    down_halves = weight_columns(activated, branch_low[None], which)
    down_shard = scatter_bulk(*down_halves, core)
    delta_inner, delta_one, one_low, delta_attended, sums_one = inner_back(
        branch_low, delta_two, slope, total_one, vectors, full_merge, downs, ups, which
    )
    up_halves = weight_wide(hidden_low, delta_inner, which)
    up_shard = scatter_bulk(*up_halves, core)
    merge_halves = weight_columns(flat_attended, one_low[None], which)
    merge_shard = scatter_quick(*merge_halves, core)
    delta_packed = attend_back(
        packed, share, delta_attended.reshape(docs, length, features), attended, which
    ).reshape(3, count, features)
    attend_halves = weight_columns(joined_low, delta_packed, which)
    attend_shard = scatter_quick(*attend_halves, core)
    delta_joined = joined_back(delta_one, delta_packed, attend_own, attend_other, which)
    delta_joined = delta_joined.reshape(docs, length, features)
    delta_embedded = jnp.einsum(
        "drs,drc->dsc",
        onehot_wide,
        delta_joined,
        precision=highest_precision,
        preferred_element_type=wide,
    )
    sums = jnp.stack(
        [
            sums_one[0],
            sums_one[1],
            sums_two[0],
            sums_two[1],
            jnp.sum(delta_embedded * normed, axis=(0, 1)),
            jnp.sum(delta_embedded, axis=(0, 1)),
        ]
    )
    sums = jnp.sum(spread(sums, "fsdp", None, fsdp), axis=0)
    sums = jnp.sum(spread(sums, "dp", None, dp), axis=0)
    gain_total, shift_total = sums[4], sums[5]
    visual_delta_rows = (
        valid_slot
        * full_batch_gain
        * inverse_spread
        * (delta_embedded - shift_total / segment_total - normed * gain_total / segment_total)
    ).astype(low)
    visual_local = jnp.einsum(
        "bli,blz->iz", pooled_segments, visual_delta_rows, preferred_element_type=wide
    ).astype(low)
    visual_shard = scatter_quick(half_of(visual_local, core), half_of(visual_local, 1 - core), core)
    delta_pooled = (
        jnp.einsum("zbl,wl->zbw", visual_delta_rows, full_visual, preferred_element_type=wide)
        / divisor
    )
    text_gradient = delta_joined + jnp.einsum(
        "drs,dsc->drc",
        onehot_wide,
        delta_pooled,
        precision=highest_precision,
        preferred_element_type=wide,
    )

    own = lax.dynamic_slice_in_dim(sums, lax.axis_index("fsdp") * piece, piece, 1)
    attend_gradient = join(
        attend_shard[0].reshape(piece, 3, half), attend_shard[1].reshape(piece, 3, half), core
    ).reshape(piece, 3 * features)
    return (
        layer_output.reshape(docs, length, features),
        text_gradient,
        join(*visual_shard, core).astype(wide),
        own[4],
        own[5],
        attend_gradient.astype(wide),
        join(*merge_shard, core).astype(wide),
        own[0],
        own[1],
        join(*up_shard, core).astype(wide),
        join(*down_shard, core).astype(wide),
        own[2],
        own[3],
    )


def solution(mesh):
    in_specs = (
        P(("dp", "fsdp"), None, None),
        P("fsdp", None),
        P("fsdp"),
        P("fsdp"),
        P("fsdp", None),
        P("fsdp", None),
        P("fsdp"),
        P("fsdp"),
        P("fsdp", None),
        P("fsdp", None),
        P("fsdp"),
        P("fsdp"),
        P(("dp", "fsdp")),
        P(("dp", "fsdp"), None),
        P(("dp", "fsdp"), None),
        P(("dp", "fsdp"), None, None),
    )
    out_specs = (
        P(("dp", "fsdp"), None, None),
        P(("dp", "fsdp"), None, None),
        P("fsdp", None),
        P("fsdp"),
        P("fsdp"),
        P("fsdp", None),
        P("fsdp", None),
        P("fsdp"),
        P("fsdp"),
        P("fsdp", None),
        P("fsdp", None),
        P("fsdp"),
        P("fsdp"),
    )
    return jax.shard_map(shards, mesh=mesh, in_specs=in_specs, out_specs=out_specs, check_vma=False)
```

time: 764 us -> 494 us (0.65); the launches traced: 753 us -> 491 us
  matrix products: 179 us -> 13.7 us
  Pallas kernels: 0 us -> 154 us
  local copies, waits for them, and re-layouts: 149 us -> 19.8 us
  blocking collectives: 72.4 us -> 0 us
  other arithmetic: 86.5 us -> 26.6 us
  starting transfers between devices: 90.9 us -> 57.7 us
  waiting for transfers between devices: 171 us -> 204 us
  between operations: 2.94 us -> 15.3 us
    dot_general x30 -> x4, matrix products: 172 us -> 6.55 us  [the longest x1 2.07 us: shards(): jnp.einsum('drs,drc->dsc', onehot, text_rows, preferred_element_type=wide)]
    pallas_call x0 -> x12, Pallas kernels: none -> 154 us  [the longest x1 23.2 us: inner_back(): call(inner_kernel, 'inner_back', (count // rows,), [block, block, tall, b...]
    all_to_all x10 -> x0, blocking collectives: 72.4 us -> none  [spread(): return lax.all_to_all(copies, axis, 0, 0, axis_index_groups=groups)]
    convert_element_type x21 -> x22, other arithmetic: 64.5 us -> 22.6 us  [the longest x13 15.9 us: add_low(): return (left.astype(wide) + right.astype(wide)).astype(low)]
    reshape x5 -> x3, local copies, waits for them, and re-layouts: 38.7 us -> 0.31 us  [the longest x1 0.18 us: shards(): attend_weight.reshape(piece, 3, features)]
    all_to_all x14 -> x8, waiting for transfers between devices: 91.4 us -> 126 us  [spread(): return lax.all_to_all(copies, axis, 0, 0, axis_index_groups=groups)]
    transpose x5 -> x0, local copies, waits for them, and re-layouts: 29.9 us -> none  [the longest x4 27.6 us: gather_weight(): full = full.transpose(2, 1, 3, 0, 4)]
    all_to_all x14 -> x8, starting transfers between devices: 56.9 us -> 31.8 us  [spread(): return lax.all_to_all(copies, axis, 0, 0, axis_index_groups=groups)]
  transfers between devices with their start and end apart: 34 -> 38, of which waited for: 20 -> 16; matrix products, arithmetic and copies ran while one was open for 24% -> 10% of each run, Pallas kernels for 0% -> 27%
where the time goes in v2:
time: 494 us; the launch traced here: 491 us
  waiting for transfers between devices  204 us (41%)
  Pallas kernels  154 us (31%)
  starting transfers between devices  57.7 us (12%)
  other arithmetic  26.6 us (5%)
  local copies, waits for them, and re-layouts  19.8 us (4%)
  between operations  15.3 us (3%)
  matrix products  13.7 us (3%)
    all_to_all x8, waiting for transfers between devices, spread(): return lax.all_to_all(copies, axis, 0, 0, axis_index_groups=groups)  126 us
    ppermute x23, waiting for transfers between devices, swap(): return lax.ppermute(value, axis, [(i, i ^ bit) for i in range(size)])  54.7 us
    all_to_all x8, starting transfers between devices, spread(): return lax.all_to_all(copies, axis, 0, 0, axis_index_groups=groups)  31.8 us
    all_to_all x3, waiting for transfers between devices, scatter_quick(): lax.all_to_all(pair, 'fsdp', 0, 0, axis_index_groups=line_groups(fsdp))  23.6 us
    pallas_call x1, Pallas kernels, inner_back(): call(inner_kernel, 'inner_back', (count // rows,), [block, block, tall, b...  23.2 us
    pallas_call x1, Pallas kernels, up(): call(up_kernel, 'up', (2, steps, count // rows), [pl.BlockSpec((rows, fea...  22.9 us
    pallas_call x3, Pallas kernels, weight_columns(): call(columns_kernel, 'weight_columns', (parts, steps), [pl.BlockSpec((cou...  21.2 us
    pallas_call x1, Pallas kernels, attend_back(): call(attend_back_kernel, 'attend_back', (docs, pairs), [column_spec(lengt...  18.8 us
  transfers between devices with their start and end apart: 38, of which 16 were waited for; matrix products, arithmetic and copies ran while one was open for 10% of the time, Pallas kernels for 27%

profile of v2, /device:TPU:0, one launch (start us, length us, event | category | flops | bytes accessed | tf_op | source)
XLA Modules:
  0.0 491.2 jit_solution(11953104253251307376)
XLA Ops:
  7.3 1.0 copy-done
  10.8 7.4 %all-to-all-start = ((bf16[8,96,384]{2,1,0:T(8,128)(2,1)}), bf16[8,96,384]{2,1,0:T(8,128)(2,1)S(1)}, u32[]{:S(2)}, u32[]{:S(2)}) async-start(bf16[8,96,384]{2,1,0:T(8,128)(2,1)} %broadcast_in_dim.24), calls=%async_computation | async-start | bytes 1179648 | tf_op jit(solution)/shard_map/all_to_all | solution.py:80
  18.2 25.1 %all-to-all-done = bf16[8,96,384]{2,1,0:T(8,128)(2,1)S(1)} async-done(((bf16[8,96,384]{2,1,0:T(8,128)(2,1)}), bf16[8,96,384]{2,1,0:T(8,128)(2,1)S(1)}, u32[]{:S(2)}, u32[]{:S(2)}) %all-to-all-start) | async-done | bytes 589856 | tf_op jit(solution)/shard_map/all_to_all | solution.py:80
  44.3 3.9 all-to-all-start.5
  49.3 30.3 %all-to-all-done.5 = bf16[8,96,384]{2,1,0:T(8,128)(2,1)S(1)} async-done(((bf16[8,96,384]{2,1,0:T(8,128)(2,1)}), bf16[8,96,384]{2,1,0:T(8,128)(2,1)S(1)}, u32[]{:S(2)}, u32[]{:S(2)}) %all-to-all-start.5) | async-done | bytes 589856 | tf_op jit(solution)/shard_map/all_to_all | solution.py:80
  79.7 1.3 broadcast_in_dim.29
  81.1 3.7 all-to-all-start.4
  87.2 2.1 fusion.1
  90.9 53.8 %all-to-all-done.4 = bf16[8,96,1152]{2,1,0:T(8,128)(2,1)S(1)} async-done(((bf16[8,96,1152]{2,1,0:T(8,128)(2,1)}), bf16[8,96,1152]{2,1,0:T(8,128)(2,1)S(1)}, u32[]{:S(2)}, u32[]{:S(2)}) %all-to-all-start.4) | async-done | bytes 1769504 | tf_op jit(solution)/shard_map/all_to_all | solution.py:80
  145.3 3.3 all-to-all-start.3
  148.8 6.5 %all-to-all-done.3 = bf16[8,6,96]{2,1,0:T(8,128)(2,1)S(1)} async-done(((bf16[8,6,96]{2,1,0:T(8,128)(2,1)}), bf16[8,6,96]{2,1,0:T(8,128)(2,1)S(1)}, u32[]{:S(2)}, u32[]{:S(2)}) %all-to-all-start.3) | async-done | bytes 9248 | tf_op jit(solution)/shard_map/all_to_all | solution.py:80
  155.9 3.4 all-to-all-start.1
  159.3 7.0 %all-to-all-done.1 = f32[8,3,768]{2,1,0:T(4,128)S(1)} async-done(((f32[8,3,768]{2,1,0:T(4,128)}), f32[8,3,768]{2,1,0:T(4,128)S(1)}, u32[]{:S(2)}, u32[]{:S(2)}) %all-to-all-start.1) | async-done | bytes 73760 | tf_op jit(solution)/shard_map/all_to_all | solution.py:80
  167.1 3.5 all-to-all-start.2
  171.9 2.5 maximum_select_fusion.1.weight_ref.merge_ref
  174.5 2.5 all-to-all-done.2
  177.2 2.0 convert_add_fusion
  179.2 1.4 bitcast_convert_fusion.1.x_ref.left_ref
  181.4 9.5 %project.1 = bf16[1024,2304]{1,0:T(8,128)(2,1)} custom-call(s32[1]{0:T(128)} %bitcast.core_ref, bf16[1024,768]{1,0:T(8,128)(2,1)} %bitcast_convert_fusion.1.x_ref.left_ref, bf16[768,1152]{1,0:T(8,128)(2,1)} %bitcast.112, bf16[768,1152]{1,0:T(8,128)(2,1)} %collective-permute-done.1.other_ref), custom_call_target="tpu_custom_call" | custom-call | flops 3623878656 | bytes 12189696 | tf_op jit(solution)/shard_map/project/pallas_call | solution.py:155
  190.9 18.2 %attend.1 = (bf16[2,512,768]{2,1,0:T(8,128)(2,1)}, bf16[2,12,512,512]{3,2,1,0:T(8,128)(2,1)}) custom-call(s32[1]{0:T(128)} %bitcast.core_ref, bf16[2,512,2304]{2,1,0:T(8,128)(2,1)} %bitcast.94, bf16[2,512,2304]{2,1,0:T(8,128)(2,1)} %bitcast.95, bf16[2,512,2304]{2,1,0:T(8,128)(2,1)} %bitcast.96, s32[2,1,512]{2,1,0:T(1,128)} %broadcast_in_dim.30.mask_ref), custom_call_target="tpu_custom_call" | custom-call | flops 6442450944 | bytes 12582912 | tf_op jit(solution)/shard_map/attend/pallas_call | solution.py:193
  209.1 6.2 %merge.1 = (f32[1024,768]{1,0:T(8,128)}, bf16[1024,768]{1,0:T(8,128)(2,1)}) custom-call(s32[1]{0:T(128)} %bitcast.core_ref, bf16[1024,768]{1,0:T(8,128)(2,1)} %bitcast.107, f32[1024,768]{1,0:T(8,128)} %bitcast.104, bf16[768,768]{1,0:T(8,128)(2,1)} %maximum_select_fusion.1.weight_ref.merge_ref, f32[8,768]{1,0:T(8,128)} %pad.4.vectors_ref), custom_call_target="tpu_custom_call" | custom-call | flops 1207959552 | bytes 11010048 | tf_op jit(solution)/shard_map/merge/pallas_call | solution.py:329
  215.3 22.9 %up.1 = (bf16[1024,3072]{1,0:T(8,128)(2,1)}, bf16[1024,3072]{1,0:T(8,128)(2,1)}) custom-call(s32[1]{0:T(128)} %bitcast.core_ref, bf16[1024,768]{1,0:T(8,128)(2,1)} %get-tuple-element.37.x_ref.left_ref, bf16[768,1536]{1,0:T(8,128)(2,1)} %all-gather.3.cloned.1.call-done.own_ref.up_own_ref, bf16[768,1536]{1,0:T(8,128)(2,1)} %collective-permute-done.3.other_ref.up_other_ref), custom_call_target="tpu_custom_call" | custom-call | flops 4831838208 | bytes 17301504 | tf_op jit(solution)/shard_map/up/pallas_call | solution.py:290
  238.2 14.2 %down.1 = (f32[1024,768]{1,0:T(8,128)}, f32[1024,768]{1,0:T(8,128)}, bf16[1024,768]{1,0:T(8,128)(2,1)}, f32[8,768]{1,0:T(8,128)}) custom-call(s32[1]{0:T(128)} %bitcast.core_ref, bf16[1024,3072]{1,0:T(8,128)(2,1)} %get-tuple-element.38.x_ref.left_ref, f32[1024,768]{1,0:T(8,128)} %get-tuple-element.39.sum_ref, bf16[1024,768]{1,0:T(8,128)(2,1)} %bitcast.138, ...), custom_call_target="tpu_custom_call" | custom-call | flops 4831838208 | bytes 22020096 | tf_op jit(solution)/shard_map/down/pallas_call | solution.py:395
  252.5 9.2 %weight_columns.5 = (bf16[3072,384]{1,0:T(8,128)(2,1)}, bf16[3072,384]{1,0:T(8,128)(2,1)}) custom-call(s32[1]{0:T(128)} %bitcast.core_ref, bf16[1024,3072]{1,0:T(8,128)(2,1)} %get-tuple-element.38.x_ref.left_ref, bf16[1,1024,768]{2,1,0:T(8,128)(2,1)} %bitcast.140, bf16[1,1024,768]{2,1,0:T(8,128)(2,1)} %bitcast.141), custom_call_target="tpu_custom_call" | custom-call | flops 4831838208 | bytes 12582912 | tf_op jit(solution)/shard_map/weight_columns/pallas_call | solution.py:523
  262.1 4.4 collective-permute-done.20
  266.5 3.7 add_convert_fusion
  270.2 23.2 %inner_back.1 = (bf16[1024,3072]{1,0:T(8,128)(2,1)}, f32[1024,768]{1,0:T(8,128)}, bf16[1024,768]{1,0:T(8,128)(2,1)}, bf16[1024,768]{1,0:T(8,128)(2,1)}, f32[8,768]{1,0:T(8,128)}) custom-call(s32[1]{0:T(128)} %bitcast.core_ref, bf16[1024,768]{1,0:T(8,128)(2,1)} %get-tuple-element.41.low_ref, f32[1024,768]{1,0:T(8,128)} %get-tuple-element.42.delta_ref, ...), custom_call_target="tpu_custom_call" | custom-call | flops 9663676416 | bytes 37748736 | tf_op jit(solution)/shard_map/inner_back/pallas_call | solution.py:476
  293.3 9.9 %weight_wide.1 = (bf16[768,1536]{1,0:T(8,128)(2,1)}, bf16[768,1536]{1,0:T(8,128)(2,1)}) custom-call(s32[1]{0:T(128)} %bitcast.core_ref, bf16[1024,768]{1,0:T(8,128)(2,1)} %get-tuple-element.37.x_ref.left_ref, bf16[1024,3072]{1,0:T(8,128)(2,1)} %get-tuple-element.54.right_ref), custom_call_target="tpu_custom_call" | custom-call | flops 4831838208 | bytes 11010048 | tf_op jit(solution)/shard_map/weight_wide/pallas_call | solution.py:555
  303.7 18.8 %attend_back.1 = bf16[3,2,512,768]{3,2,1,0:T(8,128)(2,1)} custom-call(s32[1]{0:T(128)} %bitcast.core_ref, bf16[2,512,2304]{2,1,0:T(8,128)(2,1)} %bitcast.97, bf16[2,512,2304]{2,1,0:T(8,128)(2,1)} %bitcast.98, bf16[2,512,2304]{2,1,0:T(8,128)(2,1)} %bitcast.99, bf16[2,12,512,512]{3,2,1,0:T(8,128)(2,1)} %get-tuple-element.45.share_ref, ...), custom_call_target="tpu_custom_call" | custom-call | flops 8053063680 | bytes 12582912 | tf_op jit(solution)/shard_map/attend_back/pallas_call | solution.py:239
  322.5 9.7 %joined_back.1 = f32[1024,768]{1,0:T(8,128)} custom-call(s32[1]{0:T(128)} %bitcast.core_ref, f32[1024,768]{1,0:T(8,128)} %get-tuple-element.44.one_ref, bf16[3,1024,768]{2,1,0:T(8,128)(2,1)} %bitcast.100, bf16[3,1024,768]{2,1,0:T(8,128)(2,1)} %bitcast.101, bf16[768,1152]{1,0:T(8,128)(2,1)} %bitcast.113, bf16[768,1152]{1,0:T(8,128)(2,1)} %collective-permute-done.1.other_ref), custom_call_target="tpu_custom_call" | custom-call | flops 3623878656 | bytes 11010048 | tf_op jit(solution)/shard_map/joined_back/pallas_call | solution.py:596
  332.2 3.4 multiply_reduce_fusion
  337.8 3.4 all-to-all-start.6
  341.2 7.7 %weight_columns.3 = (bf16[768,1152]{1,0:T(8,128)(2,1)}, bf16[768,1152]{1,0:T(8,128)(2,1)}) custom-call(s32[1]{0:T(128)} %bitcast.core_ref, bf16[1024,768]{1,0:T(8,128)(2,1)} %bitcast_convert_fusion.1.x_ref.left_ref, bf16[3,1024,768]{2,1,0:T(8,128)(2,1)} %bitcast.102, bf16[3,1024,768]{2,1,0:T(8,128)(2,1)} %bitcast.103), custom_call_target="tpu_custom_call" | custom-call | flops 3623878656 | bytes 9830400 | tf_op jit(solution)/shard_map/weight_columns/pallas_call | solution.py:523
  350.3 3.3 all-to-all-start.7
  353.9 4.3 weight_columns.4
  358.8 1.0 multiply_convert_fusion
  359.8 4.4 add_convert_fusion.1
  366.4 1.2 add_convert_fusion.3
  367.7 1.2 collective-permute-start.14
  369.4 1.0 dynamic-slice_bitcast_fusion
  371.4 1.2 collective-permute-start.6
  372.7 8.0 %collective-permute-done.14 = bf16[4,96,384]{2,1,0:T(8,128)(2,1)S(1)} collective-permute-done((bf16[4,96,384]{2,1,0:T(8,128)(2,1)S(1)}, bf16[4,96,384]{2,1,0:T(8,128)(2,1)S(1)}, u32[]{:S(2)}, u32[]{:S(2)}) %collective-permute-start.14) | collective-permute-done | bytes 294944 | tf_op jit(solution)/shard_map/ppermute | solution.py:85
  381.5 4.0 all-to-all-start.10
  385.4 26.1 %collective-permute-done.6 = bf16[4,96,384]{2,1,0:T(8,128)(2,1)S(1)} collective-permute-done((bf16[4,96,384]{2,1,0:T(8,128)(2,1)S(1)}, bf16[4,96,384]{2,1,0:T(8,128)(2,1)S(1)}, u32[]{:S(2)}, u32[]{:S(2)}) %collective-permute-start.6) | collective-permute-done | bytes 294944 | tf_op jit(solution)/shard_map/ppermute | solution.py:85
  412.3 4.3 all-to-all-start.8
  416.6 2.4 fusion
  419.0 6.7 %all-to-all-done.8 = bf16[4,96,384]{2,1,0:T(8,128)(2,1)S(1)} async-done(((bf16[4,96,384]{2,1,0:T(8,128)(2,1)}), bf16[4,96,384]{2,1,0:T(8,128)(2,1)S(1)}, u32[]{:S(2)}, u32[]{:S(2)}) %all-to-all-start.8) | async-done | bytes 294944 | tf_op jit(solution)/shard_map/all_to_all | solution.py:137
  425.7 3.6 all-to-all-start.9
  429.3 1.9 convolution_divide_fusion
  431.5 3.2 convolution_add_fusion
  434.8 1.7 collective-permute-start.15
  437.3 2.0 collective-permute-done.15
  439.9 1.7 collective-permute-start.7
  442.4 16.9 %all-to-all-done.9 = bf16[4,96,1152]{2,1,0:T(8,128)(2,1)S(1)} async-done(((bf16[4,96,1152]{2,1,0:T(8,128)(2,1)}), bf16[4,96,1152]{2,1,0:T(8,128)(2,1)S(1)}, u32[]{:S(2)}, u32[]{:S(2)}) %all-to-all-start.9) | async-done | bytes 884768 | tf_op jit(solution)/shard_map/all_to_all | solution.py:137
  459.4 1.7 collective-permute-start.11
  461.7 1.7 collective-permute-start.18
  463.4 4.5 collective-permute-done.11
  468.0 6.2 %collective-permute-done.21 = bf16[384,384]{1,0:T(8,128)(2,1)S(1)} collective-permute-done((bf16[384,384]{1,0:T(8,128)(2,1)}, bf16[384,384]{1,0:T(8,128)(2,1)S(1)}, u32[]{:S(2)}, u32[]{:S(2)}) %collective-permute-start.21) | collective-permute-done | bytes 294944 | tf_op jit(solution)/shard_map/ppermute | solution.py:85
  474.2 1.0 add_convert_fusion.6
  475.3 3.6 collective-permute-done.18
  478.9 1.0 add_convert_fusion.7
  481.3 1.1 copy.85
  482.4 1.1 fusion.9
  483.5 1.2 fusion.8
  (187 shorter events, 27.8 us)
Async XLA Ops:
  7.2 11.0 %copy-start.21 = (bf16[96,768]{1,0:T(8,128)(2,1)S(1)}, bf16[96,768]{1,0:T(8,128)(2,1)}, u32[]{:S(2)}) copy-start(bf16[96,768]{1,0:T(8,128)(2,1)} %param.21) | copy-start | bytes 442372
  7.2 164.5 %all-gather.3.cloned.1.call-start = ((), (), s32[]{:S(2)}) async-start(), calls=%async_computation.13 | async-start | bytes 2654208 | tf_op jit(solution)/shard_map/all_gather | solution.py:100
  9.9 38.3 %copy-start.16 = (bf16[384,768]{1,0:T(8,128)(2,1)S(1)}, bf16[384,768]{1,0:T(8,128)(2,1)}, u32[]{:S(2)}) copy-start(bf16[384,768]{1,0:T(8,128)(2,1)} %param.25) | copy-start | bytes 1769476
  10.8 38.2 %copy-start.13 = (bf16[96,2304]{1,0:T(8,128)(2,1)S(1)}, bf16[96,2304]{1,0:T(8,128)(2,1)}, u32[]{:S(2)}) copy-start(bf16[96,2304]{1,0:T(8,128)(2,1)} %param.20) | copy-start | bytes 1327108
  10.8 32.6 %all-to-all-start = ((bf16[8,96,384]{2,1,0:T(8,128)(2,1)}), bf16[8,96,384]{2,1,0:T(8,128)(2,1)S(1)}, u32[]{:S(2)}, u32[]{:S(2)}) async-start(bf16[8,96,384]{2,1,0:T(8,128)(2,1)} %broadcast_in_dim.24), calls=%async_computation | async-start | bytes 1179648 | tf_op jit(solution)/shard_map/all_to_all | solution.py:80
  43.4 5.6 %copy-start.9 = (bf16[8,96,384]{2,1,0:T(8,128)(2,1)}, bf16[8,96,384]{2,1,0:T(8,128)(2,1)S(1)}, u32[]{:S(2)}) copy-start(bf16[8,96,384]{2,1,0:T(8,128)(2,1)S(1)} %all-to-all-done) | copy-start | bytes 1769476
  44.3 35.4 %all-to-all-start.5 = ((bf16[8,96,384]{2,1,0:T(8,128)(2,1)}), bf16[8,96,384]{2,1,0:T(8,128)(2,1)S(1)}, u32[]{:S(2)}, u32[]{:S(2)}) async-start(bf16[8,96,384]{2,1,0:T(8,128)(2,1)} %broadcast_in_dim.31), calls=%async_computation.5 | async-start | bytes 1179648 | tf_op jit(solution)/shard_map/all_to_all | solution.py:80
  48.1 128.9 %all-gather.5.cloned.1.call-start = ((), (), s32[]{:S(2)}) async-start(), calls=%async_computation.14 | async-start | bytes 2654208 | tf_op jit(solution)/shard_map/all_gather | solution.py:100
  81.0 3.8 copy-start.34
  81.0 5.1 %copy-start.24 = (s32[2,512]{1,0:T(2,128)S(1)}, s32[2,512]{1,0:T(2,128)}, u32[]{:S(2)}) copy-start(s32[2,512]{1,0:T(2,128)} %param.30) | copy-start | bytes 12292
  81.0 5.8 %copy-start.27 = (bf16[96]{0:T(256)(128)(2,1)S(1)}, bf16[96]{0:T(256)(128)(2,1)}, u32[]{:S(2)}) copy-start(bf16[96]{0:T(256)(128)(2,1)} %param.22) | copy-start | bytes 580
  81.0 5.8 %copy-start.28 = (bf16[96]{0:T(256)(128)(2,1)S(1)}, bf16[96]{0:T(256)(128)(2,1)}, u32[]{:S(2)}) copy-start(bf16[96]{0:T(256)(128)(2,1)} %param.23) | copy-start | bytes 580
  81.0 5.8 %copy-start.29 = (bf16[96]{0:T(256)(128)(2,1)S(1)}, bf16[96]{0:T(256)(128)(2,1)}, u32[]{:S(2)}) copy-start(bf16[96]{0:T(256)(128)(2,1)} %param.26) | copy-start | bytes 580
  81.0 5.8 %copy-start.30 = (bf16[96]{0:T(256)(128)(2,1)S(1)}, bf16[96]{0:T(256)(128)(2,1)}, u32[]{:S(2)}) copy-start(bf16[96]{0:T(256)(128)(2,1)} %param.27) | copy-start | bytes 580
  81.0 5.8 %copy-start.31 = (bf16[96]{0:T(256)(128)(2,1)S(1)}, bf16[96]{0:T(256)(128)(2,1)}, u32[]{:S(2)}) copy-start(bf16[96]{0:T(256)(128)(2,1)} %param.18) | copy-start | bytes 580
  81.0 5.8 %copy-start.32 = (bf16[96]{0:T(256)(128)(2,1)S(1)}, bf16[96]{0:T(256)(128)(2,1)}, u32[]{:S(2)}) copy-start(bf16[96]{0:T(256)(128)(2,1)} %param.19) | copy-start | bytes 580
  81.1 5.9 %copy-start.10 = (bf16[8,96,384]{2,1,0:T(8,128)(2,1)S(1)}, bf16[8,96,384]{2,1,0:T(8,128)(2,1)}, u32[]{:S(2)}) copy-start(bf16[8,96,384]{2,1,0:T(8,128)(2,1)} %copy-done.9) | copy-start | bytes 1769476
  81.1 5.9 %copy-start.17 = (s32[2,512]{1,0:T(2,128)S(1)}, s32[2,512]{1,0:T(2,128)}, u32[]{:S(2)}) copy-start(s32[2,512]{1,0:T(2,128)} %param.29) | copy-start | bytes 12292
  81.1 63.6 %all-to-all-start.4 = ((bf16[8,96,1152]{2,1,0:T(8,128)(2,1)}), bf16[8,96,1152]{2,1,0:T(8,128)(2,1)S(1)}, u32[]{:S(2)}, u32[]{:S(2)}) async-start(bf16[8,96,1152]{2,1,0:T(8,128)(2,1)} %broadcast_in_dim.29), calls=%async_computation.4 | async-start | bytes 3538944 | tf_op jit(solution)/shard_map/all_to_all | solution.py:80
  86.9 3.8 copy-start.22
  86.9 2.9 collective-permute-start
  87.2 2.7 copy-start.11
  89.3 82.6 %collective-permute-start.2 = (bf16[768,384]{1,0:T(8,128)(2,1)S(1)}, bf16[768,384]{1,0:T(8,128)(2,1)}, u32[]{:S(2)}, u32[]{:S(2)}) collective-permute-start(bf16[768,384]{1,0:T(8,128)(2,1)S(1)} %bitcast.117), channel_id=1, source_target_pairs={{0,8},{8,0},{16,24},{24,16},{1,9},{9,1},{17,25},{25,17},{2,10},{10... | collective-permute-start | bytes 1769480 | tf_op jit(solution)/shard_map/ppermute | solution.py:85
  144.7 29.8 %copy-start.4 = (bf16[8,96,1152]{2,1,0:T(8,128)(2,1)}, bf16[8,96,1152]{2,1,0:T(8,128)(2,1)S(1)}, u32[]{:S(2)}) copy-start(bf16[8,96,1152]{2,1,0:T(8,128)(2,1)S(1)} %all-to-all-done.4) | copy-start | bytes 5308420
  145.3 10.0 %all-to-all-start.3 = ((bf16[8,6,96]{2,1,0:T(8,128)(2,1)}), bf16[8,6,96]{2,1,0:T(8,128)(2,1)S(1)}, u32[]{:S(2)}, u32[]{:S(2)}) async-start(bf16[8,6,96]{2,1,0:T(8,128)(2,1)} %broadcast_in_dim.27), calls=%async_computation.3 | async-start | bytes 32768 | tf_op jit(solution)/shard_map/all_to_all | solution.py:80
  148.7 32.8 %collective-permute-start.1 = (bf16[768,1152]{1,0:T(8,128)(2,1)S(1)}, bf16[768,1152]{1,0:T(8,128)(2,1)}, u32[]{:S(2)}, u32[]{:S(2)}) collective-permute-start(bf16[768,1152]{1,0:T(8,128)(2,1)S(1)} %bitcast.111), channel_id=1, source_target_pairs={{0,8},{8,0},{16,24},{24,16},{1,9},{9,1},{17,25},{25,17},{2,10},{10... | collective-permute-start | bytes 5308424 | tf_op jit(solution)/shard_map/ppermute | solution.py:85
  155.9 10.4 %all-to-all-start.1 = ((f32[8,3,768]{2,1,0:T(4,128)}), f32[8,3,768]{2,1,0:T(4,128)S(1)}, u32[]{:S(2)}, u32[]{:S(2)}) async-start(f32[8,3,768]{2,1,0:T(4,128)} %broadcast_in_dim.25), calls=%async_computation.1 | async-start | bytes 196608 | tf_op jit(solution)/shard_map/all_to_all | solution.py:80
  167.1 9.8 %all-to-all-start.2 = ((f32[4,8,3,768]{3,1,2,0:T(8,128)}), f32[4,8,3,768]{3,1,2,0:T(8,128)S(1)}, u32[]{:S(2)}, u32[]{:S(2)}) async-start(f32[4,8,3,768]{3,1,2,0:T(8,128)} %broadcast_in_dim.26), calls=%async_computation.2 | async-start | bytes 589824 | tf_op jit(solution)/shard_map/all_to_all | solution.py:80
  170.6 290.7 %reduce-scatter.5.cloned.1.call-start = ((), (), s32[]{:S(2)}) async-start(), calls=%async_computation.16 | async-start | bytes 2654208 | tf_op jit(solution)/shard_map/reduce_scatter | solution.py:126
  170.9 6.3 %copy-start.19 = (f32[768]{0:T(1024)}, f32[768]{0:T(1024)S(1)}, u32[]{:S(2)}) copy-start(f32[768]{0:T(1024)S(1)} %mul.93) | copy-start | bytes 9220
  171.7 43.6 %collective-permute-start.3 = (bf16[768,1536]{1,0:T(8,128)(2,1)}, bf16[768,1536]{1,0:T(8,128)(2,1)}, u32[]{:S(2)}, u32[]{:S(2)}) collective-permute-start(bf16[768,1536]{1,0:T(8,128)(2,1)} %all-gather.3.cloned.1.call-done.own_ref.up_own_ref), channel_id=1, source_target_pairs={{0,8},{8,0},{16,24},{24,16},{1,9},{9,1},{17,25},{25,17},{2,10},{10... | collective-permute-start | bytes 7077896 | tf_op jit(solution)/shard_map/ppermute | solution.py:85
  177.1 61.1 %collective-permute-start.4 = (bf16[3072,384]{1,0:T(8,128)(2,1)}, bf16[3072,384]{1,0:T(8,128)(2,1)}, u32[]{:S(2)}, u32[]{:S(2)}) collective-permute-start(bf16[3072,384]{1,0:T(8,128)(2,1)} %all-gather.5.cloned.1.call-done.own_ref.down_own_ref), channel_id=1, source_target_pairs={{0,8},{8,0},{16,24},{24,16},{1,9},{9,1},{17,25},{25,17},{2,10},{10... | collective-permute-start | bytes 7077896 | tf_op jit(solution)/shard_map/ppermute | solution.py:85
  261.6 4.8 collective-permute-start.20
  303.3 56.6 %collective-permute-start.17 = (bf16[768,1536]{1,0:T(8,128)(2,1)}, bf16[768,1536]{1,0:T(8,128)(2,1)}, u32[]{:S(2)}, u32[]{:S(2)}) collective-permute-start(bf16[768,1536]{1,0:T(8,128)(2,1)} %get-tuple-element.56), channel_id=1, source_target_pairs={{0,8},{8,0},{16,24},{24,16},{1,9},{9,1},{17,25},{25,17},{2,10},{10... | collective-permute-start | bytes 7077896 | tf_op jit(solution)/shard_map/ppermute | solution.py:85
  337.8 11.9 %all-to-all-start.6 = ((f32[8,6,768]{2,1,0:T(8,128)}), f32[8,6,768]{2,1,0:T(8,128)S(1)}, u32[]{:S(2)}, u32[]{:S(2)}) async-start(f32[8,6,768]{2,1,0:T(8,128)} %broadcast_in_dim.32), calls=%async_computation.6 | async-start | bytes 393216 | tf_op jit(solution)/shard_map/all_to_all | solution.py:80
  350.3 8.4 %all-to-all-start.7 = ((f32[4,6,768]{2,1,0:T(8,128)}), f32[4,6,768]{2,1,0:T(8,128)S(1)}, u32[]{:S(2)}, u32[]{:S(2)}) async-start(f32[4,6,768]{2,1,0:T(8,128)} %broadcast_in_dim.33), calls=%async_computation.7 | async-start | bytes 196608 | tf_op jit(solution)/shard_map/all_to_all | solution.py:80
  353.6 108.1 %reduce-scatter.3.cloned.1.call-start = ((), (), s32[]{:S(2)}) async-start(), calls=%async_computation.15 | async-start | bytes 2654208 | tf_op jit(solution)/shard_map/reduce_scatter | solution.py:126
  353.9 4.9 copy-start.20
  353.9 4.9 copy-start.23
  358.2 7.9 %collective-permute-start.13 = (bf16[768,384]{1,0:T(8,128)(2,1)}, bf16[768,384]{1,0:T(8,128)(2,1)}, u32[]{:S(2)}, u32[]{:S(2)}) collective-permute-start(bf16[768,384]{1,0:T(8,128)(2,1)} %get-tuple-element.53), channel_id=1, source_target_pairs={{0,8},{8,0},{16,24},{24,16},{1,9},{9,1},{17,25},{25,17},{2,10},{10... | collective-permute-start | bytes 1769480 | tf_op jit(solution)/shard_map/ppermute | solution.py:85
  358.4 10.5 %collective-permute-start.9 = (bf16[768,1152]{1,0:T(8,128)(2,1)}, bf16[768,1152]{1,0:T(8,128)(2,1)S(1)}, u32[]{:S(2)}, u32[]{:S(2)}) collective-permute-start(bf16[768,1152]{1,0:T(8,128)(2,1)} %get-tuple-element.50), channel_id=1, source_target_pairs={{0,8},{8,0},{16,24},{24,16},{1,9},{9,1},{17,25},{25,17},{2,10},{10... | collective-permute-start | bytes 5308424 | tf_op jit(solution)/shard_map/ppermute | solution.py:85
  358.8 5.4 %copy-start.18 = (f32[6,768]{1,0:T(8,128)}, f32[6,768]{1,0:T(8,128)S(1)}, u32[]{:S(2)}) copy-start(f32[6,768]{1,0:T(8,128)S(1)} %reduce_sum.145) | copy-start | bytes 55300
  365.8 3.1 copy-start.5
  365.9 5.3 %collective-permute-start.5 = (bf16[768,384]{1,0:T(8,128)(2,1)S(1)}, bf16[768,384]{1,0:T(8,128)(2,1)S(1)}, u32[]{:S(2)}, u32[]{:S(2)}) collective-permute-start(bf16[768,384]{1,0:T(8,128)(2,1)S(1)} %constant_dynamic-slice_fusion.1), channel_id=1, source_target_pairs={{0,8},{8,0},{16,24},{24,16},{1,9},{9,1},{17,25},{25,17},{2,10},{10... | collective-permute-start | bytes 1769480 | tf_op jit(solution)/shard_map/ppermute | solution.py:85
  367.7 13.0 %collective-permute-start.14 = (bf16[4,96,384]{2,1,0:T(8,128)(2,1)S(1)}, bf16[4,96,384]{2,1,0:T(8,128)(2,1)S(1)}, u32[]{:S(2)}, u32[]{:S(2)}) collective-permute-start(bf16[4,96,384]{2,1,0:T(8,128)(2,1)S(1)} %dynamic-slice_bitcast_fusion.1), channel_id=1, source_target_pairs={{0,1},{1,0},{2,3},{3,2},{4,5},{5,4},{6,7},{7,6},{8,9},{9,8},{10,11... | collective-permute-start | bytes 884744 | tf_op jit(solution)/shard_map/ppermute | solution.py:85
  370.4 46.3 %collective-permute-start.10 = (bf16[4,96,1152]{2,1,0:T(8,128)(2,1)}, bf16[4,96,1152]{2,1,0:T(8,128)(2,1)}, u32[]{:S(2)}, u32[]{:S(2)}) collective-permute-start(bf16[4,96,1152]{2,1,0:T(8,128)(2,1)} %dynamic-slice_bitcast_fusion), channel_id=1, source_target_pairs={{0,1},{1,0},{2,3},{3,2},{4,5},{5,4},{6,7},{7,6},{8,9},{9,8},{10,11... | collective-permute-start | bytes 2654216 | tf_op jit(solution)/shard_map/ppermute | solution.py:85
  371.4 40.1 %collective-permute-start.6 = (bf16[4,96,384]{2,1,0:T(8,128)(2,1)S(1)}, bf16[4,96,384]{2,1,0:T(8,128)(2,1)S(1)}, u32[]{:S(2)}, u32[]{:S(2)}) collective-permute-start(bf16[4,96,384]{2,1,0:T(8,128)(2,1)S(1)} %dynamic-slice_bitcast_fusion.2), channel_id=1, source_target_pairs={{0,1},{1,0},{2,3},{3,2},{4,5},{5,4},{6,7},{7,6},{8,9},{9,8},{10,11... | collective-permute-start | bytes 884744 | tf_op jit(solution)/shard_map/ppermute | solution.py:85
  381.5 30.9 %all-to-all-start.10 = ((bf16[4,96,384]{2,1,0:T(8,128)(2,1)}), bf16[4,96,384]{2,1,0:T(8,128)(2,1)S(1)}, u32[]{:S(2)}, u32[]{:S(2)}) async-start(bf16[4,96,384]{2,1,0:T(8,128)(2,1)} %fusion.10), calls=%async_computation.10 | async-start | bytes 589824 | tf_op jit(solution)/shard_map/all_to_all | solution.py:137
  412.3 13.3 %all-to-all-start.8 = ((bf16[4,96,384]{2,1,0:T(8,128)(2,1)}), bf16[4,96,384]{2,1,0:T(8,128)(2,1)S(1)}, u32[]{:S(2)}, u32[]{:S(2)}) async-start(bf16[4,96,384]{2,1,0:T(8,128)(2,1)} %fusion.11), calls=%async_computation.8 | async-start | bytes 589824 | tf_op jit(solution)/shard_map/all_to_all | solution.py:137
  416.6 12.6 %copy-start.7 = (bf16[2,128,768]{2,1,0:T(8,128)(2,1)S(1)}, bf16[2,128,768]{2,1,0:T(8,128)(2,1)}, u32[]{:S(2)}) copy-start(bf16[2,128,768]{2,1,0:T(8,128)(2,1)} %multiply_convert_fusion) | copy-start | bytes 1179652
  416.6 12.6 %copy-start.12 = (bf16[8,96,384]{2,1,0:T(8,128)(2,1)S(1)}, bf16[8,96,384]{2,1,0:T(8,128)(2,1)}, u32[]{:S(2)}) copy-start(bf16[8,96,384]{2,1,0:T(8,128)(2,1)} %copy-done.9) | copy-start | bytes 1769476
  416.6 12.6 %copy-start.26 = (f32[2,128]{1,0:T(2,128)S(1)}, f32[2,128]{1,0:T(2,128)}, u32[]{:S(2)}) copy-start(f32[2,128]{1,0:T(2,128)} %copy-done.25) | copy-start | bytes 3076
  425.7 33.6 %all-to-all-start.9 = ((bf16[4,96,1152]{2,1,0:T(8,128)(2,1)}), bf16[4,96,1152]{2,1,0:T(8,128)(2,1)S(1)}, u32[]{:S(2)}, u32[]{:S(2)}) async-start(bf16[4,96,1152]{2,1,0:T(8,128)(2,1)} %fusion), calls=%async_computation.9 | async-start | bytes 1769472 | tf_op jit(solution)/shard_map/all_to_all | solution.py:137
  434.8 4.4 collective-permute-start.15
  439.2 2.4 collective-permute-start.16
  439.9 21.2 %collective-permute-start.7 = (bf16[96,384]{1,0:T(8,128)(2,1)S(1)}, bf16[96,384]{1,0:T(8,128)(2,1)S(1)}, u32[]{:S(2)}, u32[]{:S(2)}) collective-permute-start(bf16[96,384]{1,0:T(8,128)(2,1)S(1)} %reduce_sum.146), channel_id=1, source_target_pairs={{0,16},{8,24},{16,0},{24,8},{1,17},{9,25},{17,1},{25,9},{2,18},{10... | collective-permute-start | bytes 221192 | tf_op jit(solution)/shard_map/ppermute | solution.py:85
  459.4 8.4 %collective-permute-start.11 = (bf16[96,1152]{1,0:T(8,128)(2,1)S(1)}, bf16[96,1152]{1,0:T(8,128)(2,1)S(1)}, u32[]{:S(2)}, u32[]{:S(2)}) collective-permute-start(bf16[96,1152]{1,0:T(8,128)(2,1)S(1)} %reduce_sum.147), channel_id=1, source_target_pairs={{0,16},{8,24},{16,0},{24,8},{1,17},{9,25},{17,1},{25,9},{2,18},{10... | collective-permute-start | bytes 663560 | tf_op jit(solution)/shard_map/ppermute | solution.py:85
  461.2 18.8 %collective-permute-start.8 = (bf16[96,384]{1,0:T(8,128)(2,1)S(1)}, bf16[96,384]{1,0:T(8,128)(2,1)S(1)}, u32[]{:S(2)}, u32[]{:S(2)}) collective-permute-start(bf16[96,384]{1,0:T(8,128)(2,1)S(1)} %add_convert_fusion.11), channel_id=1, source_target_pairs={{0,8},{8,0},{16,24},{24,16},{1,9},{9,1},{17,25},{25,17},{2,10},{10... | collective-permute-start | bytes 221192 | tf_op jit(solution)/shard_map/ppermute | solution.py:85
  461.3 12.9 %collective-permute-start.21 = (bf16[384,384]{1,0:T(8,128)(2,1)}, bf16[384,384]{1,0:T(8,128)(2,1)S(1)}, u32[]{:S(2)}, u32[]{:S(2)}) collective-permute-start(bf16[384,384]{1,0:T(8,128)(2,1)} %reduce-scatter.5.cloned.1.call-done), channel_id=1, source_target_pairs={{0,16},{8,24},{16,0},{24,8},{1,17},{9,25},{17,1},{25,9},{2,18},{10... | collective-permute-start | bytes 884744 | tf_op jit(solution)/shard_map/ppermute | solution.py:85
  461.7 17.2 %collective-permute-start.18 = (bf16[96,1536]{1,0:T(8,128)(2,1)}, bf16[96,1536]{1,0:T(8,128)(2,1)S(1)}, u32[]{:S(2)}, u32[]{:S(2)}) collective-permute-start(bf16[96,1536]{1,0:T(8,128)(2,1)} %reduce-scatter.3.cloned.1.call-done), channel_id=1, source_target_pairs={{0,16},{8,24},{16,0},{24,8},{1,17},{9,25},{17,1},{25,9},{2,18},{10... | collective-permute-start | bytes 884744 | tf_op jit(solution)/shard_map/ppermute | solution.py:85
  467.9 12.9 %collective-permute-start.12 = (bf16[96,1152]{1,0:T(8,128)(2,1)S(1)}, bf16[96,1152]{1,0:T(8,128)(2,1)S(1)}, u32[]{:S(2)}, u32[]{:S(2)}) collective-permute-start(bf16[96,1152]{1,0:T(8,128)(2,1)S(1)} %add_convert_fusion.8), channel_id=1, source_target_pairs={{0,8},{8,0},{16,24},{24,16},{1,9},{9,1},{17,25},{25,17},{2,10},{10... | collective-permute-start | bytes 663560 | tf_op jit(solution)/shard_map/ppermute | solution.py:85
  475.2 7.2 %collective-permute-start.22 = (bf16[384,384]{1,0:T(8,128)(2,1)S(1)}, bf16[384,384]{1,0:T(8,128)(2,1)S(1)}, u32[]{:S(2)}, u32[]{:S(2)}) collective-permute-start(bf16[384,384]{1,0:T(8,128)(2,1)S(1)} %add_convert_fusion.6), channel_id=1, source_target_pairs={{0,8},{8,0},{16,24},{24,16},{1,9},{9,1},{17,25},{25,17},{2,10},{10... | collective-permute-start | bytes 884744 | tf_op jit(solution)/shard_map/ppermute | solution.py:85
  479.9 3.6 collective-permute-start.19
  481.3 3.4 copy-start.1
  (9 other events, 12.7 us)
Sparse Core Ops, SparseCore 0:
  10.8 72.0 all-gather.2
  85.7 68.9 all-gather.4
  270.3 65.8 reduce-scatter.4
  364.4 87.4 reduce-scatter.2

commit v3 on v2

--- a/solution.py
+++ b/solution.py
@@ -45,7 +45,7 @@
     return jax.ShapeDtypeStruct(dims, dtype)
 
 
-def call(kernel, name, grid, in_specs, out_specs, out_shape, scratch=(), aliases=None, cost=None):
+def call(kernel, name, grid, in_specs, out_specs, out_shape, scratch=(), aliases=None):
     return pl.pallas_call(
         kernel,
         name=name,
@@ -58,13 +58,8 @@
         ),
         out_shape=out_shape,
         input_output_aliases=aliases or {},
-        cost_estimate=cost,
         compiler_params=pltpu.CompilerParams(vmem_limit_bytes=56 * 2**20),
     )
-
-
-def cost(flops, moved):
-    return pl.CostEstimate(flops=int(flops), bytes_accessed=int(moved), transcendentals=0)
 
 
 def pair_groups(size):
@@ -90,15 +85,32 @@
     return lax.dynamic_slice_in_dim(value, index * half, half, value.ndim - 1)
 
 
-def gather_quick(mine):
-    fsdp = lax.axis_size("fsdp")
-    own = spread(mine, "fsdp", None, fsdp).reshape((fsdp * mine.shape[0],) + mine.shape[1:])
-    return own, swap(own, "dp", 1)
+def after(value, *others):
+    return lax.optimization_barrier((value, *others))[0]
+
+
+def gather_line(mine):
+    line = lax.axis_index("fsdp") // 2
+    around = [mine] + [
+        lax.ppermute(mine, "fsdp", [(i, (i + 2 * step) % 8) for i in range(8)]) for step in (1, 2, 3)
+    ]
+    column = jnp.zeros((4,) + mine.shape, mine.dtype)
+    for step in range(4):
+        column = lax.dynamic_update_index_in_dim(column, around[step], (line - step) % 4, 0)
+    return column
+
+
+def gather_side(column):
+    side = lax.axis_index("fsdp") % 2
+    beside = swap(column, "fsdp", 1)
+    own = jnp.where(
+        side == 0, jnp.stack([column, beside], axis=1), jnp.stack([beside, column], axis=1)
+    )
+    return own.reshape(-1, column.shape[-1])
 
 
 def gather_bulk(mine):
-    own = lax.all_gather(mine, "fsdp", axis=0, tiled=True)
-    return own, swap(own, "dp", 1)
+    return lax.all_gather(mine, "fsdp", axis=0, tiled=True)
 
 
 def join(own, other, core):
@@ -121,49 +133,65 @@
     return total, swap(total, "dp", 1)
 
 
-def scatter_bulk(keep, give, core):
-    chip = add_low(keep, swap(give, "dp", 1))
-    return finish(lax.psum_scatter(chip, "fsdp", scatter_dimension=0, tiled=True), core)
-
-
-def scatter_quick(keep, give, core):
+def scatter_small(keep, give, core):
     rows, half = keep.shape
     fsdp = lax.axis_size("fsdp")
+    chip = add_low(keep, swap(give, "dp", 1)).reshape(fsdp, rows // fsdp, half)
+    parts = lax.all_to_all(chip, "fsdp", 0, 0)
+    return finish(jnp.sum(parts.astype(wide), axis=0).astype(low), core)
+
+
+def scatter_begin(chip):
+    rows, half = chip.shape
+    fsdp = lax.axis_size("fsdp")
     side = lax.axis_index("fsdp") % 2
-    chip = add_low(keep, swap(give, "dp", 1)).reshape(fsdp // 2, 2, rows // fsdp, half)
+    chip = chip.reshape(fsdp // 2, 2, rows // fsdp, half)
     keep = lax.dynamic_index_in_dim(chip, side, 1, False)
-    give = lax.dynamic_index_in_dim(chip, 1 - side, 1, False)
-    pair = add_low(keep, swap(give, "fsdp", 1))
-    parts = lax.all_to_all(pair, "fsdp", 0, 0, axis_index_groups=line_groups(fsdp))
-    return finish(jnp.sum(parts.astype(wide), axis=0).astype(low), core)
+    return keep, lax.dynamic_index_in_dim(chip, 1 - side, 1, False)
+
+
+def scatter_end(keep, given, core):
+    lines = keep.shape[0]
+    line = lax.axis_index("fsdp") // 2
+    pair = add_low(keep, given)
+    total = lax.dynamic_index_in_dim(pair, line, 0, False).astype(wide)
+    for step in range(1, lines):
+        away = lax.dynamic_index_in_dim(pair, (line + step) % lines, 0, False)
+        away = lax.ppermute(
+            away, "fsdp", [(i, (i + 2 * step) % (2 * lines)) for i in range(2 * lines)]
+        )
+        total = total + away.astype(wide)
+    return finish(total.astype(low), core)
+
+
+def sum_all(value):
+    for axis in ("dp", "fsdp"):
+        bit = 1
+        while bit < lax.axis_size(axis):
+            value = value + swap(value, axis, bit)
+            bit *= 2
+    return value
 
 
 def project_kernel(core_ref, x_ref, own_ref, other_ref, out_ref):
-    @pl.when(pl.program_id(0) == 0)
-    def _():
-        out_ref[...] = dot(x_ref[...], own_ref[...]).astype(low)
-
-    @pl.when(pl.program_id(0) == 1)
-    def _():
-        out_ref[...] = dot(x_ref[...], other_ref[...]).astype(low)
-
-
-def project(x, own, other, core):
-    rows, features = x.shape
+    half = own_ref.shape[1]
+    both = jnp.concatenate([own_ref[...], other_ref[...]], axis=1)
+    total = dot(x_ref[...], both).astype(low)
+    out_ref[:, pl.ds(pl.multiple_of(core_ref[0] * half, 128), half)] = total[:, :half]
+    out_ref[:, pl.ds(pl.multiple_of((1 - core_ref[0]) * half, 128), half)] = total[:, half:]
+
+
+def project(x, own, other, core, rows=512):
+    count, features = x.shape
     half = features // 2
-    parts = own.shape[1] // half
+    weight = pl.BlockSpec((features, half), lambda j, i, c: (0, j))
     return call(
         project_kernel,
         "project",
-        (2, parts),
-        [
-            pl.BlockSpec((rows, features), lambda s, j, c: (0, 0)),
-            pl.BlockSpec((features, half), lambda s, j, c: (0, jnp.where(s == 0, j, parts - 1))),
-            pl.BlockSpec((features, half), lambda s, j, c: (0, jnp.where(s == 1, j, 0))),
-        ],
-        pl.BlockSpec((rows, half), lambda s, j, c: (0, 2 * j + jnp.where(s == 0, c[0], 1 - c[0]))),
-        shape((rows, 2 * own.shape[1])),
-        cost=cost(4 * rows * features * own.shape[1], 2 * (rows * features + 2 * own.size * 3)),
+        (3, count // rows),
+        [pl.BlockSpec((rows, features), lambda j, i, c: (i, 0)), weight, weight],
+        pl.BlockSpec((rows, features), lambda j, i, c: (i, j)),
+        shape((count, 3 * features)),
     )(core, x, own, other)
 
 
@@ -208,7 +236,6 @@
             shape((docs, length, columns // 3)),
             shape((docs, 2 * pairs, length, length)),
         ],
-        cost=cost(docs * pairs * 8 * length * length * 256, docs * pairs * 4 * length * length),
     )(core, packed, packed, packed, mask[:, None, :])
 
 
@@ -250,7 +277,6 @@
         ],
         pl.BlockSpec((3, None, length, 128), lambda d, h, c: (0, d, 0, h)),
         shape((3, docs, length, columns // 3)),
-        cost=cost(docs * pairs * 20 * length * length * 128, docs * pairs * 4 * length * length),
     )(core, packed, packed, packed, share, delta, mixed)
 
 
@@ -298,7 +324,6 @@
         ],
         [out, out],
         [shape((count, 2 * half))] * 2,
-        cost=cost(4 * count * features * half, 4 * (features * half + 2 * count * half)),
     )(core, x, own, other)
 
 
@@ -316,40 +341,53 @@
     )
 
 
-def merge_kernel(core_ref, x_ref, joined_ref, weight_ref, vectors_ref, sum_ref, low_ref):
-    total = joined_ref[...] + dot(x_ref[...], weight_ref[...])
-    sum_ref[...] = total
-    unit, _ = normalize(total)
-    low_ref[...] = (unit * vectors_ref[0:1, :] + vectors_ref[1:2, :]).astype(low)
-
-
-def merge(x, joined, weight, vectors, core, rows=256):
-    count, features = x.shape
-    block = pl.BlockSpec((rows, features), lambda i, c: (i, 0))
-    return call(
-        merge_kernel,
-        "merge",
-        (count // rows,),
-        [
-            block,
-            block,
-            pl.BlockSpec(weight.shape, lambda i, c: (0, 0)),
-            pl.BlockSpec(vectors.shape, lambda i, c: (0, 0)),
-        ],
-        [block, block],
-        [shape((count, features), wide), shape((count, features))],
-        cost=cost(2 * count * features * features, 14 * count * features),
-    )(core, x, joined, weight, vectors)
-
-
-def fetch(own, other, target, sems, core):
-    half = own.shape[1]
+def fetch(own, other, target, sems, core, start=0):
+    half = target.shape[1] // 2
+    own, other = own.at[:, pl.ds(start, half)], other.at[:, pl.ds(start, half)]
     mine = pl.multiple_of(core * half, 128)
     theirs = pl.multiple_of((1 - core) * half, 128)
     return (
         pltpu.make_async_copy(own, target.at[:, pl.ds(mine, half)], sems.at[0]),
         pltpu.make_async_copy(other, target.at[:, pl.ds(theirs, half)], sems.at[1]),
     )
+
+
+def merge_kernel(
+    core_ref, x_ref, joined_ref, vectors_ref, own_ref, other_ref, sum_ref, low_ref, weight, sems
+):
+    @pl.when(pl.program_id(0) == 0)
+    def _():
+        half = weight.shape[1] // 2
+        copies = fetch(own_ref, other_ref, weight, sems, core_ref[0], 3 * half)
+        for copy in copies:
+            copy.start()
+        for copy in copies:
+            copy.wait()
+
+    total = joined_ref[...] + dot(x_ref[...], weight[...])
+    sum_ref[...] = total
+    unit, _ = normalize(total)
+    low_ref[...] = (unit * vectors_ref[0:1, :] + vectors_ref[1:2, :]).astype(low)
+
+
+def merge(x, joined, vectors, own, other, core, rows=256):
+    count, features = x.shape
+    block = pl.BlockSpec((rows, features), lambda i, c: (i, 0))
+    return call(
+        merge_kernel,
+        "merge",
+        (count // rows,),
+        [
+            block,
+            block,
+            pl.BlockSpec(vectors.shape, lambda i, c: (0, 0)),
+            pl.BlockSpec(memory_space=pl.ANY),
+            pl.BlockSpec(memory_space=pl.ANY),
+        ],
+        [block, block],
+        [shape((count, features), wide), shape((count, features))],
+        [pltpu.VMEM((features, features), low), pltpu.SemaphoreType.DMA((2,))],
+    )(core, x, joined, vectors, own, other)
 
 
 def down_kernel(
@@ -412,7 +450,6 @@
             shape((8, features), wide),
         ],
         [pltpu.VMEM((hidden, features), low), pltpu.SemaphoreType.DMA((2,))],
-        cost=cost(2 * count * features * hidden, 12 * count * features + 4 * count * hidden),
     )(core, x, total, cotangent, vectors, own, other)
 
 
@@ -423,7 +460,8 @@
     slope_ref,
     sum_ref,
     vectors_ref,
-    merge_ref,
+    merge_own_ref,
+    merge_other_ref,
     down_own_ref,
     down_other_ref,
     up_own_ref,
@@ -435,6 +473,7 @@
     sums_ref,
     down_weight,
     up_weight,
+    merge_weight,
     sems,
 ):
     core = core_ref[0]
@@ -443,6 +482,14 @@
         return (
             *fetch(down_own_ref, down_other_ref, down_weight, sems.at[0], core),
             *fetch(up_own_ref, up_other_ref, up_weight, sems.at[1], core),
+            *fetch(
+                merge_own_ref,
+                merge_other_ref,
+                merge_weight,
+                sems.at[2],
+                core,
+                3 * merge_weight.shape[1] // 2,
+            ),
         )
 
     @pl.when(pl.program_id(0) == 0)
@@ -462,12 +509,12 @@
     one_ref[...] = one
     one_low = one.astype(low)
     one_low_ref[...] = one_low
-    mixed_ref[...] = dot(one_low, merge_ref[...], NT).astype(low)
+    mixed_ref[...] = dot(one_low, merge_weight[...], NT).astype(low)
     sums_ref[0:1, :] += jnp.sum(delta * unit, axis=0, keepdims=True)
     sums_ref[1:2, :] += jnp.sum(delta, axis=0, keepdims=True)
 
 
-def inner_back(branch, delta, slope, total, vectors, weight, downs, ups, core, rows=256):
+def inner_back(branch, delta, slope, total, vectors, merges, downs, ups, core, rows=256):
     count, hidden = slope.shape
     features = total.shape[1]
     block = pl.BlockSpec((rows, features), lambda i, c: (i, 0))
@@ -483,11 +530,7 @@
             tall,
             block,
             pl.BlockSpec(vectors.shape, lambda i, c: (0, 0)),
-            pl.BlockSpec(weight.shape, lambda i, c: (0, 0)),
-            anywhere,
-            anywhere,
-            anywhere,
-            anywhere,
+            *[anywhere] * 6,
         ],
         [tall, block, block, block, pl.BlockSpec((8, features), lambda i, c: (0, 0))],
         [
@@ -500,10 +543,10 @@
         [
             pltpu.VMEM((hidden, features), low),
             pltpu.VMEM((features, hidden), low),
-            pltpu.SemaphoreType.DMA((2, 2)),
-        ],
-        cost=cost(4 * count * features * hidden, 16 * count * features + 8 * count * hidden),
-    )(core, branch, delta, slope, total, vectors, weight, *downs, *ups)
+            pltpu.VMEM((features, features), low),
+            pltpu.SemaphoreType.DMA((3, 2)),
+        ],
+    )(core, branch, delta, slope, total, vectors, *merges, *downs, *ups)
 
 
 def columns_kernel(core_ref, left_ref, own_ref, other_ref, keep_ref, give_ref):
@@ -514,6 +557,32 @@
     give_ref[...] = total[:, half:].astype(low)
 
 
+def into_kernel(core_ref, left_ref, own_ref, other_ref, kept_ref, given_ref, keep_ref, give_ref):
+    columns_kernel(core_ref, left_ref, own_ref, other_ref, keep_ref, give_ref)
+
+
+def weight_into(left, right, keep, give, core):
+    count, height = left.shape
+    half = right.shape[1] // 2
+    last = keep.shape[1] // half - 1
+    out = pl.BlockSpec((height, half), lambda i, c: (0, last))
+    return call(
+        into_kernel,
+        "weight_into",
+        (1,),
+        [
+            pl.BlockSpec((count, height), lambda i, c: (0, 0)),
+            pl.BlockSpec((count, half), lambda i, c: (0, c[0])),
+            pl.BlockSpec((count, half), lambda i, c: (0, 1 - c[0])),
+            pl.BlockSpec(memory_space=pl.ANY),
+            pl.BlockSpec(memory_space=pl.ANY),
+        ],
+        [out, out],
+        [shape(keep.shape)] * 2,
+        aliases={4: 0, 5: 1},
+    )(core, left, right, right, keep, give)
+
+
 def weight_columns(left, right, core, rows=768):
     count, height = left.shape
     parts, _, width = right.shape
@@ -531,9 +600,6 @@
         ],
         [out, out],
         [shape((height, parts * half))] * 2,
-        cost=cost(
-            2 * parts * count * height * width, 2 * (count * height + parts * width * (count + height))
-        ),
     )(core, left, right, right)
 
 
@@ -549,7 +615,7 @@
         keep_ref[...] = total
 
 
-def weight_wide(left, right, core, columns=768):
+def weight_wide(left, right, core, spare, columns=768):
     count, height = left.shape
     steps = right.shape[1] // 2 // columns
     return call(
@@ -566,8 +632,7 @@
             pl.BlockSpec((height, columns), lambda s, j, c: (0, jnp.where(s == 1, j, 0))),
             pl.BlockSpec((height, columns), lambda s, j, c: (0, jnp.where(s == 0, j, steps - 1))),
         ],
-        [shape((height, right.shape[1] // 2))] * 2,
-        cost=cost(2 * count * height * right.shape[1], 2 * (count + height) * right.shape[1]),
+        [shape((height, right.shape[1] // 2 + spare))] * 2,
     )(core, left, right)
 
 
@@ -607,8 +672,17 @@
         block,
         shape((count, features), wide),
         [pltpu.VMEM((rows, features), wide)],
-        cost=cost(2 * parts * count * features * features, 14 * count * features),
     )(core, one, packed, packed, own, other)
+
+
+def pool_stats(left, right):
+    total, size = left[0] + right[0], left[2] + right[2]
+    center = total / size
+    apart = (left[1] + right[1]) + (
+        left[2] * jnp.square(left[0] / left[2] - center)
+        + right[2] * jnp.square(right[0] / right[2] - center)
+    )
+    return jnp.stack([total, apart, size])
 
 
 def shards(
@@ -631,6 +705,7 @@
 ):
     docs, length, features = text_rows.shape
     count = docs * length
+    hidden = up_matrix.shape[1]
     half = features // 2
     dp, fsdp = lax.axis_size("dp"), lax.axis_size("fsdp")
     core = lax.axis_index("dp") % 2
@@ -639,18 +714,37 @@
 
     small = jnp.stack(
         [first_gain, first_shift, second_gain, second_shift, batch_gain, batch_shift]
-    )
-    visual_own, visual_other = gather_quick(half_of(visual_matrix, core))
-    small = spread(small, "fsdp", None, fsdp).transpose(1, 0, 2).reshape(6, features)
+    ).reshape(-1)
+    first = jnp.concatenate(
+        [
+            half_of(visual_matrix, core),
+            jnp.pad(small, (0, 16 * half - small.size)).reshape(16, half),
+        ]
+    )
+    mine = jnp.concatenate(
+        [
+            half_of(attend_weight.reshape(piece, 3, features), core).reshape(piece, 3 * half),
+            half_of(merge_weight, core),
+        ],
+        axis=1,
+    )
+    attend_own = gather_bulk(mine)
+    attends = (attend_own, swap(attend_own, "dp", 1))
+    first_own = spread(first, "fsdp", None, fsdp)
+    first_other = swap(first_own, "dp", 1)
+    direct = fsdp == 8
+    up_half = half_of(up_matrix, core)
+    if direct:
+        chip = lax.axis_index("dp") // 2 % 2
+        up_column = gather_line(after(half_of(up_half, chip), first_own))
+    else:
+        up_own = gather_bulk(up_half)
+    down_own = gather_bulk(after(half_of(down_matrix, core), first_own))
+    full_visual = join(first_own[:, :piece], first_other[:, :piece], core).reshape(features, features)
+    small = first_own[:, piece:].reshape(fsdp, 16 * half)[:, : 6 * piece]
+    small = small.reshape(fsdp, 6, piece).transpose(1, 0, 2).reshape(6, features)
     vectors = jnp.pad(small.astype(wide), ((0, 2), (0, 0)))
     full_batch_gain, full_batch_shift = vectors[4], vectors[5]
-    mine = half_of(attend_weight.reshape(piece, 3, features), core).reshape(piece, 3 * half)
-    attend_own, attend_other = gather_quick(mine)
-    merge_own, merge_other = gather_quick(half_of(merge_weight, core))
-    ups = gather_bulk(half_of(up_matrix, core))
-    downs = gather_bulk(half_of(down_matrix, core))
-    full_visual = join(visual_own, visual_other, core)
-    full_merge = join(merge_own, merge_other, core)
 
     slot_index = jnp.arange(SEGMAX)
     matches = segment_ids[:, :, None] == slot_index[None, None, :]
@@ -669,15 +763,17 @@
     local_center = visual_rows - local_sum / local_count
     local_square = jnp.sum(valid_slot * local_center * local_center, axis=(0, 1))
     stats = jnp.stack([local_sum, local_square, jnp.full_like(local_sum, local_count)])
-    stats = spread(stats, "fsdp", None, fsdp)
-    stats = spread(stats, "dp", None, dp).reshape(-1, 3, features)
-    sums, squares, sizes = stats[:, 0], stats[:, 1], stats[:, 2]
-    segment_total = jnp.sum(sizes, axis=0)
-    batch_center = jnp.sum(sums, axis=0) / segment_total
+    for axis in ("dp", "fsdp"):
+        bit = 1
+        while bit < lax.axis_size(axis):
+            stats = pool_stats(stats, swap(stats, axis, bit))
+            bit *= 2
+    if direct:
+        up_quarter = gather_side(after(up_column, stats))
+    segment_total = stats[2]
+    batch_center = stats[0] / segment_total
     center = visual_rows - batch_center
-    variance = (
-        jnp.sum(squares + sizes * jnp.square(sums / sizes - batch_center), axis=0) / segment_total
-    )
+    variance = stats[1] / segment_total
     inverse_spread = lax.rsqrt(variance + eps_batch)
     normed = center * inverse_spread
     embedded = (normed * full_batch_gain + full_batch_shift).astype(low)
@@ -686,31 +782,48 @@
     )
     joined = joined.reshape(count, features)
     joined_low = joined.astype(low)
-
-    packed = project(joined_low, attend_own, attend_other, which).reshape(docs, length, -1)
+    if direct:
+        joined_low, up_quarter = lax.optimization_barrier((joined_low, up_quarter))
+        up_far = swap(up_quarter, "dp", 2)
+
+    packed = project(joined_low, *attends, which).reshape(docs, length, -1)
     attended, share = attend(packed, padding_mask, which)
     flat_attended = attended.reshape(count, features)
-    total_one, hidden_low = merge(flat_attended, joined, full_merge, vectors, which)
+    if direct:
+        up_own = join(up_quarter, after(up_far, attended), chip)
+    total_one, hidden_low = merge(flat_attended, joined, vectors, *attends, which)
+    ups = (up_own, swap(up_own, "dp", 1))
     activated, slope = up(hidden_low, *ups, which)
+    downs = (down_own, swap(after(down_own, activated), "dp", 1))
     layer_output, delta_two, branch_low, sums_two = down(
         activated, total_one, cotangent.reshape(count, features), vectors, *downs, which
     )
 
     down_halves = weight_columns(activated, branch_low[None], which)
-    down_shard = scatter_bulk(*down_halves, core)
+    down_chip = add_low(down_halves[0], swap(down_halves[1], "dp", 1))
+    down_chip, branch_low = lax.optimization_barrier((down_chip, branch_low))
+    down_shard = finish(
+        lax.psum_scatter(down_chip, "fsdp", scatter_dimension=0, tiled=True), core
+    )
     delta_inner, delta_one, one_low, delta_attended, sums_one = inner_back(
-        branch_low, delta_two, slope, total_one, vectors, full_merge, downs, ups, which
-    )
-    up_halves = weight_wide(hidden_low, delta_inner, which)
-    up_shard = scatter_bulk(*up_halves, core)
-    merge_halves = weight_columns(flat_attended, one_low[None], which)
-    merge_shard = scatter_quick(*merge_halves, core)
+        branch_low, delta_two, slope, total_one, vectors, attends, downs, ups, which
+    )
+    keep, give = weight_wide(hidden_low, delta_inner, which, half)
+    keep, give = weight_into(flat_attended, one_low, keep, give, which)
+    chip = add_low(keep, swap(give, "dp", 1))
+    chip, delta_attended = lax.optimization_barrier((chip, delta_attended))
+    up_merge_shard = finish(
+        lax.psum_scatter(chip, "fsdp", scatter_dimension=0, tiled=True), core
+    )
     delta_packed = attend_back(
         packed, share, delta_attended.reshape(docs, length, features), attended, which
     ).reshape(3, count, features)
-    attend_halves = weight_columns(joined_low, delta_packed, which)
-    attend_shard = scatter_quick(*attend_halves, core)
-    delta_joined = joined_back(delta_one, delta_packed, attend_own, attend_other, which)
+    keep, give = weight_columns(joined_low, delta_packed, which)
+    keep, give = scatter_begin(add_low(keep, swap(give, "dp", 1)))
+    give, delta_packed = lax.optimization_barrier((give, delta_packed))
+    given = swap(give, "fsdp", 1)
+    delta_joined = joined_back(delta_one, delta_packed, *attends, which)
+    attend_shard = scatter_end(keep, given, core)
     delta_joined = delta_joined.reshape(docs, length, features)
     delta_embedded = jnp.einsum(
         "drs,drc->dsc",
@@ -729,8 +842,7 @@
             jnp.sum(delta_embedded, axis=(0, 1)),
         ]
     )
-    sums = jnp.sum(spread(sums, "fsdp", None, fsdp), axis=0)
-    sums = jnp.sum(spread(sums, "dp", None, dp), axis=0)
+    sums = sum_all(sums)
     gain_total, shift_total = sums[4], sums[5]
     visual_delta_rows = (
         valid_slot
@@ -741,7 +853,7 @@
     visual_local = jnp.einsum(
         "bli,blz->iz", pooled_segments, visual_delta_rows, preferred_element_type=wide
     ).astype(low)
-    visual_shard = scatter_quick(half_of(visual_local, core), half_of(visual_local, 1 - core), core)
+    visual_shard = scatter_small(half_of(visual_local, core), half_of(visual_local, 1 - core), core)
     delta_pooled = (
         jnp.einsum("zbl,wl->zbw", visual_delta_rows, full_visual, preferred_element_type=wide)
         / divisor
@@ -765,10 +877,10 @@
         own[4],
         own[5],
         attend_gradient.astype(wide),
-        join(*merge_shard, core).astype(wide),
+        join(*(part[:, hidden // 2 :] for part in up_merge_shard), core).astype(wide),
         own[0],
         own[1],
-        join(*up_shard, core).astype(wide),
+        join(*(part[:, : hidden // 2] for part in up_merge_shard), core).astype(wide),
         join(*down_shard, core).astype(wide),
         own[2],
         own[3],

time: 494 us -> 396 us (0.80)
  waiting for transfers between devices: 204 us -> 114 us
  starting transfers between devices: 57.7 us -> 41.1 us
    all_to_all x8 -> x1, waiting for transfers between devices: 126 us -> 24.7 us  [spread(): return lax.all_to_all(copies, axis, 0, 0, axis_index_groups=groups)]
    all_to_all x8 -> x1, starting transfers between devices: 31.8 us -> 7.28 us  [spread(): return lax.all_to_all(copies, axis, 0, 0, axis_index_groups=groups)]
    ppermute x0 -> x6, waiting for transfers between devices: none -> 21.5 us  [the longest x3 17.9 us: scatter_end(): lax.ppermute(away, 'fsdp', [(i, (i + 2 * step) % (2 * lines)) for i in ra...]
    all_to_all x3 -> x1, waiting for transfers between devices: 23.6 us -> 7.81 us  [scatter_small(): parts = lax.all_to_all(chip, 'fsdp', 0, 0)]
    ppermute x0 -> x6, starting transfers between devices: none -> 8.83 us  [the longest x3 5 us: scatter_end(): lax.ppermute(away, 'fsdp', [(i, (i + 2 * step) % (2 * lines)) for i in ra...]
    all_to_all x3 -> x1, starting transfers between devices: 11.8 us -> 3.54 us  [scatter_small(): parts = lax.all_to_all(chip, 'fsdp', 0, 0)]
    ppermute x23 -> x29, starting transfers between devices: 13.4 us -> 20.9 us  [swap(): return lax.ppermute(value, axis, [(i, i ^ bit) for i in range(size)])]
    broadcast_in_dim x8 -> x1, local copies, waits for them, and re-layouts: 6.48 us -> 0.91 us  [spread(): copies = jnp.broadcast_to(value[None], (count,) + value.shape)]
  transfers between devices with their start and end apart: 38 -> 41, of which waited for: 16 -> 23; matrix products, arithmetic and copies ran while one was open for 10% -> 12% of each run, Pallas kernels for 27% -> 34%
where the time goes in v3:
time: 396 us; the launch traced here: 390 us
  Pallas kernels  154 us (39%)
  waiting for transfers between devices  114 us (29%)
  starting transfers between devices  41.1 us (10%)
  other arithmetic  31.1 us (8%)
  local copies, waits for them, and re-layouts  21.6 us (5%)
  between operations  15.5 us (4%)
  matrix products  12 us (3%)
    ppermute x29, waiting for transfers between devices, swap(): return lax.ppermute(value, axis, [(i, i ^ bit) for i in range(size)])  57.1 us
    all_to_all x1, waiting for transfers between devices, spread(): return lax.all_to_all(copies, axis, 0, 0, axis_index_groups=groups)  24.7 us
    pallas_call x1, Pallas kernels, up(): call(up_kernel, 'up', (2, steps, count // rows), [pl.BlockSpec((rows, fea...  22.9 us
    pallas_call x1, Pallas kernels, inner_back(): call(inner_kernel, 'inner_back', (count // rows,), [block, block, tall, b...  22.8 us
    ppermute x29, starting transfers between devices, swap(): return lax.ppermute(value, axis, [(i, i ^ bit) for i in range(size)])  20.9 us
    pallas_call x1, Pallas kernels, attend_back(): call(attend_back_kernel, 'attend_back', (docs, pairs), [column_spec(lengt...  18.9 us
    pallas_call x1, Pallas kernels, attend(): call(attend_kernel, 'attend', (docs, pairs), [column_spec(length, 0), col...  18.1 us
    ppermute x3, waiting for transfers between devices, scatter_end(): lax.ppermute(away, 'fsdp', [(i, (i + 2 * step) % (2 * lines)) for i in ra...  17.9 us
  transfers between devices with their start and end apart: 41, of which 23 were waited for; matrix products, arithmetic and copies ran while one was open for 12% of the time, Pallas kernels for 34%

profile of v3, /device:TPU:0, one launch (start us, length us, event | category | flops | bytes accessed | tf_op | source)
XLA Modules:
  0.0 390.3 jit_solution(3826982021743307855)
XLA Ops:
  7.3 1.7 reshape.410
  11.2 7.3 %all-to-all-start = ((bf16[8,112,384]{2,1,0:T(8,128)(2,1)}), bf16[8,112,384]{2,1,0:T(8,128)(2,1)S(1)}, u32[]{:S(2)}, u32[]{:S(2)}) async-start(bf16[8,112,384]{2,1,0:T(8,128)(2,1)} %broadcast_in_dim.39), calls=%async_computation | async-start | bytes 1376256 | tf_op jit(solution)/shard_map/all_to_all | solution.py:75
  21.3 24.7 %all-to-all-done = bf16[8,112,384]{2,1,0:T(8,128)(2,1)S(1)} async-done(((bf16[8,112,384]{2,1,0:T(8,128)(2,1)}), bf16[8,112,384]{2,1,0:T(8,128)(2,1)S(1)}, u32[]{:S(2)}, u32[]{:S(2)}) %all-to-all-start) | async-done | bytes 688160 | tf_op jit(solution)/shard_map/all_to_all | solution.py:75
  47.7 1.4 collective-permute-start.7
  49.1 2.1 collective-permute-start.8
  55.3 1.6 collective-permute-start.2
  59.7 1.5 collective-permute-start.3
  61.3 2.4 collective-permute-done.3
  65.0 3.6 collective-permute-done.7
  69.7 2.9 collective-permute-start.5
  72.6 1.5 collective-permute-start.9
  74.1 6.1 %collective-permute-done.5 = f32[3,768]{1,0:T(4,128)S(1)} collective-permute-done((f32[3,768]{1,0:T(4,128)S(1)}, f32[3,768]{1,0:T(4,128)S(1)}, u32[]{:S(2)}, u32[]{:S(2)}) %collective-permute-start.5) | collective-permute-done | bytes 9248 | tf_op jit(solution)/shard_map/ppermute | solution.py:80
  80.8 3.3 all-gather.3.cloned.1.call-done.own_ref.merge_own_ref
  86.3 2.3 convert_add_fusion
  88.6 1.5 bitcast_convert_fusion.1.x_ref.left_ref
  90.8 1.1 maximum_select_fusion.2
  91.9 1.5 collective-permute-start.11
  94.0 1.4 copy-done.2
  95.5 9.5 %project.1 = bf16[1024,2304]{1,0:T(8,128)(2,1)} custom-call(s32[1]{0:T(128)} %bitcast.core_ref, bf16[1024,768]{1,0:T(8,128)(2,1)} %bitcast_convert_fusion.1.x_ref.left_ref, bf16[768,1536]{1,0:T(8,128)(2,1)} %all-gather.3.cloned.1.call-done.own_ref.merge_own_ref, bf16[768,1536]{1,0:T(8,128)(2,1)} %copy-done.2), custom_call_target="tpu_custom_call" | custom-call | tf_op jit(solution)/shard_map/project/pallas_call | solution.py:188
  105.0 18.1 %attend.1 = (bf16[2,512,768]{2,1,0:T(8,128)(2,1)}, bf16[2,12,512,512]{3,2,1,0:T(8,128)(2,1)}) custom-call(s32[1]{0:T(128)} %bitcast.core_ref, bf16[2,512,2304]{2,1,0:T(8,128)(2,1)} %bitcast.83, bf16[2,512,2304]{2,1,0:T(8,128)(2,1)} %bitcast.84, bf16[2,512,2304]{2,1,0:T(8,128)(2,1)} %bitcast.85, s32[2,1,512]{2,1,0:T(1,128)} %broadcast_in_dim.45.mask_ref), custom_call_target="tpu_custom_call" | custom-call | tf_op jit(solution)/shard_map/attend/pallas_call | solution.py:221
  123.1 2.9 maximum_select_fusion.own_ref.up_own_ref
  127.3 7.1 %merge.1 = (f32[1024,768]{1,0:T(8,128)}, bf16[1024,768]{1,0:T(8,128)(2,1)}) custom-call(s32[1]{0:T(128)} %bitcast.core_ref, bf16[1024,768]{1,0:T(8,128)(2,1)} %bitcast.96, f32[1024,768]{1,0:T(8,128)} %bitcast.93, f32[8,768]{1,0:T(8,128)} %pad.9.vectors_ref, bf16[768,1536]{1,0:T(8,128)(2,1)} %all-gather.3.cloned.1.call-done.own_ref.merge_own_ref, ...), custom_call_target="tpu_custom_call" | custom-call | tf_op jit(solution)/shard_map/merge/pallas_call | solution.py:376
  134.4 22.9 %up.1 = (bf16[1024,3072]{1,0:T(8,128)(2,1)}, bf16[1024,3072]{1,0:T(8,128)(2,1)}) custom-call(s32[1]{0:T(128)} %bitcast.core_ref, bf16[1024,768]{1,0:T(8,128)(2,1)} %get-tuple-element.51.x_ref.left_ref, bf16[768,1536]{1,0:T(8,128)(2,1)} %copy-done.5, bf16[768,1536]{1,0:T(8,128)(2,1)} %collective-permute-done.12.other_ref.up_other_ref), custom_call_target="tpu_custom_call" | custom-call | tf_op jit(solution)/shard_map/up/pallas_call | solution.py:316
  157.6 4.4 %collective-permute-done.13.other_ref.down_other_ref = bf16[3072,384]{1,0:T(8,128)(2,1)S(1)} collective-permute-done((bf16[3072,384]{1,0:T(8,128)(2,1)}, bf16[3072,384]{1,0:T(8,128)(2,1)S(1)}, u32[]{:S(2)}, u32[]{:S(2)}) %collective-permute-start.13) | collective-permute-done | bytes 2359328 | tf_op jit(solution)/shard_map/ppermute | solution.py:80
  162.1 1.4 copy-done.8
  163.5 14.2 %down.1 = (f32[1024,768]{1,0:T(8,128)}, f32[1024,768]{1,0:T(8,128)}, bf16[1024,768]{1,0:T(8,128)(2,1)}, f32[8,768]{1,0:T(8,128)}) custom-call(s32[1]{0:T(128)} %bitcast.core_ref, bf16[1024,3072]{1,0:T(8,128)(2,1)} %get-tuple-element.54.x_ref.left_ref, f32[1024,768]{1,0:T(8,128)} %get-tuple-element.55.sum_ref, bf16[1024,768]{1,0:T(8,128)(2,1)} %bitcast.105, ...), custom_call_target="tpu_custom_call" | custom-call | tf_op jit(solution)/shard_map/down/pallas_call | solution.py:433
  177.7 9.2 %weight_columns.2 = (bf16[3072,384]{1,0:T(8,128)(2,1)}, bf16[3072,384]{1,0:T(8,128)(2,1)}) custom-call(s32[1]{0:T(128)} %bitcast.core_ref, bf16[1024,3072]{1,0:T(8,128)(2,1)} %get-tuple-element.54.x_ref.left_ref, bf16[1,1024,768]{2,1,0:T(8,128)(2,1)} %bitcast.98, bf16[1,1024,768]{2,1,0:T(8,128)(2,1)} %bitcast.99), custom_call_target="tpu_custom_call" | custom-call | tf_op jit(solution)/shard_map/weight_columns/pallas_call | solution.py:592
  187.2 4.4 %collective-permute-done.14 = bf16[3072,384]{1,0:T(8,128)(2,1)S(1)} collective-permute-done((bf16[3072,384]{1,0:T(8,128)(2,1)}, bf16[3072,384]{1,0:T(8,128)(2,1)S(1)}, u32[]{:S(2)}, u32[]{:S(2)}) %collective-permute-start.14) | collective-permute-done | bytes 2359328 | tf_op jit(solution)/shard_map/ppermute | solution.py:80
  191.6 3.6 add_convert_fusion.1
  195.6 22.8 %inner_back.1 = (bf16[1024,3072]{1,0:T(8,128)(2,1)}, f32[1024,768]{1,0:T(8,128)}, bf16[1024,768]{1,0:T(8,128)(2,1)}, bf16[1024,768]{1,0:T(8,128)(2,1)}, f32[8,768]{1,0:T(8,128)}) custom-call(s32[1]{0:T(128)} %bitcast.core_ref, bf16[1024,768]{1,0:T(8,128)(2,1)} %get-tuple-element.62.low_ref, f32[1024,768]{1,0:T(8,128)} %get-tuple-element.63.delta_ref, ...), custom_call_target="tpu_custom_call" | custom-call | tf_op jit(solution)/shard_map/inner_back/pallas_call | solution.py:523
  218.3 10.0 %weight_wide.1 = (bf16[768,1920]{1,0:T(8,128)(2,1)}, bf16[768,1920]{1,0:T(8,128)(2,1)}) custom-call(s32[1]{0:T(128)} %bitcast.core_ref, bf16[1024,768]{1,0:T(8,128)(2,1)} %get-tuple-element.51.x_ref.left_ref, bf16[1024,3072]{1,0:T(8,128)(2,1)} %get-tuple-element.68.right_ref), custom_call_target="tpu_custom_call" | custom-call | tf_op jit(solution)/shard_map/weight_wide/pallas_call | solution.py:621
  228.4 4.3 %weight_into.1 = (bf16[768,1920]{1,0:T(8,128)(2,1)}, bf16[768,1920]{1,0:T(8,128)(2,1)}) custom-call(s32[1]{0:T(128)} %bitcast.core_ref, bf16[1024,768]{1,0:T(8,128)(2,1)} %bitcast.97, bf16[1024,768]{1,0:T(8,128)(2,1)} %get-tuple-element.67.own_ref.other_ref, ...), custom_call_target="tpu_custom_call", output_to_operand_aliasing={{0}: (4, {}), {1}: (5, {})} | custom-call | tf_op jit(solution)/shard_map/weight_into/pallas_call | solution.py:569
  233.1 5.2 %collective-permute-done.15 = bf16[768,1920]{1,0:T(8,128)(2,1)S(1)} collective-permute-done((bf16[768,1920]{1,0:T(8,128)(2,1)}, bf16[768,1920]{1,0:T(8,128)(2,1)S(1)}, u32[]{:S(2)}, u32[]{:S(2)}) %collective-permute-start.15) | collective-permute-done | bytes 2949152 | tf_op jit(solution)/shard_map/ppermute | solution.py:80
  238.3 4.2 %add_convert_fusion = bf16[768,1920]{1,0:T(8,128)(2,1)} fusion(bf16[768,1920]{1,0:T(8,128)(2,1)S(1)} %collective-permute-done.15, bf16[768,1920]{1,0:T(8,128)(2,1)} %get-tuple-element.71), kind=kLoop, calls=%fused_computation | loop fusion | flops 5898240 | bytes 8847360 | tf_op jit(solution)/shard_map/convert_element_type | solution.py:125
  242.5 18.9 %attend_back.1 = bf16[3,2,512,768]{3,2,1,0:T(8,128)(2,1)} custom-call(s32[1]{0:T(128)} %bitcast.core_ref, bf16[2,512,2304]{2,1,0:T(8,128)(2,1)} %bitcast.86, bf16[2,512,2304]{2,1,0:T(8,128)(2,1)} %bitcast.87, bf16[2,512,2304]{2,1,0:T(8,128)(2,1)} %bitcast.88, bf16[2,12,512,512]{3,2,1,0:T(8,128)(2,1)} %get-tuple-element.66.share_ref, ...), custom_call_target="tpu_custom_call" | custom-call | tf_op jit(solution)/shard_map/attend_back/pallas_call | solution.py:266
  261.4 7.6 %weight_columns.3 = (bf16[768,1152]{1,0:T(8,128)(2,1)}, bf16[768,1152]{1,0:T(8,128)(2,1)}) custom-call(s32[1]{0:T(128)} %bitcast.core_ref, bf16[1024,768]{1,0:T(8,128)(2,1)} %bitcast_convert_fusion.1.x_ref.left_ref, bf16[3,1024,768]{2,1,0:T(8,128)(2,1)} %bitcast.89, bf16[3,1024,768]{2,1,0:T(8,128)(2,1)} %bitcast.90), custom_call_target="tpu_custom_call" | custom-call | tf_op jit(solution)/shard_map/weight_columns/pallas_call | solution.py:592
  270.9 2.1 collective-permute-done.16
  272.9 1.2 copy-done.9
  274.1 2.5 add_convert_fusion.2
  277.6 9.7 %joined_back.1 = f32[1024,768]{1,0:T(8,128)} custom-call(s32[1]{0:T(128)} %bitcast.core_ref, f32[1024,768]{1,0:T(8,128)} %get-tuple-element.65.one_ref, bf16[3,1024,768]{2,1,0:T(8,128)(2,1)} %bitcast.91, bf16[3,1024,768]{2,1,0:T(8,128)(2,1)} %bitcast.92, bf16[768,1536]{1,0:T(8,128)(2,1)} %all-gather.3.cloned.1.call-done.own_ref.merge_own_ref, ...), custom_call_target="tpu_custom_call" | custom-call | tf_op jit(solution)/shard_map/joined_back/pallas_call | solution.py:661
  287.4 4.3 %multiply_reduce_fusion = (f32[768]{0:T(1024)S(1)}, f32[768]{0:T(1024)S(1)}, f32[2,128,768]{2,1,0:T(8,128)}) fusion(f32[2,128,768]{2,1,0:T(8,128)S(1)} %copy-done.7, f32[768]{0:T(1024)S(1)} %copy-done.23, f32[768]{0:T(1024)S(1)} %copy-done.25, f32[2,512,768]{2,1,0:T(8,128)} %bitcast.94, s32[2,512]{1,0:T(2,128)S(1)} %copy-done.21), kind=kOutput, calls=%fused_computation.20 | convolution fusion | flops 1209072128 | bytes 4734976 | tf_op jit(solution)/shard_map/drs,drc->dsc/dot_general | solution.py:828
  293.7 3.3 collective-permute-done.18
  296.9 1.5 collective-permute-start.19
  298.4 2.4 collective-permute-done.19
  301.8 2.9 collective-permute-done.20
  304.8 1.6 collective-permute-start.25
  306.8 2.6 collective-permute-done.21
  309.5 1.4 multiply_convert_fusion
  312.8 1.3 copy-done.4
  314.1 3.2 convolution_add_fusion
  317.3 11.7 %collective-permute-done.25 = bf16[4,96,1152]{2,1,0:T(8,128)(2,1)} collective-permute-done((bf16[4,96,1152]{2,1,0:T(8,128)(2,1)}, bf16[4,96,1152]{2,1,0:T(8,128)(2,1)}, u32[]{:S(2)}, u32[]{:S(2)}) %collective-permute-start.25) | collective-permute-done | bytes 884768 | tf_op jit(solution)/shard_map/ppermute | solution.py:80
  329.1 1.4 fusion
  331.6 2.0 collective-permute-start.27
  333.7 1.8 collective-permute-start.28
  336.5 3.5 all-to-all-start.1
  340.0 5.3 %collective-permute-done.26 = bf16[96,1152]{1,0:T(8,128)(2,1)S(1)} collective-permute-done((bf16[96,1152]{1,0:T(8,128)(2,1)S(1)}, bf16[96,1152]{1,0:T(8,128)(2,1)S(1)}, u32[]{:S(2)}, u32[]{:S(2)}) %collective-permute-start.26) | collective-permute-done | bytes 221216 | tf_op jit(solution)/shard_map/ppermute | solution.py:160
  345.4 12.6 %collective-permute-done.27 = bf16[96,1152]{1,0:T(8,128)(2,1)S(1)} collective-permute-done((bf16[96,1152]{1,0:T(8,128)(2,1)S(1)}, bf16[96,1152]{1,0:T(8,128)(2,1)S(1)}, u32[]{:S(2)}, u32[]{:S(2)}) %collective-permute-start.27) | collective-permute-done | bytes 221216 | tf_op jit(solution)/shard_map/ppermute | solution.py:160
  358.1 1.4 collective-permute-start.29
  361.4 3.8 collective-permute-done.29
  365.9 1.1 fusion.9
  367.1 7.8 %all-to-all-done.1 = bf16[8,96,384]{2,1,0:T(8,128)(2,1)S(1)} async-done(((bf16[8,96,384]{2,1,0:T(8,128)(2,1)}), bf16[8,96,384]{2,1,0:T(8,128)(2,1)S(1)}, u32[]{:S(2)}, u32[]{:S(2)}) %all-to-all-start.1) | async-done | bytes 589856 | tf_op jit(solution)/shard_map/all_to_all | solution.py:140
  375.0 1.5 collective-permute-start.23
  376.7 2.7 collective-permute-done.23
  381.9 1.2 fusion.8
  (220 shorter events, 37.8 us)
Async XLA Ops:
  7.2 12.5 %copy-start = (bf16[384,768]{1,0:T(8,128)(2,1)S(1)}, bf16[384,768]{1,0:T(8,128)(2,1)}, u32[]{:S(2)}) copy-start(bf16[384,768]{1,0:T(8,128)(2,1)} %param.25) | copy-start | bytes 1769476
  7.2 2.8 copy-start.34
  7.2 2.8 copy-start.35
  7.2 2.8 copy-start.36
  7.2 2.8 copy-start.37
  7.2 2.8 copy-start.38
  7.3 3.0 copy-start.28
  7.3 76.8 %all-gather.3.cloned.1.call-start = ((), (), s32[]{:S(2)}) async-start(), calls=%async_computation.4 | async-start | bytes 2654208 | tf_op jit(solution)/shard_map/all_gather | solution.py:113
  10.0 10.4 %copy-start.21 = (s32[2,512]{1,0:T(2,128)S(1)}, s32[2,512]{1,0:T(2,128)}, u32[]{:S(2)}) copy-start(s32[2,512]{1,0:T(2,128)} %param.29) | copy-start | bytes 12292
  10.0 10.6 %copy-start.10 = (bf16[2,512,768]{2,1,0:T(8,128)(2,1)S(1)}, bf16[2,512,768]{2,1,0:T(8,128)(2,1)}, u32[]{:S(2)}) copy-start(bf16[2,512,768]{2,1,0:T(8,128)(2,1)} %param.16) | copy-start | bytes 4718596
  11.2 34.8 %all-to-all-start = ((bf16[8,112,384]{2,1,0:T(8,128)(2,1)}), bf16[8,112,384]{2,1,0:T(8,128)(2,1)S(1)}, u32[]{:S(2)}, u32[]{:S(2)}) async-start(bf16[8,112,384]{2,1,0:T(8,128)(2,1)} %broadcast_in_dim.39), calls=%async_computation | async-start | bytes 1376256 | tf_op jit(solution)/shard_map/all_to_all | solution.py:75
  18.5 138.8 %all-gather.5.cloned.1.call-start = ((), (), s32[]{:S(2)}) async-start(), calls=%async_computation.5 | async-start | bytes 2654208 | tf_op jit(solution)/shard_map/all_gather | solution.py:113
  20.7 25.3 %copy-start.40 = (s32[2]{0:T(128)S(1)}, s32[2]{0:T(128)}, u32[]{:S(2)}) copy-start(s32[2]{0:T(128)} %param.28) | copy-start | bytes 28
  21.3 30.2 %copy-start.15 = (bf16[2,128,768]{2,1,0:T(8,128)(2,1)}, bf16[2,128,768]{2,1,0:T(8,128)(2,1)S(1)}, u32[]{:S(2)}) copy-start(bf16[2,128,768]{2,1,0:T(8,128)(2,1)S(1)} %fusion.1) | copy-start | bytes 1179652
  46.0 5.4 %collective-permute-start = (bf16[8,112,384]{2,1,0:T(8,128)(2,1)S(1)}, bf16[8,112,384]{2,1,0:T(8,128)(2,1)S(1)}, u32[]{:S(2)}, u32[]{:S(2)}) collective-permute-start(bf16[8,112,384]{2,1,0:T(8,128)(2,1)S(1)} %all-to-all-done), channel_id=1, source_target_pairs={{0,8},{8,0},{16,24},{24,16},{1,9},{9,1},{17,25},{25,17},{2,10},{10... | collective-permute-start | bytes 2064392 | tf_op jit(solution)/shard_map/ppermute | solution.py:80
  47.4 5.0 %copy-start.29 = (f32[2,128]{1,0:T(2,128)}, f32[2,128]{1,0:T(2,128)S(1)}, u32[]{:S(2)}) copy-start(f32[2,128]{1,0:T(2,128)S(1)} %compare_convert_fusion) | copy-start | bytes 3076
  47.4 13.9 %collective-permute-start.6 = (bf16[96,768]{1,0:T(8,128)(2,1)S(1)}, bf16[96,768]{1,0:T(8,128)(2,1)S(1)}, u32[]{:S(2)}, u32[]{:S(2)}) collective-permute-start(bf16[96,768]{1,0:T(8,128)(2,1)S(1)} %constant_dynamic-slice_fusion.5), channel_id=1, source_target_pairs={{0,2},{1,3},{2,4},{3,5},{4,6},{5,7},{6,0},{7,1},{8,10},{9,11},{10,... | collective-permute-start | bytes 442376 | tf_op jit(solution)/shard_map/ppermute | solution.py:95
  47.7 20.9 %collective-permute-start.7 = (bf16[96,768]{1,0:T(8,128)(2,1)S(1)}, bf16[96,768]{1,0:T(8,128)(2,1)S(1)}, u32[]{:S(2)}, u32[]{:S(2)}) collective-permute-start(bf16[96,768]{1,0:T(8,128)(2,1)S(1)} %constant_dynamic-slice_fusion.5), channel_id=1, source_target_pairs={{0,4},{1,5},{2,6},{3,7},{4,0},{5,1},{6,2},{7,3},{8,12},{9,13},{10,... | collective-permute-start | bytes 442376 | tf_op jit(solution)/shard_map/ppermute | solution.py:95
  49.1 23.4 %collective-permute-start.8 = (bf16[96,768]{1,0:T(8,128)(2,1)S(1)}, bf16[96,768]{1,0:T(8,128)(2,1)S(1)}, u32[]{:S(2)}, u32[]{:S(2)}) collective-permute-start(bf16[96,768]{1,0:T(8,128)(2,1)S(1)} %constant_dynamic-slice_fusion.5), channel_id=1, source_target_pairs={{0,6},{1,7},{2,0},{3,1},{4,2},{5,3},{6,4},{7,5},{8,14},{9,15},{10,... | collective-permute-start | bytes 442376 | tf_op jit(solution)/shard_map/ppermute | solution.py:95
  53.4 1.2 collective-permute-start.1
  53.6 27.2 %copy-start.19 = (f32[8,6,96]{2,1,0:T(8,128)}, f32[8,6,96]{2,1,0:T(8,128)S(1)}, u32[]{:S(2)}) copy-start(f32[8,6,96]{2,1,0:T(8,128)S(1)} %reshape.426) | copy-start | bytes 55300
  55.3 3.8 collective-permute-start.2
  58.3 248.2 %reduce-scatter.5.cloned.1.call-start = ((), (), s32[]{:S(2)}) async-start(), calls=%async_computation.7 | async-start | bytes 2654208 | tf_op jit(solution)/shard_map/reduce_scatter | solution.py:806
  59.7 4.0 %collective-permute-start.3 = (f32[3,768]{1,0:T(4,128)S(1)}, f32[3,768]{1,0:T(4,128)S(1)}, u32[]{:S(2)}, u32[]{:S(2)}) collective-permute-start(f32[3,768]{1,0:T(4,128)S(1)} %pad_maximum_fusion.5), channel_id=1, source_target_pairs={{0,1},{1,0},{2,3},{3,2},{4,5},{5,4},{6,7},{7,6},{8,9},{9,8},{10,11... | collective-permute-start | bytes 27656 | tf_op jit(solution)/shard_map/ppermute | solution.py:80
  64.4 4.6 %collective-permute-start.4 = (f32[3,768]{1,0:T(4,128)S(1)}, f32[3,768]{1,0:T(4,128)S(1)}, u32[]{:S(2)}, u32[]{:S(2)}) collective-permute-start(f32[3,768]{1,0:T(4,128)S(1)} %pad_maximum_fusion.6), channel_id=1, source_target_pairs={{0,2},{1,3},{2,0},{3,1},{4,6},{5,7},{6,4},{7,5},{8,10},{9,11},{10,... | collective-permute-start | bytes 27656 | tf_op jit(solution)/shard_map/ppermute | solution.py:80
  69.7 10.5 %collective-permute-start.5 = (f32[3,768]{1,0:T(4,128)S(1)}, f32[3,768]{1,0:T(4,128)S(1)}, u32[]{:S(2)}, u32[]{:S(2)}) collective-permute-start(f32[3,768]{1,0:T(4,128)S(1)} %pad_maximum_fusion.7), channel_id=1, source_target_pairs={{0,4},{1,5},{2,6},{3,7},{4,0},{5,1},{6,2},{7,3},{8,12},{9,13},{10,... | collective-permute-start | bytes 27656 | tf_op jit(solution)/shard_map/ppermute | solution.py:80
  72.6 18.2 %collective-permute-start.9 = (bf16[4,96,768]{2,1,0:T(8,128)(2,1)S(1)}, bf16[4,96,768]{2,1,0:T(8,128)(2,1)S(1)}, u32[]{:S(2)}, u32[]{:S(2)}) collective-permute-start(bf16[4,96,768]{2,1,0:T(8,128)(2,1)S(1)} %bitcast_dynamic-update-slice_fusion), channel_id=1, source_target_pairs={{0,1},{1,0},{2,3},{3,2},{4,5},{5,4},{6,7},{7,6},{8,9},{9,8},{10,11... | collective-permute-start | bytes 1769480 | tf_op jit(solution)/shard_map/ppermute | solution.py:80
  84.1 9.9 %collective-permute-start.10 = (bf16[768,1536]{1,0:T(8,128)(2,1)}, bf16[768,1536]{1,0:T(8,128)(2,1)S(1)}, u32[]{:S(2)}, u32[]{:S(2)}) collective-permute-start(bf16[768,1536]{1,0:T(8,128)(2,1)} %all-gather.3.cloned.1.call-done.own_ref.merge_own_ref), channel_id=1, source_target_pairs={{0,8},{8,0},{16,24},{24,16},{1,9},{9,1},{17,25},{25,17},{2,10},{10... | collective-permute-start | bytes 7077896 | tf_op jit(solution)/shard_map/ppermute | solution.py:80
  91.9 31.1 %collective-permute-start.11 = (bf16[768,768]{1,0:T(8,128)(2,1)}, bf16[768,768]{1,0:T(8,128)(2,1)}, u32[]{:S(2)}, u32[]{:S(2)}) collective-permute-start(bf16[768,768]{1,0:T(8,128)(2,1)} %bitcast.18), channel_id=1, source_target_pairs={{0,16},{8,24},{16,0},{24,8},{1,17},{9,25},{17,1},{25,9},{2,18},{10... | collective-permute-start | bytes 3538952 | tf_op jit(solution)/shard_map/ppermute | solution.py:80
  123.1 3.2 copy-start.20
  126.0 8.4 %copy-start.5 = (bf16[768,1536]{1,0:T(8,128)(2,1)}, bf16[768,1536]{1,0:T(8,128)(2,1)S(1)}, u32[]{:S(2)}) copy-start(bf16[768,1536]{1,0:T(8,128)(2,1)S(1)} %maximum_select_fusion.own_ref.up_own_ref) | copy-start | bytes 7077892
  126.0 8.4 %collective-permute-start.12 = (bf16[768,1536]{1,0:T(8,128)(2,1)S(1)}, bf16[768,1536]{1,0:T(8,128)(2,1)}, u32[]{:S(2)}, u32[]{:S(2)}) collective-permute-start(bf16[768,1536]{1,0:T(8,128)(2,1)S(1)} %maximum_select_fusion.own_ref.up_own_ref), channel_id=1, source_target_pairs={{0,8},{8,0},{16,24},{24,16},{1,9},{9,1},{17,25},{25,17},{2,10},{10... | collective-permute-start | bytes 7077896 | tf_op jit(solution)/shard_map/ppermute | solution.py:80
  157.3 4.7 %collective-permute-start.13 = (bf16[3072,384]{1,0:T(8,128)(2,1)}, bf16[3072,384]{1,0:T(8,128)(2,1)S(1)}, u32[]{:S(2)}, u32[]{:S(2)}) collective-permute-start(bf16[3072,384]{1,0:T(8,128)(2,1)} %all-gather.5.cloned.1.call-done.own_ref.down_own_ref), channel_id=1, source_target_pairs={{0,8},{8,0},{16,24},{24,16},{1,9},{9,1},{17,25},{25,17},{2,10},{10... | collective-permute-start | bytes 7077896 | tf_op jit(solution)/shard_map/ppermute | solution.py:80
  186.9 4.7 %collective-permute-start.14 = (bf16[3072,384]{1,0:T(8,128)(2,1)}, bf16[3072,384]{1,0:T(8,128)(2,1)S(1)}, u32[]{:S(2)}, u32[]{:S(2)}) collective-permute-start(bf16[3072,384]{1,0:T(8,128)(2,1)} %get-tuple-element.61), channel_id=1, source_target_pairs={{0,8},{8,0},{16,24},{24,16},{1,9},{9,1},{17,25},{25,17},{2,10},{10... | collective-permute-start | bytes 7077896 | tf_op jit(solution)/shard_map/ppermute | solution.py:80
  195.3 165.4 %reduce-scatter.3.cloned.1.call-start = ((), (), s32[]{:S(2)}) async-start(), calls=%async_computation.6 | async-start | bytes 3317760 | tf_op jit(solution)/shard_map/reduce_scatter | solution.py:816
  232.7 5.6 %collective-permute-start.15 = (bf16[768,1920]{1,0:T(8,128)(2,1)}, bf16[768,1920]{1,0:T(8,128)(2,1)S(1)}, u32[]{:S(2)}, u32[]{:S(2)}) collective-permute-start(bf16[768,1920]{1,0:T(8,128)(2,1)} %get-tuple-element.72), channel_id=1, source_target_pairs={{0,8},{8,0},{16,24},{24,16},{1,9},{9,1},{17,25},{25,17},{2,10},{10... | collective-permute-start | bytes 8847368 | tf_op jit(solution)/shard_map/ppermute | solution.py:80
  269.0 3.9 collective-permute-start.16
  277.6 9.8 %copy-start.7 = (f32[2,128,768]{2,1,0:T(8,128)S(1)}, f32[2,128,768]{2,1,0:T(8,128)}, u32[]{:S(2)}) copy-start(f32[2,128,768]{2,1,0:T(8,128)} %copy-done.6) | copy-start | bytes 2359300
  277.6 9.8 %copy-start.23 = (f32[768]{0:T(1024)S(1)}, f32[768]{0:T(1024)}, u32[]{:S(2)}) copy-start(f32[768]{0:T(1024)} %copy-done.22) | copy-start | bytes 9220
  277.6 9.8 %copy-start.25 = (f32[768]{0:T(1024)S(1)}, f32[768]{0:T(1024)}, u32[]{:S(2)}) copy-start(f32[768]{0:T(1024)} %copy-done.24) | copy-start | bytes 9220
  287.4 22.1 %copy-start.26 = (f32[768]{0:T(1024)S(1)}, f32[768]{0:T(1024)}, u32[]{:S(2)}) copy-start(f32[768]{0:T(1024)} %mul.216) | copy-start | bytes 9220
  287.4 22.1 %copy-start.30 = (f32[2,128]{1,0:T(2,128)S(1)}, f32[2,128]{1,0:T(2,128)}, u32[]{:S(2)}) copy-start(f32[2,128]{1,0:T(2,128)} %copy-done.29) | copy-start | bytes 3076
  291.7 19.3 %copy-start.16 = (bf16[2,128,768]{2,1,0:T(8,128)(2,1)S(1)}, bf16[2,128,768]{2,1,0:T(8,128)(2,1)}, u32[]{:S(2)}) copy-start(bf16[2,128,768]{2,1,0:T(8,128)(2,1)} %copy-done.15) | copy-start | bytes 1179652
  291.7 1.3 collective-permute-start.17
  293.1 3.9 collective-permute-start.18
  296.9 3.9 %collective-permute-start.19 = (f32[6,768]{1,0:T(8,128)S(1)}, f32[6,768]{1,0:T(8,128)S(1)}, u32[]{:S(2)}, u32[]{:S(2)}) collective-permute-start(f32[6,768]{1,0:T(8,128)S(1)} %add.601), channel_id=1, source_target_pairs={{0,1},{1,0},{2,3},{3,2},{4,5},{5,4},{6,7},{7,6},{8,9},{9,8},{10,11... | collective-permute-start | bytes 55304 | tf_op jit(solution)/shard_map/ppermute | solution.py:80
  300.9 3.8 collective-permute-start.20
  304.7 4.7 %collective-permute-start.21 = (f32[6,768]{1,0:T(8,128)S(1)}, f32[6,768]{1,0:T(8,128)S(1)}, u32[]{:S(2)}, u32[]{:S(2)}) collective-permute-start(f32[6,768]{1,0:T(8,128)S(1)} %add.603), channel_id=1, source_target_pairs={{0,4},{1,5},{2,6},{3,7},{4,0},{5,1},{6,2},{7,3},{8,12},{9,13},{10,... | collective-permute-start | bytes 55304 | tf_op jit(solution)/shard_map/ppermute | solution.py:80
  304.8 24.3 %collective-permute-start.25 = (bf16[4,96,1152]{2,1,0:T(8,128)(2,1)}, bf16[4,96,1152]{2,1,0:T(8,128)(2,1)}, u32[]{:S(2)}, u32[]{:S(2)}) collective-permute-start(bf16[4,96,1152]{2,1,0:T(8,128)(2,1)} %dynamic-slice_bitcast_fusion), channel_id=1, source_target_pairs={{0,1},{1,0},{2,3},{3,2},{4,5},{5,4},{6,7},{7,6},{8,9},{9,8},{10,11... | collective-permute-start | bytes 2654216 | tf_op jit(solution)/shard_map/ppermute | solution.py:80
  306.5 53.1 %collective-permute-start.33 = (bf16[384,384]{1,0:T(8,128)(2,1)}, bf16[384,384]{1,0:T(8,128)(2,1)}, u32[]{:S(2)}, u32[]{:S(2)}) collective-permute-start(bf16[384,384]{1,0:T(8,128)(2,1)} %reduce-scatter.5.cloned.1.call-done), channel_id=1, source_target_pairs={{0,16},{8,24},{16,0},{24,8},{1,17},{9,25},{17,1},{25,9},{2,18},{10... | collective-permute-start | bytes 884744 | tf_op jit(solution)/shard_map/ppermute | solution.py:80
  311.6 24.0 %collective-permute-start.22 = (bf16[768,384]{1,0:T(8,128)(2,1)S(1)}, bf16[768,384]{1,0:T(8,128)(2,1)S(1)}, u32[]{:S(2)}, u32[]{:S(2)}) collective-permute-start(bf16[768,384]{1,0:T(8,128)(2,1)S(1)} %constant_dynamic-slice_fusion.1), channel_id=1, source_target_pairs={{0,8},{8,0},{16,24},{24,16},{1,9},{9,1},{17,25},{25,17},{2,10},{10... | collective-permute-start | bytes 1769480 | tf_op jit(solution)/shard_map/ppermute | solution.py:80
  330.5 14.9 %collective-permute-start.26 = (bf16[96,1152]{1,0:T(8,128)(2,1)S(1)}, bf16[96,1152]{1,0:T(8,128)(2,1)S(1)}, u32[]{:S(2)}, u32[]{:S(2)}) collective-permute-start(bf16[96,1152]{1,0:T(8,128)(2,1)S(1)} %get-tuple-element.120), channel_id=1, source_target_pairs={{0,2},{1,3},{2,4},{3,5},{4,6},{5,7},{6,0},{7,1},{8,10},{9,11},{10,... | collective-permute-start | bytes 663560 | tf_op jit(solution)/shard_map/ppermute | solution.py:160
  331.6 26.3 %collective-permute-start.27 = (bf16[96,1152]{1,0:T(8,128)(2,1)S(1)}, bf16[96,1152]{1,0:T(8,128)(2,1)S(1)}, u32[]{:S(2)}, u32[]{:S(2)}) collective-permute-start(bf16[96,1152]{1,0:T(8,128)(2,1)S(1)} %get-tuple-element.122), channel_id=1, source_target_pairs={{0,4},{1,5},{2,6},{3,7},{4,0},{5,1},{6,2},{7,3},{8,12},{9,13},{10,... | collective-permute-start | bytes 663560 | tf_op jit(solution)/shard_map/ppermute | solution.py:160
  333.7 25.9 %copy-start.18 = (bf16[384,384]{1,0:T(8,128)(2,1)S(1)}, bf16[384,384]{1,0:T(8,128)(2,1)}, u32[]{:S(2)}) copy-start(bf16[384,384]{1,0:T(8,128)(2,1)} %reduce-scatter.5.cloned.1.call-done) | copy-start | bytes 884740
  333.7 24.3 %collective-permute-start.28 = (bf16[96,1152]{1,0:T(8,128)(2,1)S(1)}, bf16[96,1152]{1,0:T(8,128)(2,1)S(1)}, u32[]{:S(2)}, u32[]{:S(2)}) collective-permute-start(bf16[96,1152]{1,0:T(8,128)(2,1)S(1)} %get-tuple-element.121), channel_id=1, source_target_pairs={{0,6},{1,7},{2,0},{3,1},{4,2},{5,3},{6,4},{7,5},{8,14},{9,15},{10,... | collective-permute-start | bytes 663560 | tf_op jit(solution)/shard_map/ppermute | solution.py:160
  336.5 38.4 %all-to-all-start.1 = ((bf16[8,96,384]{2,1,0:T(8,128)(2,1)}), bf16[8,96,384]{2,1,0:T(8,128)(2,1)S(1)}, u32[]{:S(2)}, u32[]{:S(2)}) async-start(bf16[8,96,384]{2,1,0:T(8,128)(2,1)} %bitcast.30), calls=%async_computation.1 | async-start | bytes 1179648 | tf_op jit(solution)/shard_map/all_to_all | solution.py:140
  358.1 7.1 %collective-permute-start.29 = (bf16[96,1152]{1,0:T(8,128)(2,1)S(1)}, bf16[96,1152]{1,0:T(8,128)(2,1)S(1)}, u32[]{:S(2)}, u32[]{:S(2)}) collective-permute-start(bf16[96,1152]{1,0:T(8,128)(2,1)S(1)} %fusion.13), channel_id=1, source_target_pairs={{0,16},{8,24},{16,0},{24,8},{1,17},{9,25},{17,1},{25,9},{2,18},{10... | collective-permute-start | bytes 663560 | tf_op jit(solution)/shard_map/ppermute | solution.py:80
  360.6 5.3 %collective-permute-start.34 = (bf16[384,384]{1,0:T(8,128)(2,1)S(1)}, bf16[384,384]{1,0:T(8,128)(2,1)S(1)}, u32[]{:S(2)}, u32[]{:S(2)}) collective-permute-start(bf16[384,384]{1,0:T(8,128)(2,1)S(1)} %add_convert_fusion.6), channel_id=1, source_target_pairs={{0,8},{8,0},{16,24},{24,16},{1,9},{9,1},{17,25},{25,17},{2,10},{10... | collective-permute-start | bytes 884744 | tf_op jit(solution)/shard_map/ppermute | solution.py:80
  360.7 15.9 %collective-permute-start.31 = (bf16[96,1920]{1,0:T(8,128)(2,1)}, bf16[96,1920]{1,0:T(8,128)(2,1)S(1)}, u32[]{:S(2)}, u32[]{:S(2)}) collective-permute-start(bf16[96,1920]{1,0:T(8,128)(2,1)} %reduce-scatter.3.cloned.1.call-done), channel_id=1, source_target_pairs={{0,16},{8,24},{16,0},{24,8},{1,17},{9,25},{17,1},{25,9},{2,18},{10... | collective-permute-start | bytes 1105928 | tf_op jit(solution)/shard_map/ppermute | solution.py:80
  365.2 11.3 %copy-start.17 = (bf16[96,1920]{1,0:T(8,128)(2,1)S(1)}, bf16[96,1920]{1,0:T(8,128)(2,1)}, u32[]{:S(2)}) copy-start(bf16[96,1920]{1,0:T(8,128)(2,1)} %reduce-scatter.3.cloned.1.call-done) | copy-start | bytes 1105924
  365.2 1.8 collective-permute-start.30
  375.0 4.4 %collective-permute-start.23 = (bf16[96,384]{1,0:T(8,128)(2,1)S(1)}, bf16[96,384]{1,0:T(8,128)(2,1)S(1)}, u32[]{:S(2)}, u32[]{:S(2)}) collective-permute-start(bf16[96,384]{1,0:T(8,128)(2,1)S(1)} %reduce_sum.72), channel_id=1, source_target_pairs={{0,16},{8,24},{16,0},{24,8},{1,17},{9,25},{17,1},{25,9},{2,18},{10... | collective-permute-start | bytes 221192 | tf_op jit(solution)/shard_map/ppermute | solution.py:80
  376.7 5.2 %collective-permute-start.32 = (bf16[96,1920]{1,0:T(8,128)(2,1)S(1)}, bf16[96,1920]{1,0:T(8,128)(2,1)S(1)}, u32[]{:S(2)}, u32[]{:S(2)}) collective-permute-start(bf16[96,1920]{1,0:T(8,128)(2,1)S(1)} %add_convert_fusion.5), channel_id=1, source_target_pairs={{0,8},{8,0},{16,24},{24,16},{1,9},{9,1},{17,25},{25,17},{2,10},{10... | collective-permute-start | bytes 1105928 | tf_op jit(solution)/shard_map/ppermute | solution.py:80
  379.5 1.6 collective-permute-start.24
  (18 other events, 26.5 us)
Sparse Core Ops, SparseCore 0:
  10.9 73.2 all-gather.2
  86.9 50.2 all-gather.4
  195.4 66.8 reduce-scatter.4
  269.5 89.4 reduce-scatter.2

commit v4 on v3

--- a/solution.py
+++ b/solution.py
@@ -195,19 +195,25 @@
     )(core, x, own, other)
 
 
-def attend_kernel(core_ref, q_ref, k_ref, v_ref, mask_ref, out_ref, share_ref):
+def attend_kernel(
+    core_ref, q_ref, k_ref, v_ref, mask_ref, out_ref, share_ref, scores_ref, chunk=64
+):
     queries, keys, values = q_ref[...], k_ref[...], v_ref[...]
+    length = queries.shape[0]
     first = lax.broadcasted_iota(jnp.int32, queries.shape, 1) < queries.shape[1] // 2
-    real = mask_ref[...] > 0
+    real = jnp.broadcast_to(mask_ref[...], (chunk, length)) > 0
     mixed = []
     for head in range(2):
         mine = first if head == 0 else jnp.logical_not(first)
         scaled = jnp.where(mine, queries, jnp.zeros_like(queries)) * jnp.asarray(0.125, low)
-        scores = jnp.where(real, dot(scaled, keys, NT), masked_score)
-        raised = jnp.exp(scores - jnp.max(scores, axis=-1, keepdims=True))
-        share = (raised * (1.0 / jnp.sum(raised, axis=-1, keepdims=True))).astype(low)
-        share_ref[head] = share
-        mixed.append(dot(share, values))
+        scores_ref[head] = dot(scaled, keys, NT)
+    for head in range(2):
+        for row in range(0, length, chunk):
+            scores = jnp.where(real, scores_ref[head, row : row + chunk], masked_score)
+            raised = jnp.exp(scores - jnp.max(scores, axis=-1, keepdims=True))
+            share = raised * (1.0 / jnp.sum(raised, axis=-1, keepdims=True))
+            share_ref[head, row : row + chunk] = share.astype(low)
+        mixed.append(dot(share_ref[head], values))
     out_ref[...] = jnp.where(first, mixed[0], mixed[1]).astype(low)
 
 
@@ -236,6 +242,7 @@
             shape((docs, length, columns // 3)),
             shape((docs, 2 * pairs, length, length)),
         ],
+        [pltpu.VMEM((2, length, length), wide)],
     )(core, packed, packed, packed, mask[:, None, :])
 
 
@@ -291,11 +298,13 @@
     return value * below, below + value * (bell * 0.3989422804014327)
 
 
-def up_kernel(core_ref, x_ref, own_ref, other_ref, out_ref, slope_ref):
+def up_kernel(core_ref, x_ref, own_ref, other_ref, out_ref, slope_ref, inner, chunk=16):
     def block(weight):
-        value, slope = gelu_parts(dot(x_ref[...], weight))
-        out_ref[...] = value.astype(low)
-        slope_ref[...] = slope.astype(low)
+        inner[...] = dot(x_ref[...], weight)
+        for row in range(0, inner.shape[0], chunk):
+            value, slope = gelu_parts(inner[row : row + chunk])
+            out_ref[row : row + chunk] = value.astype(low)
+            slope_ref[row : row + chunk] = slope.astype(low)
 
     @pl.when(pl.program_id(0) == 0)
     def _():
@@ -306,7 +315,7 @@
         block(other_ref[...])
 
 
-def up(x, own, other, core, columns=512, rows=512):
+def up(x, own, other, core, columns=768, rows=512):
     count, features = x.shape
     half = own.shape[1]
     steps = half // columns
@@ -324,6 +333,7 @@
         ],
         [out, out],
         [shape((count, 2 * half))] * 2,
+        [pltpu.VMEM((rows, columns), wide)],
     )(core, x, own, other)
 
 

time: 396 us -> 398 us (level)
  the two profiles are of different devices: /device:TPU:0 before, /device:TPU:11 now
where the time goes in v4:
time: 398 us; the launch traced here: 392 us
  Pallas kernels  151 us (38%)
  waiting for transfers between devices  106 us (27%)
  starting transfers between devices  54.8 us (14%)
  other arithmetic  31.1 us (8%)
  local copies, waits for them, and re-layouts  20.8 us (5%)
  between operations  15.9 us (4%)
  matrix products  12 us (3%)
    ppermute x29, waiting for transfers between devices, swap(): return lax.ppermute(value, axis, [(i, i ^ bit) for i in range(size)])  43.1 us
    ppermute x29, starting transfers between devices, swap(): return lax.ppermute(value, axis, [(i, i ^ bit) for i in range(size)])  37.7 us
    ppermute x3, waiting for transfers between devices, scatter_end(): lax.ppermute(away, 'fsdp', [(i, (i + 2 * step) % (2 * lines)) for i in ra...  30.8 us
    pallas_call x1, Pallas kernels, inner_back(): call(inner_kernel, 'inner_back', (count // rows,), [block, block, tall, b...  22.8 us
    pallas_call x1, Pallas kernels, up(): call(up_kernel, 'up', (2, steps, count // rows), [pl.BlockSpec((rows, fea...  21.5 us
    all_to_all x1, waiting for transfers between devices, spread(): return lax.all_to_all(copies, axis, 0, 0, axis_index_groups=groups)  21.2 us
    pallas_call x1, Pallas kernels, attend_back(): call(attend_back_kernel, 'attend_back', (docs, pairs), [column_spec(lengt...  18.9 us
    pallas_call x2, Pallas kernels, weight_columns(): call(columns_kernel, 'weight_columns', (parts, steps), [pl.BlockSpec((cou...  16.8 us
  transfers between devices with their start and end apart: 41, of which 22 were waited for; matrix products, arithmetic and copies ran while one was open for 12% of the time, Pallas kernels for 33%

profile of v4, /device:TPU:11, one launch (start us, length us, event | category | flops | bytes accessed | tf_op | source)
XLA Modules:
  0.0 391.6 jit_solution(12105873727446478974)
XLA Ops:
  7.3 1.7 reshape.410
  11.2 5.7 %all-to-all-start = ((bf16[8,112,384]{2,1,0:T(8,128)(2,1)}), bf16[8,112,384]{2,1,0:T(8,128)(2,1)S(1)}, u32[]{:S(2)}, u32[]{:S(2)}) async-start(bf16[8,112,384]{2,1,0:T(8,128)(2,1)} %broadcast_in_dim.39), calls=%async_computation | async-start | bytes 1376256 | tf_op jit(solution)/shard_map/all_to_all | solution.py:75
  19.6 21.2 %all-to-all-done = bf16[8,112,384]{2,1,0:T(8,128)(2,1)S(1)} async-done(((bf16[8,112,384]{2,1,0:T(8,128)(2,1)}), bf16[8,112,384]{2,1,0:T(8,128)(2,1)S(1)}, u32[]{:S(2)}, u32[]{:S(2)}) %all-to-all-start) | async-done | bytes 688160 | tf_op jit(solution)/shard_map/all_to_all | solution.py:75
  40.8 3.2 collective-permute-start
  45.4 3.5 collective-permute-start.7
  54.9 1.3 collective-permute-done.2
  56.9 1.2 collective-permute-start.3
  58.1 2.0 collective-permute-done.3
  60.7 1.2 collective-permute-start.4
  62.0 4.5 %collective-permute-done.7 = bf16[96,768]{1,0:T(8,128)(2,1)S(1)} collective-permute-done((bf16[96,768]{1,0:T(8,128)(2,1)S(1)}, bf16[96,768]{1,0:T(8,128)(2,1)S(1)}, u32[]{:S(2)}, u32[]{:S(2)}) %collective-permute-start.7) | collective-permute-done | bytes 147488 | tf_op jit(solution)/shard_map/ppermute | solution.py:95
  67.2 4.3 %collective-permute-start.5 = (f32[3,768]{1,0:T(4,128)S(1)}, f32[3,768]{1,0:T(4,128)S(1)}, u32[]{:S(2)}, u32[]{:S(2)}) collective-permute-start(f32[3,768]{1,0:T(4,128)S(1)} %pad_maximum_fusion.7), channel_id=1, source_target_pairs={{0,4},{1,5},{2,6},{3,7},{4,0},{5,1},{6,2},{7,3},{8,12},{9,13},{10,... | collective-permute-start | bytes 27656 | tf_op jit(solution)/shard_map/ppermute | solution.py:80
  72.4 2.9 collective-permute-start.9
  76.0 5.1 %all-gather.3.cloned.1.call-done.own_ref.merge_own_ref = bf16[768,1536]{1,0:T(8,128)(2,1)} async-done(((bf16[96,1536]{1,0:T(8,128)(2,1)}), bf16[768,1536]{1,0:T(8,128)(2,1)}) %all-gather.3.cloned.1.call-update) | async-done | bytes 2359312 | tf_op jit(solution)/shard_map/all_gather | solution.py:113
  81.1 1.3 collective-permute-start.10
  84.5 2.3 convert_add_fusion
  86.9 1.5 bitcast_convert_fusion.1.x_ref.left_ref
  90.9 1.4 copy-done.2
  92.3 9.7 %project.1 = bf16[1024,2304]{1,0:T(8,128)(2,1)} custom-call(s32[1]{0:T(128)} %bitcast.core_ref, bf16[1024,768]{1,0:T(8,128)(2,1)} %bitcast_convert_fusion.1.x_ref.left_ref, bf16[768,1536]{1,0:T(8,128)(2,1)} %all-gather.3.cloned.1.call-done.own_ref.merge_own_ref, bf16[768,1536]{1,0:T(8,128)(2,1)} %copy-done.2), custom_call_target="tpu_custom_call" | custom-call | tf_op jit(solution)/shard_map/project/pallas_call | solution.py:188
  102.0 15.9 %attend.1 = (bf16[2,512,768]{2,1,0:T(8,128)(2,1)}, bf16[2,12,512,512]{3,2,1,0:T(8,128)(2,1)}) custom-call(s32[1]{0:T(128)} %bitcast.core_ref, bf16[2,512,2304]{2,1,0:T(8,128)(2,1)} %bitcast.83, bf16[2,512,2304]{2,1,0:T(8,128)(2,1)} %bitcast.84, bf16[2,512,2304]{2,1,0:T(8,128)(2,1)} %bitcast.85, s32[2,1,512]{2,1,0:T(1,128)} %broadcast_in_dim.45.mask_ref), custom_call_target="tpu_custom_call" | custom-call | tf_op jit(solution)/shard_map/attend/pallas_call | solution.py:227
  117.9 2.9 maximum_select_fusion.own_ref.up_own_ref
  122.5 7.2 %merge.1 = (f32[1024,768]{1,0:T(8,128)}, bf16[1024,768]{1,0:T(8,128)(2,1)}) custom-call(s32[1]{0:T(128)} %bitcast.core_ref, bf16[1024,768]{1,0:T(8,128)(2,1)} %bitcast.96, f32[1024,768]{1,0:T(8,128)} %bitcast.93, f32[8,768]{1,0:T(8,128)} %pad.9.vectors_ref, bf16[768,1536]{1,0:T(8,128)(2,1)} %all-gather.3.cloned.1.call-done.own_ref.merge_own_ref, ...), custom_call_target="tpu_custom_call" | custom-call | tf_op jit(solution)/shard_map/merge/pallas_call | solution.py:386
  129.8 21.5 %up.1 = (bf16[1024,3072]{1,0:T(8,128)(2,1)}, bf16[1024,3072]{1,0:T(8,128)(2,1)}) custom-call(s32[1]{0:T(128)} %bitcast.core_ref, bf16[1024,768]{1,0:T(8,128)(2,1)} %get-tuple-element.51.x_ref.left_ref, bf16[768,1536]{1,0:T(8,128)(2,1)} %copy-done.5, bf16[768,1536]{1,0:T(8,128)(2,1)} %collective-permute-done.12.other_ref.up_other_ref), custom_call_target="tpu_custom_call" | custom-call | tf_op jit(solution)/shard_map/up/pallas_call | solution.py:325
  151.4 4.6 %collective-permute-done.13.other_ref.down_other_ref = bf16[3072,384]{1,0:T(8,128)(2,1)S(1)} collective-permute-done((bf16[3072,384]{1,0:T(8,128)(2,1)}, bf16[3072,384]{1,0:T(8,128)(2,1)S(1)}, u32[]{:S(2)}, u32[]{:S(2)}) %collective-permute-start.13) | collective-permute-done | bytes 2359328 | tf_op jit(solution)/shard_map/ppermute | solution.py:80
  156.0 1.4 copy-done.8
  157.4 14.2 %down.1 = (f32[1024,768]{1,0:T(8,128)}, f32[1024,768]{1,0:T(8,128)}, bf16[1024,768]{1,0:T(8,128)(2,1)}, f32[8,768]{1,0:T(8,128)}) custom-call(s32[1]{0:T(128)} %bitcast.core_ref, bf16[1024,3072]{1,0:T(8,128)(2,1)} %get-tuple-element.54.x_ref.left_ref, f32[1024,768]{1,0:T(8,128)} %get-tuple-element.55.sum_ref, bf16[1024,768]{1,0:T(8,128)(2,1)} %bitcast.105, ...), custom_call_target="tpu_custom_call" | custom-call | tf_op jit(solution)/shard_map/down/pallas_call | solution.py:443
  171.6 9.2 %weight_columns.2 = (bf16[3072,384]{1,0:T(8,128)(2,1)}, bf16[3072,384]{1,0:T(8,128)(2,1)}) custom-call(s32[1]{0:T(128)} %bitcast.core_ref, bf16[1024,3072]{1,0:T(8,128)(2,1)} %get-tuple-element.54.x_ref.left_ref, bf16[1,1024,768]{2,1,0:T(8,128)(2,1)} %bitcast.98, bf16[1,1024,768]{2,1,0:T(8,128)(2,1)} %bitcast.99), custom_call_target="tpu_custom_call" | custom-call | tf_op jit(solution)/shard_map/weight_columns/pallas_call | solution.py:602
  180.9 4.6 %collective-permute-done.14 = bf16[3072,384]{1,0:T(8,128)(2,1)S(1)} collective-permute-done((bf16[3072,384]{1,0:T(8,128)(2,1)}, bf16[3072,384]{1,0:T(8,128)(2,1)S(1)}, u32[]{:S(2)}, u32[]{:S(2)}) %collective-permute-start.14) | collective-permute-done | bytes 2359328 | tf_op jit(solution)/shard_map/ppermute | solution.py:80
  185.5 3.6 add_convert_fusion.1
  189.2 22.8 %inner_back.1 = (bf16[1024,3072]{1,0:T(8,128)(2,1)}, f32[1024,768]{1,0:T(8,128)}, bf16[1024,768]{1,0:T(8,128)(2,1)}, bf16[1024,768]{1,0:T(8,128)(2,1)}, f32[8,768]{1,0:T(8,128)}) custom-call(s32[1]{0:T(128)} %bitcast.core_ref, bf16[1024,768]{1,0:T(8,128)(2,1)} %get-tuple-element.62.low_ref, f32[1024,768]{1,0:T(8,128)} %get-tuple-element.63.delta_ref, ...), custom_call_target="tpu_custom_call" | custom-call | tf_op jit(solution)/shard_map/inner_back/pallas_call | solution.py:533
  212.0 10.1 %weight_wide.1 = (bf16[768,1920]{1,0:T(8,128)(2,1)}, bf16[768,1920]{1,0:T(8,128)(2,1)}) custom-call(s32[1]{0:T(128)} %bitcast.core_ref, bf16[1024,768]{1,0:T(8,128)(2,1)} %get-tuple-element.51.x_ref.left_ref, bf16[1024,3072]{1,0:T(8,128)(2,1)} %get-tuple-element.68.right_ref), custom_call_target="tpu_custom_call" | custom-call | tf_op jit(solution)/shard_map/weight_wide/pallas_call | solution.py:631
  222.1 4.4 %weight_into.1 = (bf16[768,1920]{1,0:T(8,128)(2,1)}, bf16[768,1920]{1,0:T(8,128)(2,1)}) custom-call(s32[1]{0:T(128)} %bitcast.core_ref, bf16[1024,768]{1,0:T(8,128)(2,1)} %bitcast.97, bf16[1024,768]{1,0:T(8,128)(2,1)} %get-tuple-element.67.own_ref.other_ref, ...), custom_call_target="tpu_custom_call", output_to_operand_aliasing={{0}: (4, {}), {1}: (5, {})} | custom-call | tf_op jit(solution)/shard_map/weight_into/pallas_call | solution.py:579
  226.5 5.5 %collective-permute-done.15 = bf16[768,1920]{1,0:T(8,128)(2,1)S(1)} collective-permute-done((bf16[768,1920]{1,0:T(8,128)(2,1)}, bf16[768,1920]{1,0:T(8,128)(2,1)S(1)}, u32[]{:S(2)}, u32[]{:S(2)}) %collective-permute-start.15) | collective-permute-done | bytes 2949152 | tf_op jit(solution)/shard_map/ppermute | solution.py:80
  232.0 4.2 %add_convert_fusion = bf16[768,1920]{1,0:T(8,128)(2,1)} fusion(bf16[768,1920]{1,0:T(8,128)(2,1)S(1)} %collective-permute-done.15, bf16[768,1920]{1,0:T(8,128)(2,1)} %get-tuple-element.71), kind=kLoop, calls=%fused_computation | loop fusion | flops 5898240 | bytes 8847360 | tf_op jit(solution)/shard_map/convert_element_type | solution.py:125
  236.2 18.9 %attend_back.1 = bf16[3,2,512,768]{3,2,1,0:T(8,128)(2,1)} custom-call(s32[1]{0:T(128)} %bitcast.core_ref, bf16[2,512,2304]{2,1,0:T(8,128)(2,1)} %bitcast.86, bf16[2,512,2304]{2,1,0:T(8,128)(2,1)} %bitcast.87, bf16[2,512,2304]{2,1,0:T(8,128)(2,1)} %bitcast.88, bf16[2,12,512,512]{3,2,1,0:T(8,128)(2,1)} %get-tuple-element.66.share_ref, ...), custom_call_target="tpu_custom_call" | custom-call | tf_op jit(solution)/shard_map/attend_back/pallas_call | solution.py:273
  255.1 7.6 %weight_columns.3 = (bf16[768,1152]{1,0:T(8,128)(2,1)}, bf16[768,1152]{1,0:T(8,128)(2,1)}) custom-call(s32[1]{0:T(128)} %bitcast.core_ref, bf16[1024,768]{1,0:T(8,128)(2,1)} %bitcast_convert_fusion.1.x_ref.left_ref, bf16[3,1024,768]{2,1,0:T(8,128)(2,1)} %bitcast.89, bf16[3,1024,768]{2,1,0:T(8,128)(2,1)} %bitcast.90), custom_call_target="tpu_custom_call" | custom-call | tf_op jit(solution)/shard_map/weight_columns/pallas_call | solution.py:602
  264.4 2.3 collective-permute-done.16
  266.6 1.2 copy-done.9
  267.9 2.4 add_convert_fusion.2
  271.3 10.0 %joined_back.1 = f32[1024,768]{1,0:T(8,128)} custom-call(s32[1]{0:T(128)} %bitcast.core_ref, f32[1024,768]{1,0:T(8,128)} %get-tuple-element.65.one_ref, bf16[3,1024,768]{2,1,0:T(8,128)(2,1)} %bitcast.91, bf16[3,1024,768]{2,1,0:T(8,128)(2,1)} %bitcast.92, bf16[768,1536]{1,0:T(8,128)(2,1)} %all-gather.3.cloned.1.call-done.own_ref.merge_own_ref, ...), custom_call_target="tpu_custom_call" | custom-call | tf_op jit(solution)/shard_map/joined_back/pallas_call | solution.py:671
  281.3 4.3 %multiply_reduce_fusion = (f32[768]{0:T(1024)S(1)}, f32[768]{0:T(1024)S(1)}, f32[2,128,768]{2,1,0:T(8,128)}) fusion(f32[2,128,768]{2,1,0:T(8,128)S(1)} %copy-done.7, f32[768]{0:T(1024)S(1)} %copy-done.23, f32[768]{0:T(1024)S(1)} %copy-done.25, f32[2,512,768]{2,1,0:T(8,128)} %bitcast.94, s32[2,512]{1,0:T(2,128)S(1)} %copy-done.21), kind=kOutput, calls=%fused_computation.20 | convolution fusion | flops 1209072128 | bytes 4734976 | tf_op jit(solution)/shard_map/drs,drc->dsc/dot_general | solution.py:838
  287.0 1.5 collective-permute-start.18
  288.5 1.7 collective-permute-done.18
  290.1 1.6 collective-permute-start.19
  291.7 1.6 collective-permute-done.19
  293.3 1.3 collective-permute-start.20
  294.6 1.9 collective-permute-done.20
  296.6 1.2 collective-permute-start.25
  297.8 1.4 collective-permute-start.33
  300.1 1.4 multiply_convert_fusion
  302.2 3.4 collective-permute-start.22
  306.2 1.3 copy-done.4
  307.6 3.2 convolution_add_fusion
  310.8 11.0 %collective-permute-done.25 = bf16[4,96,1152]{2,1,0:T(8,128)(2,1)} collective-permute-done((bf16[4,96,1152]{2,1,0:T(8,128)(2,1)}, bf16[4,96,1152]{2,1,0:T(8,128)(2,1)}, u32[]{:S(2)}, u32[]{:S(2)}) %collective-permute-start.25) | collective-permute-done | bytes 884768 | tf_op jit(solution)/shard_map/ppermute | solution.py:80
  321.8 1.4 fusion
  324.1 1.7 collective-permute-start.27
  326.8 5.3 %all-to-all-start.1 = ((bf16[8,96,384]{2,1,0:T(8,128)(2,1)}), bf16[8,96,384]{2,1,0:T(8,128)(2,1)S(1)}, u32[]{:S(2)}, u32[]{:S(2)}) async-start(bf16[8,96,384]{2,1,0:T(8,128)(2,1)} %bitcast.30), calls=%async_computation.1 | async-start | bytes 1179648 | tf_op jit(solution)/shard_map/all_to_all | solution.py:140
  332.0 3.6 collective-permute-done.26
  335.6 24.6 %collective-permute-done.27 = bf16[96,1152]{1,0:T(8,128)(2,1)S(1)} collective-permute-done((bf16[96,1152]{1,0:T(8,128)(2,1)S(1)}, bf16[96,1152]{1,0:T(8,128)(2,1)S(1)}, u32[]{:S(2)}, u32[]{:S(2)}) %collective-permute-start.27) | collective-permute-done | bytes 221216 | tf_op jit(solution)/shard_map/ppermute | solution.py:160
  360.2 2.6 collective-permute-done.28
  364.3 1.5 collective-permute-start.34
  367.0 1.8 collective-permute-done.29
  368.9 3.7 collective-permute-start.30
  374.6 2.1 collective-permute-done.31
  376.8 2.9 collective-permute-start.32
  (220 shorter events, 39.3 us)
Async XLA Ops:
  7.2 10.8 %copy-start = (bf16[384,768]{1,0:T(8,128)(2,1)S(1)}, bf16[384,768]{1,0:T(8,128)(2,1)}, u32[]{:S(2)}) copy-start(bf16[384,768]{1,0:T(8,128)(2,1)} %param.25) | copy-start | bytes 1769476
  7.2 2.8 copy-start.34
  7.2 2.8 copy-start.35
  7.3 3.0 copy-start.28
  7.3 73.8 %all-gather.3.cloned.1.call-start = ((), (), s32[]{:S(2)}) async-start(), calls=%async_computation.4 | async-start | bytes 2654208 | tf_op jit(solution)/shard_map/all_gather | solution.py:113
  10.0 8.7 %copy-start.21 = (s32[2,512]{1,0:T(2,128)S(1)}, s32[2,512]{1,0:T(2,128)}, u32[]{:S(2)}) copy-start(s32[2,512]{1,0:T(2,128)} %param.29) | copy-start | bytes 12292
  10.0 8.9 %copy-start.10 = (bf16[2,512,768]{2,1,0:T(8,128)(2,1)S(1)}, bf16[2,512,768]{2,1,0:T(8,128)(2,1)}, u32[]{:S(2)}) copy-start(bf16[2,512,768]{2,1,0:T(8,128)(2,1)} %param.16) | copy-start | bytes 4718596
  11.2 29.5 %all-to-all-start = ((bf16[8,112,384]{2,1,0:T(8,128)(2,1)}), bf16[8,112,384]{2,1,0:T(8,128)(2,1)S(1)}, u32[]{:S(2)}, u32[]{:S(2)}) async-start(bf16[8,112,384]{2,1,0:T(8,128)(2,1)} %broadcast_in_dim.39), calls=%async_computation | async-start | bytes 1376256 | tf_op jit(solution)/shard_map/all_to_all | solution.py:75
  16.9 134.3 %all-gather.5.cloned.1.call-start = ((), (), s32[]{:S(2)}) async-start(), calls=%async_computation.5 | async-start | bytes 2654208 | tf_op jit(solution)/shard_map/all_gather | solution.py:113
  19.0 25.0 %copy-start.40 = (s32[2]{0:T(128)S(1)}, s32[2]{0:T(128)}, u32[]{:S(2)}) copy-start(s32[2]{0:T(128)} %param.28) | copy-start | bytes 28
  19.6 29.5 %copy-start.15 = (bf16[2,128,768]{2,1,0:T(8,128)(2,1)}, bf16[2,128,768]{2,1,0:T(8,128)(2,1)S(1)}, u32[]{:S(2)}) copy-start(bf16[2,128,768]{2,1,0:T(8,128)(2,1)S(1)} %fusion.1) | copy-start | bytes 1179652
  40.8 8.3 %collective-permute-start = (bf16[8,112,384]{2,1,0:T(8,128)(2,1)S(1)}, bf16[8,112,384]{2,1,0:T(8,128)(2,1)S(1)}, u32[]{:S(2)}, u32[]{:S(2)}) collective-permute-start(bf16[8,112,384]{2,1,0:T(8,128)(2,1)S(1)} %all-to-all-done), channel_id=1, source_target_pairs={{0,8},{8,0},{16,24},{24,16},{1,9},{9,1},{17,25},{25,17},{2,10},{10... | collective-permute-start | bytes 2064392 | tf_op jit(solution)/shard_map/ppermute | solution.py:80
  45.3 4.7 %copy-start.29 = (f32[2,128]{1,0:T(2,128)}, f32[2,128]{1,0:T(2,128)S(1)}, u32[]{:S(2)}) copy-start(f32[2,128]{1,0:T(2,128)S(1)} %compare_convert_fusion) | copy-start | bytes 3076
  45.4 12.8 %collective-permute-start.6 = (bf16[96,768]{1,0:T(8,128)(2,1)S(1)}, bf16[96,768]{1,0:T(8,128)(2,1)S(1)}, u32[]{:S(2)}, u32[]{:S(2)}) collective-permute-start(bf16[96,768]{1,0:T(8,128)(2,1)S(1)} %constant_dynamic-slice_fusion.5), channel_id=1, source_target_pairs={{0,2},{1,3},{2,4},{3,5},{4,6},{5,7},{6,0},{7,1},{8,10},{9,11},{10,... | collective-permute-start | bytes 442376 | tf_op jit(solution)/shard_map/ppermute | solution.py:95
  45.4 21.1 %collective-permute-start.7 = (bf16[96,768]{1,0:T(8,128)(2,1)S(1)}, bf16[96,768]{1,0:T(8,128)(2,1)S(1)}, u32[]{:S(2)}, u32[]{:S(2)}) collective-permute-start(bf16[96,768]{1,0:T(8,128)(2,1)S(1)} %constant_dynamic-slice_fusion.5), channel_id=1, source_target_pairs={{0,4},{1,5},{2,6},{3,7},{4,0},{5,1},{6,2},{7,3},{8,12},{9,13},{10,... | collective-permute-start | bytes 442376 | tf_op jit(solution)/shard_map/ppermute | solution.py:95
  48.8 23.6 %collective-permute-start.8 = (bf16[96,768]{1,0:T(8,128)(2,1)S(1)}, bf16[96,768]{1,0:T(8,128)(2,1)S(1)}, u32[]{:S(2)}, u32[]{:S(2)}) collective-permute-start(bf16[96,768]{1,0:T(8,128)(2,1)S(1)} %constant_dynamic-slice_fusion.5), channel_id=1, source_target_pairs={{0,6},{1,7},{2,0},{3,1},{4,2},{5,3},{6,4},{7,5},{8,14},{9,15},{10,... | collective-permute-start | bytes 442376 | tf_op jit(solution)/shard_map/ppermute | solution.py:95
  51.1 1.5 collective-permute-start.1
  51.8 24.2 %copy-start.19 = (f32[8,6,96]{2,1,0:T(8,128)}, f32[8,6,96]{2,1,0:T(8,128)S(1)}, u32[]{:S(2)}) copy-start(f32[8,6,96]{2,1,0:T(8,128)S(1)} %reshape.426) | copy-start | bytes 55300
  53.2 3.0 collective-permute-start.2
  54.9 242.9 %reduce-scatter.5.cloned.1.call-start = ((), (), s32[]{:S(2)}) async-start(), calls=%async_computation.7 | async-start | bytes 2654208 | tf_op jit(solution)/shard_map/reduce_scatter | solution.py:816
  56.9 3.2 collective-permute-start.3
  60.7 5.8 %collective-permute-start.4 = (f32[3,768]{1,0:T(4,128)S(1)}, f32[3,768]{1,0:T(4,128)S(1)}, u32[]{:S(2)}, u32[]{:S(2)}) collective-permute-start(f32[3,768]{1,0:T(4,128)S(1)} %pad_maximum_fusion.6), channel_id=1, source_target_pairs={{0,2},{1,3},{2,0},{3,1},{4,6},{5,7},{6,4},{7,5},{8,10},{9,11},{10,... | collective-permute-start | bytes 27656 | tf_op jit(solution)/shard_map/ppermute | solution.py:80
  67.2 8.2 %collective-permute-start.5 = (f32[3,768]{1,0:T(4,128)S(1)}, f32[3,768]{1,0:T(4,128)S(1)}, u32[]{:S(2)}, u32[]{:S(2)}) collective-permute-start(f32[3,768]{1,0:T(4,128)S(1)} %pad_maximum_fusion.7), channel_id=1, source_target_pairs={{0,4},{1,5},{2,6},{3,7},{4,0},{5,1},{6,2},{7,3},{8,12},{9,13},{10,... | collective-permute-start | bytes 27656 | tf_op jit(solution)/shard_map/ppermute | solution.py:80
  72.4 16.6 %collective-permute-start.9 = (bf16[4,96,768]{2,1,0:T(8,128)(2,1)S(1)}, bf16[4,96,768]{2,1,0:T(8,128)(2,1)S(1)}, u32[]{:S(2)}, u32[]{:S(2)}) collective-permute-start(bf16[4,96,768]{2,1,0:T(8,128)(2,1)S(1)} %bitcast_dynamic-update-slice_fusion), channel_id=1, source_target_pairs={{0,1},{1,0},{2,3},{3,2},{4,5},{5,4},{6,7},{7,6},{8,9},{9,8},{10,11... | collective-permute-start | bytes 1769480 | tf_op jit(solution)/shard_map/ppermute | solution.py:80
  81.1 9.8 %collective-permute-start.10 = (bf16[768,1536]{1,0:T(8,128)(2,1)}, bf16[768,1536]{1,0:T(8,128)(2,1)S(1)}, u32[]{:S(2)}, u32[]{:S(2)}) collective-permute-start(bf16[768,1536]{1,0:T(8,128)(2,1)} %all-gather.3.cloned.1.call-done.own_ref.merge_own_ref), channel_id=1, source_target_pairs={{0,8},{8,0},{16,24},{24,16},{1,9},{9,1},{17,25},{25,17},{2,10},{10... | collective-permute-start | bytes 7077896 | tf_op jit(solution)/shard_map/ppermute | solution.py:80
  90.2 27.8 %collective-permute-start.11 = (bf16[768,768]{1,0:T(8,128)(2,1)}, bf16[768,768]{1,0:T(8,128)(2,1)}, u32[]{:S(2)}, u32[]{:S(2)}) collective-permute-start(bf16[768,768]{1,0:T(8,128)(2,1)} %bitcast.18), channel_id=1, source_target_pairs={{0,16},{8,24},{16,0},{24,8},{1,17},{9,25},{17,1},{25,9},{2,18},{10... | collective-permute-start | bytes 3538952 | tf_op jit(solution)/shard_map/ppermute | solution.py:80
  117.9 3.9 copy-start.20
  120.8 8.9 %copy-start.5 = (bf16[768,1536]{1,0:T(8,128)(2,1)}, bf16[768,1536]{1,0:T(8,128)(2,1)S(1)}, u32[]{:S(2)}) copy-start(bf16[768,1536]{1,0:T(8,128)(2,1)S(1)} %maximum_select_fusion.own_ref.up_own_ref) | copy-start | bytes 7077892
  120.8 8.9 %collective-permute-start.12 = (bf16[768,1536]{1,0:T(8,128)(2,1)S(1)}, bf16[768,1536]{1,0:T(8,128)(2,1)}, u32[]{:S(2)}, u32[]{:S(2)}) collective-permute-start(bf16[768,1536]{1,0:T(8,128)(2,1)S(1)} %maximum_select_fusion.own_ref.up_own_ref), channel_id=1, source_target_pairs={{0,8},{8,0},{16,24},{24,16},{1,9},{9,1},{17,25},{25,17},{2,10},{10... | collective-permute-start | bytes 7077896 | tf_op jit(solution)/shard_map/ppermute | solution.py:80
  151.2 4.7 %collective-permute-start.13 = (bf16[3072,384]{1,0:T(8,128)(2,1)}, bf16[3072,384]{1,0:T(8,128)(2,1)S(1)}, u32[]{:S(2)}, u32[]{:S(2)}) collective-permute-start(bf16[3072,384]{1,0:T(8,128)(2,1)} %all-gather.5.cloned.1.call-done.own_ref.down_own_ref), channel_id=1, source_target_pairs={{0,8},{8,0},{16,24},{24,16},{1,9},{9,1},{17,25},{25,17},{2,10},{10... | collective-permute-start | bytes 7077896 | tf_op jit(solution)/shard_map/ppermute | solution.py:80
  180.8 4.7 %collective-permute-start.14 = (bf16[3072,384]{1,0:T(8,128)(2,1)}, bf16[3072,384]{1,0:T(8,128)(2,1)S(1)}, u32[]{:S(2)}, u32[]{:S(2)}) collective-permute-start(bf16[3072,384]{1,0:T(8,128)(2,1)} %get-tuple-element.61), channel_id=1, source_target_pairs={{0,8},{8,0},{16,24},{24,16},{1,9},{9,1},{17,25},{25,17},{2,10},{10... | collective-permute-start | bytes 7077896 | tf_op jit(solution)/shard_map/ppermute | solution.py:80
  189.2 176.7 %reduce-scatter.3.cloned.1.call-start = ((), (), s32[]{:S(2)}) async-start(), calls=%async_computation.6 | async-start | bytes 3317760 | tf_op jit(solution)/shard_map/reduce_scatter | solution.py:826
  226.4 5.6 %collective-permute-start.15 = (bf16[768,1920]{1,0:T(8,128)(2,1)}, bf16[768,1920]{1,0:T(8,128)(2,1)S(1)}, u32[]{:S(2)}, u32[]{:S(2)}) collective-permute-start(bf16[768,1920]{1,0:T(8,128)(2,1)} %get-tuple-element.72), channel_id=1, source_target_pairs={{0,8},{8,0},{16,24},{24,16},{1,9},{9,1},{17,25},{25,17},{2,10},{10... | collective-permute-start | bytes 8847368 | tf_op jit(solution)/shard_map/ppermute | solution.py:80
  262.7 3.9 collective-permute-start.16
  271.3 10.0 %copy-start.7 = (f32[2,128,768]{2,1,0:T(8,128)S(1)}, f32[2,128,768]{2,1,0:T(8,128)}, u32[]{:S(2)}) copy-start(f32[2,128,768]{2,1,0:T(8,128)} %copy-done.6) | copy-start | bytes 2359300
  271.3 10.0 %copy-start.23 = (f32[768]{0:T(1024)S(1)}, f32[768]{0:T(1024)}, u32[]{:S(2)}) copy-start(f32[768]{0:T(1024)} %copy-done.22) | copy-start | bytes 9220
  271.3 10.0 %copy-start.25 = (f32[768]{0:T(1024)S(1)}, f32[768]{0:T(1024)}, u32[]{:S(2)}) copy-start(f32[768]{0:T(1024)} %copy-done.24) | copy-start | bytes 9220
  281.3 18.8 %copy-start.26 = (f32[768]{0:T(1024)S(1)}, f32[768]{0:T(1024)}, u32[]{:S(2)}) copy-start(f32[768]{0:T(1024)} %mul.216) | copy-start | bytes 9220
  281.3 18.8 %copy-start.30 = (f32[2,128]{1,0:T(2,128)S(1)}, f32[2,128]{1,0:T(2,128)}, u32[]{:S(2)}) copy-start(f32[2,128]{1,0:T(2,128)} %copy-done.29) | copy-start | bytes 3076
  285.6 15.9 %copy-start.16 = (bf16[2,128,768]{2,1,0:T(8,128)(2,1)S(1)}, bf16[2,128,768]{2,1,0:T(8,128)(2,1)}, u32[]{:S(2)}) copy-start(bf16[2,128,768]{2,1,0:T(8,128)(2,1)} %copy-done.15) | copy-start | bytes 1179652
  285.7 1.3 collective-permute-start.17
  287.0 3.1 collective-permute-start.18
  290.1 3.2 collective-permute-start.19
  293.3 3.2 collective-permute-start.20
  296.5 3.6 collective-permute-start.21
  296.6 25.2 %collective-permute-start.25 = (bf16[4,96,1152]{2,1,0:T(8,128)(2,1)}, bf16[4,96,1152]{2,1,0:T(8,128)(2,1)}, u32[]{:S(2)}, u32[]{:S(2)}) collective-permute-start(bf16[4,96,1152]{2,1,0:T(8,128)(2,1)} %dynamic-slice_bitcast_fusion), channel_id=1, source_target_pairs={{0,1},{1,0},{2,3},{3,2},{4,5},{5,4},{6,7},{7,6},{8,9},{9,8},{10,11... | collective-permute-start | bytes 2654216 | tf_op jit(solution)/shard_map/ppermute | solution.py:80
  297.8 65.5 %collective-permute-start.33 = (bf16[384,384]{1,0:T(8,128)(2,1)}, bf16[384,384]{1,0:T(8,128)(2,1)}, u32[]{:S(2)}, u32[]{:S(2)}) collective-permute-start(bf16[384,384]{1,0:T(8,128)(2,1)} %reduce-scatter.5.cloned.1.call-done), channel_id=1, source_target_pairs={{0,16},{8,24},{16,0},{24,8},{1,17},{9,25},{17,1},{25,9},{2,18},{10... | collective-permute-start | bytes 884744 | tf_op jit(solution)/shard_map/ppermute | solution.py:80
  301.6 4.1 %copy-start.12 = (bf16[8,96,384]{2,1,0:T(8,128)(2,1)S(1)}, bf16[8,96,384]{2,1,0:T(8,128)(2,1)}, u32[]{:S(2)}) copy-start(bf16[8,96,384]{2,1,0:T(8,128)(2,1)} %copy-done.11) | copy-start | bytes 1769476
  301.6 4.1 %copy-start.14 = (bf16[8,96,384]{2,1,0:T(8,128)(2,1)S(1)}, bf16[8,96,384]{2,1,0:T(8,128)(2,1)}, u32[]{:S(2)}) copy-start(bf16[8,96,384]{2,1,0:T(8,128)(2,1)} %copy-done.13) | copy-start | bytes 1769476
  301.6 4.1 %copy-start.33 = (f32[2,128]{1,0:T(2,128)S(1)}, f32[2,128]{1,0:T(2,128)}, u32[]{:S(2)}) copy-start(f32[2,128]{1,0:T(2,128)} %copy-done.32) | copy-start | bytes 3076
  302.2 23.6 %collective-permute-start.22 = (bf16[768,384]{1,0:T(8,128)(2,1)S(1)}, bf16[768,384]{1,0:T(8,128)(2,1)S(1)}, u32[]{:S(2)}, u32[]{:S(2)}) collective-permute-start(bf16[768,384]{1,0:T(8,128)(2,1)S(1)} %constant_dynamic-slice_fusion.1), channel_id=1, source_target_pairs={{0,8},{8,0},{16,24},{24,16},{1,9},{9,1},{17,25},{25,17},{2,10},{10... | collective-permute-start | bytes 1769480 | tf_op jit(solution)/shard_map/ppermute | solution.py:80
  323.3 12.4 %collective-permute-start.26 = (bf16[96,1152]{1,0:T(8,128)(2,1)S(1)}, bf16[96,1152]{1,0:T(8,128)(2,1)S(1)}, u32[]{:S(2)}, u32[]{:S(2)}) collective-permute-start(bf16[96,1152]{1,0:T(8,128)(2,1)S(1)} %get-tuple-element.120), channel_id=1, source_target_pairs={{0,2},{1,3},{2,4},{3,5},{4,6},{5,7},{6,0},{7,1},{8,10},{9,11},{10,... | collective-permute-start | bytes 663560 | tf_op jit(solution)/shard_map/ppermute | solution.py:160
  324.1 36.2 %collective-permute-start.27 = (bf16[96,1152]{1,0:T(8,128)(2,1)S(1)}, bf16[96,1152]{1,0:T(8,128)(2,1)S(1)}, u32[]{:S(2)}, u32[]{:S(2)}) collective-permute-start(bf16[96,1152]{1,0:T(8,128)(2,1)S(1)} %get-tuple-element.122), channel_id=1, source_target_pairs={{0,4},{1,5},{2,6},{3,7},{4,0},{5,1},{6,2},{7,3},{8,12},{9,13},{10,... | collective-permute-start | bytes 663560 | tf_op jit(solution)/shard_map/ppermute | solution.py:160
  325.8 37.5 %copy-start.18 = (bf16[384,384]{1,0:T(8,128)(2,1)S(1)}, bf16[384,384]{1,0:T(8,128)(2,1)}, u32[]{:S(2)}) copy-start(bf16[384,384]{1,0:T(8,128)(2,1)} %reduce-scatter.5.cloned.1.call-done) | copy-start | bytes 884740
  325.8 37.0 %collective-permute-start.28 = (bf16[96,1152]{1,0:T(8,128)(2,1)S(1)}, bf16[96,1152]{1,0:T(8,128)(2,1)S(1)}, u32[]{:S(2)}, u32[]{:S(2)}) collective-permute-start(bf16[96,1152]{1,0:T(8,128)(2,1)S(1)} %get-tuple-element.121), channel_id=1, source_target_pairs={{0,6},{1,7},{2,0},{3,1},{4,2},{5,3},{6,4},{7,5},{8,14},{9,15},{10,... | collective-permute-start | bytes 663560 | tf_op jit(solution)/shard_map/ppermute | solution.py:160
  326.8 47.6 %all-to-all-start.1 = ((bf16[8,96,384]{2,1,0:T(8,128)(2,1)}), bf16[8,96,384]{2,1,0:T(8,128)(2,1)S(1)}, u32[]{:S(2)}, u32[]{:S(2)}) async-start(bf16[8,96,384]{2,1,0:T(8,128)(2,1)} %bitcast.30), calls=%async_computation.1 | async-start | bytes 1179648 | tf_op jit(solution)/shard_map/all_to_all | solution.py:140
  362.9 5.9 %collective-permute-start.29 = (bf16[96,1152]{1,0:T(8,128)(2,1)S(1)}, bf16[96,1152]{1,0:T(8,128)(2,1)S(1)}, u32[]{:S(2)}, u32[]{:S(2)}) collective-permute-start(bf16[96,1152]{1,0:T(8,128)(2,1)S(1)} %fusion.13), channel_id=1, source_target_pairs={{0,16},{8,24},{16,0},{24,8},{1,17},{9,25},{17,1},{25,9},{2,18},{10... | collective-permute-start | bytes 663560 | tf_op jit(solution)/shard_map/ppermute | solution.py:80
  364.3 8.8 %collective-permute-start.34 = (bf16[384,384]{1,0:T(8,128)(2,1)S(1)}, bf16[384,384]{1,0:T(8,128)(2,1)S(1)}, u32[]{:S(2)}, u32[]{:S(2)}) collective-permute-start(bf16[384,384]{1,0:T(8,128)(2,1)S(1)} %add_convert_fusion.6), channel_id=1, source_target_pairs={{0,8},{8,0},{16,24},{24,16},{1,9},{9,1},{17,25},{25,17},{2,10},{10... | collective-permute-start | bytes 884744 | tf_op jit(solution)/shard_map/ppermute | solution.py:80
  365.8 10.9 %collective-permute-start.31 = (bf16[96,1920]{1,0:T(8,128)(2,1)}, bf16[96,1920]{1,0:T(8,128)(2,1)S(1)}, u32[]{:S(2)}, u32[]{:S(2)}) collective-permute-start(bf16[96,1920]{1,0:T(8,128)(2,1)} %reduce-scatter.3.cloned.1.call-done), channel_id=1, source_target_pairs={{0,16},{8,24},{16,0},{24,8},{1,17},{9,25},{17,1},{25,9},{2,18},{10... | collective-permute-start | bytes 1105928 | tf_op jit(solution)/shard_map/ppermute | solution.py:80
  368.9 7.8 %copy-start.17 = (bf16[96,1920]{1,0:T(8,128)(2,1)S(1)}, bf16[96,1920]{1,0:T(8,128)(2,1)}, u32[]{:S(2)}) copy-start(bf16[96,1920]{1,0:T(8,128)(2,1)} %reduce-scatter.3.cloned.1.call-done) | copy-start | bytes 1105924
  368.9 5.5 %collective-permute-start.30 = (bf16[96,1152]{1,0:T(8,128)(2,1)S(1)}, bf16[96,1152]{1,0:T(8,128)(2,1)S(1)}, u32[]{:S(2)}, u32[]{:S(2)}) collective-permute-start(bf16[96,1152]{1,0:T(8,128)(2,1)S(1)} %add_convert_fusion.7), channel_id=1, source_target_pairs={{0,8},{8,0},{16,24},{24,16},{1,9},{9,1},{17,25},{25,17},{2,10},{10... | collective-permute-start | bytes 663560 | tf_op jit(solution)/shard_map/ppermute | solution.py:80
  374.5 5.2 %collective-permute-start.23 = (bf16[96,384]{1,0:T(8,128)(2,1)S(1)}, bf16[96,384]{1,0:T(8,128)(2,1)S(1)}, u32[]{:S(2)}, u32[]{:S(2)}) collective-permute-start(bf16[96,384]{1,0:T(8,128)(2,1)S(1)} %reduce_sum.72), channel_id=1, source_target_pairs={{0,16},{8,24},{16,0},{24,8},{1,17},{9,25},{17,1},{25,9},{2,18},{10... | collective-permute-start | bytes 221192 | tf_op jit(solution)/shard_map/ppermute | solution.py:80
  376.8 5.9 %collective-permute-start.32 = (bf16[96,1920]{1,0:T(8,128)(2,1)S(1)}, bf16[96,1920]{1,0:T(8,128)(2,1)S(1)}, u32[]{:S(2)}, u32[]{:S(2)}) collective-permute-start(bf16[96,1920]{1,0:T(8,128)(2,1)S(1)} %add_convert_fusion.5), channel_id=1, source_target_pairs={{0,8},{8,0},{16,24},{24,16},{1,9},{9,1},{17,25},{25,17},{2,10},{10... | collective-permute-start | bytes 1105928 | tf_op jit(solution)/shard_map/ppermute | solution.py:80
  379.7 2.2 collective-permute-start.24
  (18 other events, 30.1 us)
Sparse Core Ops, SparseCore 0:
  10.9 70.1 all-gather.2
  83.8 50.6 all-gather.4
  189.3 65.7 reduce-scatter.4
  263.0 89.9 reduce-scatter.2

commit v5 on v4

--- a/solution.py
+++ b/solution.py
@@ -94,10 +94,7 @@
     around = [mine] + [
         lax.ppermute(mine, "fsdp", [(i, (i + 2 * step) % 8) for i in range(8)]) for step in (1, 2, 3)
     ]
-    column = jnp.zeros((4,) + mine.shape, mine.dtype)
-    for step in range(4):
-        column = lax.dynamic_update_index_in_dim(column, around[step], (line - step) % 4, 0)
-    return column
+    return jnp.stack([lax.select_n((line - row) % 4, *around) for row in range(4)])
 
 
 def gather_side(column):
@@ -133,11 +130,10 @@
     return total, swap(total, "dp", 1)
 
 
-def scatter_small(keep, give, core):
-    rows, half = keep.shape
+def scatter_small(chip, core):
+    rows, half = chip.shape
     fsdp = lax.axis_size("fsdp")
-    chip = add_low(keep, swap(give, "dp", 1)).reshape(fsdp, rows // fsdp, half)
-    parts = lax.all_to_all(chip, "fsdp", 0, 0)
+    parts = lax.all_to_all(chip.reshape(fsdp, rows // fsdp, half), "fsdp", 0, 0)
     return finish(jnp.sum(parts.astype(wide), axis=0).astype(low), core)
 
 
@@ -164,12 +160,11 @@
     return finish(total.astype(low), core)
 
 
-def sum_all(value):
-    for axis in ("dp", "fsdp"):
-        bit = 1
-        while bit < lax.axis_size(axis):
-            value = value + swap(value, axis, bit)
-            bit *= 2
+def sum_axis(value, axis):
+    bit = 1
+    while bit < lax.axis_size(axis):
+        value = value + swap(value, axis, bit)
+        bit *= 2
     return value
 
 
@@ -812,9 +807,7 @@
     down_halves = weight_columns(activated, branch_low[None], which)
     down_chip = add_low(down_halves[0], swap(down_halves[1], "dp", 1))
     down_chip, branch_low = lax.optimization_barrier((down_chip, branch_low))
-    down_shard = finish(
-        lax.psum_scatter(down_chip, "fsdp", scatter_dimension=0, tiled=True), core
-    )
+    down_sum = lax.psum_scatter(down_chip, "fsdp", scatter_dimension=0, tiled=True)
     delta_inner, delta_one, one_low, delta_attended, sums_one = inner_back(
         branch_low, delta_two, slope, total_one, vectors, attends, downs, ups, which
     )
@@ -822,18 +815,12 @@
     keep, give = weight_into(flat_attended, one_low, keep, give, which)
     chip = add_low(keep, swap(give, "dp", 1))
     chip, delta_attended = lax.optimization_barrier((chip, delta_attended))
-    up_merge_shard = finish(
-        lax.psum_scatter(chip, "fsdp", scatter_dimension=0, tiled=True), core
-    )
+    up_merge_sum = lax.psum_scatter(chip, "fsdp", scatter_dimension=0, tiled=True)
     delta_packed = attend_back(
         packed, share, delta_attended.reshape(docs, length, features), attended, which
     ).reshape(3, count, features)
-    keep, give = weight_columns(joined_low, delta_packed, which)
-    keep, give = scatter_begin(add_low(keep, swap(give, "dp", 1)))
-    give, delta_packed = lax.optimization_barrier((give, delta_packed))
-    given = swap(give, "fsdp", 1)
+    down_sum, delta_packed = lax.optimization_barrier((down_sum, delta_packed))
     delta_joined = joined_back(delta_one, delta_packed, *attends, which)
-    attend_shard = scatter_end(keep, given, core)
     delta_joined = delta_joined.reshape(docs, length, features)
     delta_embedded = jnp.einsum(
         "drs,drc->dsc",
@@ -852,7 +839,13 @@
             jnp.sum(delta_embedded, axis=(0, 1)),
         ]
     )
-    sums = sum_all(sums)
+    keep, give = weight_columns(joined_low, after(delta_packed, sums), which)
+    sums, give = lax.optimization_barrier((sum_axis(sums, "dp"), give))
+    sums = sum_axis(sums, "fsdp")
+    up_merge_shard = finish(after(up_merge_sum, sums), core)
+    down_shard = finish(after(down_sum, sums), core)
+    attend_keep, attend_give = scatter_begin(add_low(keep, swap(give, "dp", 1)))
+    attend_given = swap(attend_give, "fsdp", 1)
     gain_total, shift_total = sums[4], sums[5]
     visual_delta_rows = (
         valid_slot
@@ -863,7 +856,9 @@
     visual_local = jnp.einsum(
         "bli,blz->iz", pooled_segments, visual_delta_rows, preferred_element_type=wide
     ).astype(low)
-    visual_shard = scatter_small(half_of(visual_local, core), half_of(visual_local, 1 - core), core)
+    visual_chip = add_low(half_of(visual_local, core), swap(half_of(visual_local, 1 - core), "dp", 1))
+    visual_shard = scatter_small(visual_chip, core)
+    attend_shard = scatter_end(attend_keep, after(attend_given, visual_chip), core)
     delta_pooled = (
         jnp.einsum("zbl,wl->zbw", visual_delta_rows, full_visual, preferred_element_type=wide)
         / divisor

time: 398 us -> 398 us (level)
  the two profiles are of different devices: /device:TPU:11 before, /device:TPU:0 now
where the time goes in v5:
time: 398 us; the launch traced here: 391 us
  Pallas kernels  151 us (38%)
  waiting for transfers between devices  122 us (31%)
  starting transfers between devices  40.6 us (10%)
  other arithmetic  29.9 us (8%)
  local copies, waits for them, and re-layouts  20.4 us (5%)
  between operations  16 us (4%)
  matrix products  11 us (3%)
    ppermute x29, waiting for transfers between devices, swap(): return lax.ppermute(value, axis, [(i, i ^ bit) for i in range(size)])  68.3 us
    all_to_all x1, waiting for transfers between devices, spread(): return lax.all_to_all(copies, axis, 0, 0, axis_index_groups=groups)  23.9 us
    ppermute x29, starting transfers between devices, swap(): return lax.ppermute(value, axis, [(i, i ^ bit) for i in range(size)])  23.6 us
    pallas_call x1, Pallas kernels, inner_back(): call(inner_kernel, 'inner_back', (count // rows,), [block, block, tall, b...  23 us
    pallas_call x1, Pallas kernels, up(): call(up_kernel, 'up', (2, steps, count // rows), [pl.BlockSpec((rows, fea...  21.5 us
    pallas_call x1, Pallas kernels, attend_back(): call(attend_back_kernel, 'attend_back', (docs, pairs), [column_spec(lengt...  18.8 us
    ppermute x3, waiting for transfers between devices, scatter_end(): lax.ppermute(away, 'fsdp', [(i, (i + 2 * step) % (2 * lines)) for i in ra...  17.5 us
    pallas_call x2, Pallas kernels, weight_columns(): call(columns_kernel, 'weight_columns', (parts, steps), [pl.BlockSpec((cou...  17.1 us
  transfers between devices with their start and end apart: 41, of which 21 were waited for; matrix products, arithmetic and copies ran while one was open for 12% of the time, Pallas kernels for 33%

profile of v5, /device:TPU:0, one launch (start us, length us, event | category | flops | bytes accessed | tf_op | source)
XLA Modules:
  0.0 391.1 jit_solution(6892686902791316026)
XLA Ops:
  7.3 1.7 reshape.410
  12.0 7.3 %all-to-all-start = ((bf16[8,112,384]{2,1,0:T(8,128)(2,1)}), bf16[8,112,384]{2,1,0:T(8,128)(2,1)S(1)}, u32[]{:S(2)}, u32[]{:S(2)}) async-start(bf16[8,112,384]{2,1,0:T(8,128)(2,1)} %broadcast_in_dim.6), calls=%async_computation | async-start | bytes 1376256 | tf_op jit(solution)/shard_map/all_to_all | solution.py:75
  20.8 1.0 constant_dynamic-slice_fusion.5
  22.8 23.9 %all-to-all-done = bf16[8,112,384]{2,1,0:T(8,128)(2,1)S(1)} async-done(((bf16[8,112,384]{2,1,0:T(8,128)(2,1)}), bf16[8,112,384]{2,1,0:T(8,128)(2,1)S(1)}, u32[]{:S(2)}, u32[]{:S(2)}) %all-to-all-start) | async-done | bytes 688160 | tf_op jit(solution)/shard_map/all_to_all | solution.py:75
  47.5 1.2 collective-permute-start.8
  51.9 1.1 collective-permute-done.1
  53.6 1.6 collective-permute-start.2
  55.3 2.1 collective-permute-done.2
  58.0 1.6 collective-permute-start.3
  62.7 2.7 collective-permute-start.4
  65.4 9.7 %collective-permute-done.7 = bf16[96,768]{1,0:T(8,128)(2,1)S(1)} collective-permute-done((bf16[96,768]{1,0:T(8,128)(2,1)S(1)}, bf16[96,768]{1,0:T(8,128)(2,1)S(1)}, u32[]{:S(2)}, u32[]{:S(2)}) %collective-permute-start.7) | collective-permute-done | bytes 147488 | tf_op jit(solution)/shard_map/ppermute | solution.py:95
  75.8 2.9 collective-permute-start.5
  78.8 2.2 collective-permute-start.9
  81.6 1.6 all-gather.3.cloned.1.call-done.own_ref.merge_own_ref
  85.4 2.3 convert_add_fusion
  87.7 1.5 bitcast_convert_fusion.1.x_ref.left_ref
  89.9 2.0 collective-permute-done.9
  92.2 1.1 copy.44
  93.2 1.5 collective-permute-start.11
  95.3 1.4 copy-done.2
  96.8 9.7 %project.1 = bf16[1024,2304]{1,0:T(8,128)(2,1)} custom-call(s32[1]{0:T(128)} %bitcast.core_ref, bf16[1024,768]{1,0:T(8,128)(2,1)} %bitcast_convert_fusion.1.x_ref.left_ref, bf16[768,1536]{1,0:T(8,128)(2,1)} %all-gather.3.cloned.1.call-done.own_ref.merge_own_ref, bf16[768,1536]{1,0:T(8,128)(2,1)} %copy-done.2), custom_call_target="tpu_custom_call" | custom-call | tf_op jit(solution)/shard_map/project/pallas_call | solution.py:183
  106.5 15.9 %attend.1 = (bf16[2,512,768]{2,1,0:T(8,128)(2,1)}, bf16[2,12,512,512]{3,2,1,0:T(8,128)(2,1)}) custom-call(s32[1]{0:T(128)} %bitcast.core_ref, bf16[2,512,2304]{2,1,0:T(8,128)(2,1)} %bitcast.83, bf16[2,512,2304]{2,1,0:T(8,128)(2,1)} %bitcast.84, bf16[2,512,2304]{2,1,0:T(8,128)(2,1)} %bitcast.85, s32[2,1,512]{2,1,0:T(1,128)} %broadcast_in_dim.7.mask_ref), custom_call_target="tpu_custom_call" | custom-call | tf_op jit(solution)/shard_map/attend/pallas_call | solution.py:222
  122.4 2.9 maximum_select_fusion.own_ref.up_own_ref
  126.4 7.1 %merge.1 = (f32[1024,768]{1,0:T(8,128)}, bf16[1024,768]{1,0:T(8,128)(2,1)}) custom-call(s32[1]{0:T(128)} %bitcast.core_ref, bf16[1024,768]{1,0:T(8,128)(2,1)} %bitcast.96, f32[1024,768]{1,0:T(8,128)} %bitcast.93, f32[8,768]{1,0:T(8,128)} %pad.9.vectors_ref, bf16[768,1536]{1,0:T(8,128)(2,1)} %all-gather.3.cloned.1.call-done.own_ref.merge_own_ref, ...), custom_call_target="tpu_custom_call" | custom-call | tf_op jit(solution)/shard_map/merge/pallas_call | solution.py:381
  133.5 21.5 %up.1 = (bf16[1024,3072]{1,0:T(8,128)(2,1)}, bf16[1024,3072]{1,0:T(8,128)(2,1)}) custom-call(s32[1]{0:T(128)} %bitcast.core_ref, bf16[1024,768]{1,0:T(8,128)(2,1)} %get-tuple-element.57.x_ref.left_ref, bf16[768,1536]{1,0:T(8,128)(2,1)} %copy-done.5, bf16[768,1536]{1,0:T(8,128)(2,1)} %collective-permute-done.12.other_ref.up_other_ref), custom_call_target="tpu_custom_call" | custom-call | tf_op jit(solution)/shard_map/up/pallas_call | solution.py:320
  155.2 4.5 %collective-permute-done.13.other_ref.down_other_ref = bf16[3072,384]{1,0:T(8,128)(2,1)S(1)} collective-permute-done((bf16[3072,384]{1,0:T(8,128)(2,1)}, bf16[3072,384]{1,0:T(8,128)(2,1)S(1)}, u32[]{:S(2)}, u32[]{:S(2)}) %collective-permute-start.13) | collective-permute-done | bytes 2359328 | tf_op jit(solution)/shard_map/ppermute | solution.py:80
  159.8 1.4 copy-done.8
  161.2 14.2 %down.1 = (f32[1024,768]{1,0:T(8,128)}, f32[1024,768]{1,0:T(8,128)}, bf16[1024,768]{1,0:T(8,128)(2,1)}, f32[8,768]{1,0:T(8,128)}) custom-call(s32[1]{0:T(128)} %bitcast.core_ref, bf16[1024,3072]{1,0:T(8,128)(2,1)} %get-tuple-element.60.x_ref.left_ref, f32[1024,768]{1,0:T(8,128)} %get-tuple-element.61.sum_ref, bf16[1024,768]{1,0:T(8,128)(2,1)} %bitcast.105, ...), custom_call_target="tpu_custom_call" | custom-call | tf_op jit(solution)/shard_map/down/pallas_call | solution.py:438
  175.4 9.2 %weight_columns.2 = (bf16[3072,384]{1,0:T(8,128)(2,1)}, bf16[3072,384]{1,0:T(8,128)(2,1)}) custom-call(s32[1]{0:T(128)} %bitcast.core_ref, bf16[1024,3072]{1,0:T(8,128)(2,1)} %get-tuple-element.60.x_ref.left_ref, bf16[1,1024,768]{2,1,0:T(8,128)(2,1)} %bitcast.98, bf16[1,1024,768]{2,1,0:T(8,128)(2,1)} %bitcast.99), custom_call_target="tpu_custom_call" | custom-call | tf_op jit(solution)/shard_map/weight_columns/pallas_call | solution.py:597
  184.8 4.5 %collective-permute-done.14 = bf16[3072,384]{1,0:T(8,128)(2,1)S(1)} collective-permute-done((bf16[3072,384]{1,0:T(8,128)(2,1)}, bf16[3072,384]{1,0:T(8,128)(2,1)S(1)}, u32[]{:S(2)}, u32[]{:S(2)}) %collective-permute-start.14) | collective-permute-done | bytes 2359328 | tf_op jit(solution)/shard_map/ppermute | solution.py:80
  189.3 3.6 add_convert_fusion.1
  193.0 23.0 %inner_back.1 = (bf16[1024,3072]{1,0:T(8,128)(2,1)}, f32[1024,768]{1,0:T(8,128)}, bf16[1024,768]{1,0:T(8,128)(2,1)}, bf16[1024,768]{1,0:T(8,128)(2,1)}, f32[8,768]{1,0:T(8,128)}) custom-call(s32[1]{0:T(128)} %bitcast.core_ref, bf16[1024,768]{1,0:T(8,128)(2,1)} %get-tuple-element.68.low_ref, f32[1024,768]{1,0:T(8,128)} %get-tuple-element.69.delta_ref, ...), custom_call_target="tpu_custom_call" | custom-call | tf_op jit(solution)/shard_map/inner_back/pallas_call | solution.py:528
  216.0 10.0 %weight_wide.1 = (bf16[768,1920]{1,0:T(8,128)(2,1)}, bf16[768,1920]{1,0:T(8,128)(2,1)}) custom-call(s32[1]{0:T(128)} %bitcast.core_ref, bf16[1024,768]{1,0:T(8,128)(2,1)} %get-tuple-element.57.x_ref.left_ref, bf16[1024,3072]{1,0:T(8,128)(2,1)} %get-tuple-element.75.right_ref), custom_call_target="tpu_custom_call" | custom-call | tf_op jit(solution)/shard_map/weight_wide/pallas_call | solution.py:626
  226.0 4.4 %weight_into.1 = (bf16[768,1920]{1,0:T(8,128)(2,1)}, bf16[768,1920]{1,0:T(8,128)(2,1)}) custom-call(s32[1]{0:T(128)} %bitcast.core_ref, bf16[1024,768]{1,0:T(8,128)(2,1)} %bitcast.97, bf16[1024,768]{1,0:T(8,128)(2,1)} %get-tuple-element.74.own_ref.other_ref, ...), custom_call_target="tpu_custom_call", output_to_operand_aliasing={{0}: (4, {}), {1}: (5, {})} | custom-call | tf_op jit(solution)/shard_map/weight_into/pallas_call | solution.py:574
  232.2 3.8 collective-permute-done.15
  236.0 4.2 %add_convert_fusion = bf16[768,1920]{1,0:T(8,128)(2,1)} fusion(bf16[768,1920]{1,0:T(8,128)(2,1)S(1)} %collective-permute-done.15, bf16[768,1920]{1,0:T(8,128)(2,1)} %get-tuple-element.78), kind=kLoop, calls=%fused_computation | loop fusion | flops 5898240 | bytes 8847360 | tf_op jit(solution)/shard_map/convert_element_type | solution.py:122
  240.2 18.8 %attend_back.1 = bf16[3,2,512,768]{3,2,1,0:T(8,128)(2,1)} custom-call(s32[1]{0:T(128)} %bitcast.core_ref, bf16[2,512,2304]{2,1,0:T(8,128)(2,1)} %bitcast.86, bf16[2,512,2304]{2,1,0:T(8,128)(2,1)} %bitcast.87, bf16[2,512,2304]{2,1,0:T(8,128)(2,1)} %bitcast.88, bf16[2,12,512,512]{3,2,1,0:T(8,128)(2,1)} %get-tuple-element.73.share_ref, ...), custom_call_target="tpu_custom_call" | custom-call | tf_op jit(solution)/shard_map/attend_back/pallas_call | solution.py:268
  259.7 9.7 %joined_back.1 = f32[1024,768]{1,0:T(8,128)} custom-call(s32[1]{0:T(128)} %bitcast.core_ref, f32[1024,768]{1,0:T(8,128)} %get-tuple-element.71.one_ref, bf16[3,1024,768]{2,1,0:T(8,128)(2,1)} %bitcast.89, bf16[3,1024,768]{2,1,0:T(8,128)(2,1)} %bitcast.90, bf16[768,1536]{1,0:T(8,128)(2,1)} %all-gather.3.cloned.1.call-done.own_ref.merge_own_ref, ...), custom_call_target="tpu_custom_call" | custom-call | tf_op jit(solution)/shard_map/joined_back/pallas_call | solution.py:666
  269.4 3.4 multiply_reduce_fusion
  272.9 1.2 collective-permute-done.16
  274.1 1.6 collective-permute-start.17
  275.7 7.9 %weight_columns.3 = (bf16[768,1152]{1,0:T(8,128)(2,1)}, bf16[768,1152]{1,0:T(8,128)(2,1)}) custom-call(s32[1]{0:T(128)} %bitcast.core_ref, bf16[1024,768]{1,0:T(8,128)(2,1)} %bitcast_convert_fusion.1.x_ref.left_ref, bf16[3,1024,768]{2,1,0:T(8,128)(2,1)} %bitcast.91, bf16[3,1024,768]{2,1,0:T(8,128)(2,1)} %bitcast.92), custom_call_target="tpu_custom_call" | custom-call | tf_op jit(solution)/shard_map/weight_columns/pallas_call | solution.py:597
  284.7 3.1 collective-permute-done.18
  288.9 4.3 %collective-permute-done.19 = f32[6,768]{1,0:T(8,128)S(1)} collective-permute-done((f32[6,768]{1,0:T(8,128)S(1)}, f32[6,768]{1,0:T(8,128)S(1)}, u32[]{:S(2)}, u32[]{:S(2)}) %collective-permute-start.19) | collective-permute-done | bytes 18464 | tf_op jit(solution)/shard_map/ppermute | solution.py:80
  293.7 4.7 %collective-permute-done.20 = f32[6,768]{1,0:T(8,128)S(1)} collective-permute-done((f32[6,768]{1,0:T(8,128)S(1)}, f32[6,768]{1,0:T(8,128)S(1)}, u32[]{:S(2)}, u32[]{:S(2)}) %collective-permute-start.20) | collective-permute-done | bytes 18464 | tf_op jit(solution)/shard_map/ppermute | solution.py:80
  300.9 2.1 add_convert_fusion.2
  303.1 1.4 collective-permute-start.25
  304.6 3.2 convolution_add_fusion
  308.7 3.5 all-to-all-start.1
  313.7 23.3 %collective-permute-done.25 = bf16[4,96,1152]{2,1,0:T(8,128)(2,1)} collective-permute-done((bf16[4,96,1152]{2,1,0:T(8,128)(2,1)S(1)}, bf16[4,96,1152]{2,1,0:T(8,128)(2,1)}, u32[]{:S(2)}, u32[]{:S(2)}) %collective-permute-start.25) | collective-permute-done | bytes 884768 | tf_op jit(solution)/shard_map/ppermute | solution.py:80
  337.0 1.4 fusion
  339.2 3.2 collective-permute-start.28
  342.6 1.3 collective-permute-start.22
  343.9 4.9 %collective-permute-done.26 = bf16[96,1152]{1,0:T(8,128)(2,1)S(1)} collective-permute-done((bf16[96,1152]{1,0:T(8,128)(2,1)S(1)}, bf16[96,1152]{1,0:T(8,128)(2,1)S(1)}, u32[]{:S(2)}, u32[]{:S(2)}) %collective-permute-start.26) | collective-permute-done | bytes 221216 | tf_op jit(solution)/shard_map/ppermute | solution.py:156
  348.8 2.8 collective-permute-done.28
  351.5 9.9 %collective-permute-done.27 = bf16[96,1152]{1,0:T(8,128)(2,1)} collective-permute-done((bf16[96,1152]{1,0:T(8,128)(2,1)S(1)}, bf16[96,1152]{1,0:T(8,128)(2,1)}, u32[]{:S(2)}, u32[]{:S(2)}) %collective-permute-start.27) | collective-permute-done | bytes 221216 | tf_op jit(solution)/shard_map/ppermute | solution.py:156
  361.5 1.0 fusion.13
  362.5 1.5 collective-permute-start.29
  364.8 6.1 %collective-permute-done.29 = bf16[96,1152]{1,0:T(8,128)(2,1)S(1)} collective-permute-done((bf16[96,1152]{1,0:T(8,128)(2,1)S(1)}, bf16[96,1152]{1,0:T(8,128)(2,1)S(1)}, u32[]{:S(2)}, u32[]{:S(2)}) %collective-permute-start.29) | collective-permute-done | bytes 221216 | tf_op jit(solution)/shard_map/ppermute | solution.py:80
  371.1 6.4 %collective-permute-done.31 = bf16[96,1920]{1,0:T(8,128)(2,1)S(1)} collective-permute-done((bf16[96,1920]{1,0:T(8,128)(2,1)}, bf16[96,1920]{1,0:T(8,128)(2,1)S(1)}, u32[]{:S(2)}, u32[]{:S(2)}) %collective-permute-start.31) | collective-permute-done | bytes 368672 | tf_op jit(solution)/shard_map/ppermute | solution.py:80
  377.4 1.1 add_convert_fusion.5
  378.6 1.1 fusion.9
  381.1 1.1 copy.55
  383.0 1.2 fusion.8
  (214 shorter events, 33.5 us)
Async XLA Ops:
  7.2 14.7 %copy-start = (bf16[384,768]{1,0:T(8,128)(2,1)S(1)}, bf16[384,768]{1,0:T(8,128)(2,1)}, u32[]{:S(2)}) copy-start(bf16[384,768]{1,0:T(8,128)(2,1)} %param.25) | copy-start | bytes 1769476
  7.2 3.6 copy-start.35
  7.2 3.6 copy-start.34
  7.2 3.6 copy-start.33
  7.2 3.6 copy-start.32
  7.2 3.6 copy-start.37
  7.2 3.6 copy-start.36
  7.3 3.8 copy-start.26
  7.3 75.9 %all-gather.3.cloned.1.call-start = ((), (), s32[]{:S(2)}) async-start(), calls=%async_computation.4 | async-start | bytes 2654208 | tf_op jit(solution)/shard_map/all_gather | solution.py:110
  10.0 9.5 %copy-start.38 = (s32[2]{0:T(128)S(1)}, s32[2]{0:T(128)}, u32[]{:S(2)}) copy-start(s32[2]{0:T(128)} %param.28) | copy-start | bytes 28
  11.0 11.6 %copy-start.20 = (s32[2,512]{1,0:T(2,128)S(1)}, s32[2,512]{1,0:T(2,128)}, u32[]{:S(2)}) copy-start(s32[2,512]{1,0:T(2,128)} %param.29) | copy-start | bytes 12292
  11.1 35.8 %copy-start.10 = (bf16[2,512,768]{2,1,0:T(8,128)(2,1)S(1)}, bf16[2,512,768]{2,1,0:T(8,128)(2,1)}, u32[]{:S(2)}) copy-start(bf16[2,512,768]{2,1,0:T(8,128)(2,1)} %param.16) | copy-start | bytes 4718596
  12.0 34.8 %all-to-all-start = ((bf16[8,112,384]{2,1,0:T(8,128)(2,1)}), bf16[8,112,384]{2,1,0:T(8,128)(2,1)S(1)}, u32[]{:S(2)}, u32[]{:S(2)}) async-start(bf16[8,112,384]{2,1,0:T(8,128)(2,1)} %broadcast_in_dim.6), calls=%async_computation | async-start | bytes 1376256 | tf_op jit(solution)/shard_map/all_to_all | solution.py:75
  19.3 135.7 %all-gather.5.cloned.1.call-start = ((), (), s32[]{:S(2)}) async-start(), calls=%async_computation.5 | async-start | bytes 2654208 | tf_op jit(solution)/shard_map/all_gather | solution.py:110
  46.8 2.9 collective-permute-start
  46.9 3.8 copy-start.27
  47.5 17.9 %collective-permute-start.8 = (bf16[96,768]{1,0:T(8,128)(2,1)S(1)}, bf16[96,768]{1,0:T(8,128)(2,1)S(1)}, u32[]{:S(2)}, u32[]{:S(2)}) collective-permute-start(bf16[96,768]{1,0:T(8,128)(2,1)S(1)} %constant_dynamic-slice_fusion.5), channel_id=1, source_target_pairs={{0,6},{1,7},{2,0},{3,1},{4,2},{5,3},{6,4},{7,5},{8,14},{9,15},{10,... | collective-permute-start | bytes 442376 | tf_op jit(solution)/shard_map/ppermute | solution.py:95
  48.7 26.4 %collective-permute-start.7 = (bf16[96,768]{1,0:T(8,128)(2,1)S(1)}, bf16[96,768]{1,0:T(8,128)(2,1)S(1)}, u32[]{:S(2)}, u32[]{:S(2)}) collective-permute-start(bf16[96,768]{1,0:T(8,128)(2,1)S(1)} %constant_dynamic-slice_fusion.5), channel_id=1, source_target_pairs={{0,4},{1,5},{2,6},{3,7},{4,0},{5,1},{6,2},{7,3},{8,12},{9,13},{10,... | collective-permute-start | bytes 442376 | tf_op jit(solution)/shard_map/ppermute | solution.py:95
  49.5 25.6 %collective-permute-start.6 = (bf16[96,768]{1,0:T(8,128)(2,1)S(1)}, bf16[96,768]{1,0:T(8,128)(2,1)S(1)}, u32[]{:S(2)}, u32[]{:S(2)}) collective-permute-start(bf16[96,768]{1,0:T(8,128)(2,1)S(1)} %constant_dynamic-slice_fusion.5), channel_id=1, source_target_pairs={{0,2},{1,3},{2,4},{3,5},{4,6},{5,7},{6,0},{7,1},{8,10},{9,11},{10,... | collective-permute-start | bytes 442376 | tf_op jit(solution)/shard_map/ppermute | solution.py:95
  51.7 1.2 collective-permute-start.1
  53.6 3.8 collective-permute-start.2
  55.3 23.5 %copy-start.18 = (f32[8,6,96]{2,1,0:T(8,128)}, f32[8,6,96]{2,1,0:T(8,128)S(1)}, u32[]{:S(2)}) copy-start(f32[8,6,96]{2,1,0:T(8,128)S(1)} %reshape.426) | copy-start | bytes 55300
  58.0 4.0 %collective-permute-start.3 = (f32[3,768]{1,0:T(4,128)S(1)}, f32[3,768]{1,0:T(4,128)S(1)}, u32[]{:S(2)}, u32[]{:S(2)}) collective-permute-start(f32[3,768]{1,0:T(4,128)S(1)} %pad_maximum_fusion.6), channel_id=1, source_target_pairs={{0,1},{1,0},{2,3},{3,2},{4,5},{5,4},{6,7},{7,6},{8,9},{9,8},{10,11... | collective-permute-start | bytes 27656 | tf_op jit(solution)/shard_map/ppermute | solution.py:80
  61.0 198.6 %reduce-scatter.3.cloned.1.call-start = ((), (), s32[]{:S(2)}) async-start(), calls=%async_computation.6 | async-start | bytes 2654208 | tf_op jit(solution)/shard_map/reduce_scatter | solution.py:810
  62.7 12.5 %collective-permute-start.4 = (f32[3,768]{1,0:T(4,128)S(1)}, f32[3,768]{1,0:T(4,128)S(1)}, u32[]{:S(2)}, u32[]{:S(2)}) collective-permute-start(f32[3,768]{1,0:T(4,128)S(1)} %pad_maximum_fusion.7), channel_id=1, source_target_pairs={{0,2},{1,3},{2,0},{3,1},{4,6},{5,7},{6,4},{7,5},{8,10},{9,11},{10,... | collective-permute-start | bytes 27656 | tf_op jit(solution)/shard_map/ppermute | solution.py:80
  75.8 5.2 %collective-permute-start.5 = (f32[3,768]{1,0:T(4,128)S(1)}, f32[3,768]{1,0:T(4,128)S(1)}, u32[]{:S(2)}, u32[]{:S(2)}) collective-permute-start(f32[3,768]{1,0:T(4,128)S(1)} %pad_maximum_fusion.8), channel_id=1, source_target_pairs={{0,4},{1,5},{2,6},{3,7},{4,0},{5,1},{6,2},{7,3},{8,12},{9,13},{10,... | collective-permute-start | bytes 27656 | tf_op jit(solution)/shard_map/ppermute | solution.py:80
  78.8 13.1 %collective-permute-start.9 = (bf16[4,96,768]{2,1,0:T(8,128)(2,1)S(1)}, bf16[4,96,768]{2,1,0:T(8,128)(2,1)S(1)}, u32[]{:S(2)}, u32[]{:S(2)}) collective-permute-start(bf16[4,96,768]{2,1,0:T(8,128)(2,1)S(1)} %pad_maximum_fusion), channel_id=1, source_target_pairs={{0,1},{1,0},{2,3},{3,2},{4,5},{5,4},{6,7},{7,6},{8,9},{9,8},{10,11... | collective-permute-start | bytes 1769480 | tf_op jit(solution)/shard_map/ppermute | solution.py:80
  83.2 12.1 %collective-permute-start.10 = (bf16[768,1536]{1,0:T(8,128)(2,1)}, bf16[768,1536]{1,0:T(8,128)(2,1)S(1)}, u32[]{:S(2)}, u32[]{:S(2)}) collective-permute-start(bf16[768,1536]{1,0:T(8,128)(2,1)} %all-gather.3.cloned.1.call-done.own_ref.merge_own_ref), channel_id=1, source_target_pairs={{0,8},{8,0},{16,24},{24,16},{1,9},{9,1},{17,25},{25,17},{2,10},{10... | collective-permute-start | bytes 7077896 | tf_op jit(solution)/shard_map/ppermute | solution.py:80
  93.2 29.1 %collective-permute-start.11 = (bf16[768,768]{1,0:T(8,128)(2,1)}, bf16[768,768]{1,0:T(8,128)(2,1)}, u32[]{:S(2)}, u32[]{:S(2)}) collective-permute-start(bf16[768,768]{1,0:T(8,128)(2,1)} %bitcast.18), channel_id=1, source_target_pairs={{0,16},{8,24},{16,0},{24,8},{1,17},{9,25},{17,1},{25,9},{2,18},{10... | collective-permute-start | bytes 3538952 | tf_op jit(solution)/shard_map/ppermute | solution.py:80
  122.4 3.1 copy-start.19
  125.4 8.1 %copy-start.5 = (bf16[768,1536]{1,0:T(8,128)(2,1)}, bf16[768,1536]{1,0:T(8,128)(2,1)S(1)}, u32[]{:S(2)}) copy-start(bf16[768,1536]{1,0:T(8,128)(2,1)S(1)} %maximum_select_fusion.own_ref.up_own_ref) | copy-start | bytes 7077892
  125.4 8.1 %collective-permute-start.12 = (bf16[768,1536]{1,0:T(8,128)(2,1)S(1)}, bf16[768,1536]{1,0:T(8,128)(2,1)}, u32[]{:S(2)}, u32[]{:S(2)}) collective-permute-start(bf16[768,1536]{1,0:T(8,128)(2,1)S(1)} %maximum_select_fusion.own_ref.up_own_ref), channel_id=1, source_target_pairs={{0,8},{8,0},{16,24},{24,16},{1,9},{9,1},{17,25},{25,17},{2,10},{10... | collective-permute-start | bytes 7077896 | tf_op jit(solution)/shard_map/ppermute | solution.py:80
  155.0 4.7 %collective-permute-start.13 = (bf16[3072,384]{1,0:T(8,128)(2,1)}, bf16[3072,384]{1,0:T(8,128)(2,1)S(1)}, u32[]{:S(2)}, u32[]{:S(2)}) collective-permute-start(bf16[3072,384]{1,0:T(8,128)(2,1)} %all-gather.5.cloned.1.call-done.own_ref.down_own_ref), channel_id=1, source_target_pairs={{0,8},{8,0},{16,24},{24,16},{1,9},{9,1},{17,25},{25,17},{2,10},{10... | collective-permute-start | bytes 7077896 | tf_op jit(solution)/shard_map/ppermute | solution.py:80
  184.6 4.7 %collective-permute-start.14 = (bf16[3072,384]{1,0:T(8,128)(2,1)}, bf16[3072,384]{1,0:T(8,128)(2,1)S(1)}, u32[]{:S(2)}, u32[]{:S(2)}) collective-permute-start(bf16[3072,384]{1,0:T(8,128)(2,1)} %get-tuple-element.67), channel_id=1, source_target_pairs={{0,8},{8,0},{16,24},{24,16},{1,9},{9,1},{17,25},{25,17},{2,10},{10... | collective-permute-start | bytes 7077896 | tf_op jit(solution)/shard_map/ppermute | solution.py:80
  193.0 171.1 %reduce-scatter.5.cloned.1.call-start = ((), (), s32[]{:S(2)}) async-start(), calls=%async_computation.7 | async-start | bytes 3317760 | tf_op jit(solution)/shard_map/reduce_scatter | solution.py:818
  230.4 5.6 %collective-permute-start.15 = (bf16[768,1920]{1,0:T(8,128)(2,1)}, bf16[768,1920]{1,0:T(8,128)(2,1)S(1)}, u32[]{:S(2)}, u32[]{:S(2)}) collective-permute-start(bf16[768,1920]{1,0:T(8,128)(2,1)} %get-tuple-element.79), channel_id=1, source_target_pairs={{0,8},{8,0},{16,24},{24,16},{1,9},{9,1},{17,25},{25,17},{2,10},{10... | collective-permute-start | bytes 8847368 | tf_op jit(solution)/shard_map/ppermute | solution.py:80
  259.6 9.7 %copy-start.7 = (f32[2,128,768]{2,1,0:T(8,128)S(1)}, f32[2,128,768]{2,1,0:T(8,128)}, u32[]{:S(2)}) copy-start(f32[2,128,768]{2,1,0:T(8,128)} %copy-done.6) | copy-start | bytes 2359300
  259.6 9.7 %copy-start.22 = (f32[768]{0:T(1024)S(1)}, f32[768]{0:T(1024)}, u32[]{:S(2)}) copy-start(f32[768]{0:T(1024)} %copy-done.21) | copy-start | bytes 9220
  259.7 9.7 %copy-start.24 = (f32[768]{0:T(1024)S(1)}, f32[768]{0:T(1024)}, u32[]{:S(2)}) copy-start(f32[768]{0:T(1024)} %copy-done.23) | copy-start | bytes 9220
  272.8 1.3 collective-permute-start.16
  274.1 24.3 %copy-start.25 = (f32[768]{0:T(1024)S(1)}, f32[768]{0:T(1024)}, u32[]{:S(2)}) copy-start(f32[768]{0:T(1024)} %mul.216) | copy-start | bytes 9220
  274.1 24.3 %copy-start.28 = (f32[2,128]{1,0:T(2,128)S(1)}, f32[2,128]{1,0:T(2,128)}, u32[]{:S(2)}) copy-start(f32[2,128]{1,0:T(2,128)} %copy-done.27) | copy-start | bytes 3076
  274.1 9.5 %collective-permute-start.17 = (f32[6,768]{1,0:T(8,128)S(1)}, f32[6,768]{1,0:T(8,128)S(1)}, u32[]{:S(2)}, u32[]{:S(2)}) collective-permute-start(f32[6,768]{1,0:T(8,128)S(1)} %fusion.30), channel_id=1, source_target_pairs={{0,16},{8,24},{16,0},{24,8},{1,17},{9,25},{17,1},{25,9},{2,18},{10... | collective-permute-start | bytes 55304 | tf_op jit(solution)/shard_map/ppermute | solution.py:80
  283.6 15.1 %copy-start.16 = (bf16[2,128,768]{2,1,0:T(8,128)(2,1)S(1)}, bf16[2,128,768]{2,1,0:T(8,128)(2,1)}, u32[]{:S(2)}) copy-start(bf16[2,128,768]{2,1,0:T(8,128)(2,1)} %copy-done.15) | copy-start | bytes 1179652
  283.7 16.9 %collective-permute-start.24 = (bf16[768,1152]{1,0:T(8,128)(2,1)}, bf16[768,1152]{1,0:T(8,128)(2,1)}, u32[]{:S(2)}, u32[]{:S(2)}) collective-permute-start(bf16[768,1152]{1,0:T(8,128)(2,1)} %get-tuple-element.89), channel_id=1, source_target_pairs={{0,8},{8,0},{16,24},{24,16},{1,9},{9,1},{17,25},{25,17},{2,10},{10... | collective-permute-start | bytes 5308424 | tf_op jit(solution)/shard_map/ppermute | solution.py:80
  283.7 4.1 %collective-permute-start.18 = (f32[6,768]{1,0:T(8,128)S(1)}, f32[6,768]{1,0:T(8,128)S(1)}, u32[]{:S(2)}, u32[]{:S(2)}) collective-permute-start(f32[6,768]{1,0:T(8,128)S(1)} %add.582), channel_id=1, source_target_pairs={{0,1},{1,0},{2,3},{3,2},{4,5},{5,4},{6,7},{7,6},{8,9},{9,8},{10,11... | collective-permute-start | bytes 55304 | tf_op jit(solution)/shard_map/ppermute | solution.py:80
  287.9 5.3 %collective-permute-start.19 = (f32[6,768]{1,0:T(8,128)S(1)}, f32[6,768]{1,0:T(8,128)S(1)}, u32[]{:S(2)}, u32[]{:S(2)}) collective-permute-start(f32[6,768]{1,0:T(8,128)S(1)} %add.583), channel_id=1, source_target_pairs={{0,2},{1,3},{2,0},{3,1},{4,6},{5,7},{6,4},{7,5},{8,10},{9,11},{10,... | collective-permute-start | bytes 55304 | tf_op jit(solution)/shard_map/ppermute | solution.py:80
  293.2 5.2 %collective-permute-start.20 = (f32[6,768]{1,0:T(8,128)S(1)}, f32[6,768]{1,0:T(8,128)S(1)}, u32[]{:S(2)}, u32[]{:S(2)}) collective-permute-start(f32[6,768]{1,0:T(8,128)S(1)} %add.584), channel_id=1, source_target_pairs={{0,4},{1,5},{2,6},{3,7},{4,0},{5,1},{6,2},{7,3},{8,12},{9,13},{10,... | collective-permute-start | bytes 55304 | tf_op jit(solution)/shard_map/ppermute | solution.py:80
  299.4 8.4 %collective-permute-start.21 = (bf16[768,384]{1,0:T(8,128)(2,1)S(1)}, bf16[768,384]{1,0:T(8,128)(2,1)S(1)}, u32[]{:S(2)}, u32[]{:S(2)}) collective-permute-start(bf16[768,384]{1,0:T(8,128)(2,1)S(1)} %constant_dynamic-slice_fusion.1), channel_id=1, source_target_pairs={{0,8},{8,0},{16,24},{24,16},{1,9},{9,1},{17,25},{25,17},{2,10},{10... | collective-permute-start | bytes 1769480 | tf_op jit(solution)/shard_map/ppermute | solution.py:80
  300.9 3.6 copy-start.4
  303.1 33.9 %collective-permute-start.25 = (bf16[4,96,1152]{2,1,0:T(8,128)(2,1)S(1)}, bf16[4,96,1152]{2,1,0:T(8,128)(2,1)}, u32[]{:S(2)}, u32[]{:S(2)}) collective-permute-start(bf16[4,96,1152]{2,1,0:T(8,128)(2,1)S(1)} %dynamic-slice_bitcast_fusion), channel_id=1, source_target_pairs={{0,1},{1,0},{2,3},{3,2},{4,5},{5,4},{6,7},{7,6},{8,9},{9,8},{10,11... | collective-permute-start | bytes 2654216 | tf_op jit(solution)/shard_map/ppermute | solution.py:80
  307.8 5.1 %copy-start.17 = (bf16[384,384]{1,0:T(8,128)(2,1)S(1)}, bf16[384,384]{1,0:T(8,128)(2,1)}, u32[]{:S(2)}) copy-start(bf16[384,384]{1,0:T(8,128)(2,1)} %reduce-scatter.3.cloned.1.call-done) | copy-start | bytes 884740
  308.7 33.8 %all-to-all-start.1 = ((bf16[8,96,384]{2,1,0:T(8,128)(2,1)}), bf16[8,96,384]{2,1,0:T(8,128)(2,1)S(1)}, u32[]{:S(2)}, u32[]{:S(2)}) async-start(bf16[8,96,384]{2,1,0:T(8,128)(2,1)} %bitcast.28), calls=%async_computation.2 | async-start | bytes 1179648 | tf_op jit(solution)/shard_map/all_to_all | solution.py:136
  312.8 29.5 %collective-permute-start.33 = (bf16[384,384]{1,0:T(8,128)(2,1)S(1)}, bf16[384,384]{1,0:T(8,128)(2,1)S(1)}, u32[]{:S(2)}, u32[]{:S(2)}) collective-permute-start(bf16[384,384]{1,0:T(8,128)(2,1)S(1)} %copy-done.17), channel_id=1, source_target_pairs={{0,16},{8,24},{16,0},{24,8},{1,17},{9,25},{17,1},{25,9},{2,18},{10... | collective-permute-start | bytes 884744 | tf_op jit(solution)/shard_map/ppermute | solution.py:80
  338.5 10.3 %collective-permute-start.26 = (bf16[96,1152]{1,0:T(8,128)(2,1)S(1)}, bf16[96,1152]{1,0:T(8,128)(2,1)S(1)}, u32[]{:S(2)}, u32[]{:S(2)}) collective-permute-start(bf16[96,1152]{1,0:T(8,128)(2,1)S(1)} %get-tuple-element.132), channel_id=1, source_target_pairs={{0,2},{1,3},{2,4},{3,5},{4,6},{5,7},{6,0},{7,1},{8,10},{9,11},{10,... | collective-permute-start | bytes 663560 | tf_op jit(solution)/shard_map/ppermute | solution.py:156
  339.2 12.3 %collective-permute-start.28 = (bf16[96,1152]{1,0:T(8,128)(2,1)S(1)}, bf16[96,1152]{1,0:T(8,128)(2,1)S(1)}, u32[]{:S(2)}, u32[]{:S(2)}) collective-permute-start(bf16[96,1152]{1,0:T(8,128)(2,1)S(1)} %get-tuple-element.133), channel_id=1, source_target_pairs={{0,6},{1,7},{2,0},{3,1},{4,2},{5,3},{6,4},{7,5},{8,14},{9,15},{10,... | collective-permute-start | bytes 663560 | tf_op jit(solution)/shard_map/ppermute | solution.py:156
  342.4 19.1 %collective-permute-start.27 = (bf16[96,1152]{1,0:T(8,128)(2,1)S(1)}, bf16[96,1152]{1,0:T(8,128)(2,1)}, u32[]{:S(2)}, u32[]{:S(2)}) collective-permute-start(bf16[96,1152]{1,0:T(8,128)(2,1)S(1)} %get-tuple-element.134), channel_id=1, source_target_pairs={{0,4},{1,5},{2,6},{3,7},{4,0},{5,1},{6,2},{7,3},{8,12},{9,13},{10,... | collective-permute-start | bytes 663560 | tf_op jit(solution)/shard_map/ppermute | solution.py:156
  342.5 36.2 %collective-permute-start.34 = (bf16[384,384]{1,0:T(8,128)(2,1)S(1)}, bf16[384,384]{1,0:T(8,128)(2,1)S(1)}, u32[]{:S(2)}, u32[]{:S(2)}) collective-permute-start(bf16[384,384]{1,0:T(8,128)(2,1)S(1)} %add_convert_fusion.6), channel_id=1, source_target_pairs={{0,8},{8,0},{16,24},{24,16},{1,9},{9,1},{17,25},{25,17},{2,10},{10... | collective-permute-start | bytes 884744 | tf_op jit(solution)/shard_map/ppermute | solution.py:80
  342.6 21.4 %collective-permute-start.22 = (bf16[96,384]{1,0:T(8,128)(2,1)S(1)}, bf16[96,384]{1,0:T(8,128)(2,1)S(1)}, u32[]{:S(2)}, u32[]{:S(2)}) collective-permute-start(bf16[96,384]{1,0:T(8,128)(2,1)S(1)} %reduce_sum.72), channel_id=1, source_target_pairs={{0,16},{8,24},{16,0},{24,8},{1,17},{9,25},{17,1},{25,9},{2,18},{10... | collective-permute-start | bytes 221192 | tf_op jit(solution)/shard_map/ppermute | solution.py:80
  362.5 8.4 %collective-permute-start.29 = (bf16[96,1152]{1,0:T(8,128)(2,1)S(1)}, bf16[96,1152]{1,0:T(8,128)(2,1)S(1)}, u32[]{:S(2)}, u32[]{:S(2)}) collective-permute-start(bf16[96,1152]{1,0:T(8,128)(2,1)S(1)} %fusion.13), channel_id=1, source_target_pairs={{0,16},{8,24},{16,0},{24,8},{1,17},{9,25},{17,1},{25,9},{2,18},{10... | collective-permute-start | bytes 663560 | tf_op jit(solution)/shard_map/ppermute | solution.py:80
  364.0 15.7 %collective-permute-start.23 = (bf16[96,384]{1,0:T(8,128)(2,1)S(1)}, bf16[96,384]{1,0:T(8,128)(2,1)S(1)}, u32[]{:S(2)}, u32[]{:S(2)}) collective-permute-start(bf16[96,384]{1,0:T(8,128)(2,1)S(1)} %add_convert_fusion.9), channel_id=1, source_target_pairs={{0,8},{8,0},{16,24},{24,16},{1,9},{9,1},{17,25},{25,17},{2,10},{10... | collective-permute-start | bytes 221192 | tf_op jit(solution)/shard_map/ppermute | solution.py:80
  364.1 13.3 %collective-permute-start.31 = (bf16[96,1920]{1,0:T(8,128)(2,1)}, bf16[96,1920]{1,0:T(8,128)(2,1)S(1)}, u32[]{:S(2)}, u32[]{:S(2)}) collective-permute-start(bf16[96,1920]{1,0:T(8,128)(2,1)} %reduce-scatter.5.cloned.1.call-done), channel_id=1, source_target_pairs={{0,16},{8,24},{16,0},{24,8},{1,17},{9,25},{17,1},{25,9},{2,18},{10... | collective-permute-start | bytes 1105928 | tf_op jit(solution)/shard_map/ppermute | solution.py:80
  371.0 9.6 %collective-permute-start.30 = (bf16[96,1152]{1,0:T(8,128)(2,1)S(1)}, bf16[96,1152]{1,0:T(8,128)(2,1)S(1)}, u32[]{:S(2)}, u32[]{:S(2)}) collective-permute-start(bf16[96,1152]{1,0:T(8,128)(2,1)S(1)} %add_convert_fusion.7), channel_id=1, source_target_pairs={{0,8},{8,0},{16,24},{24,16},{1,9},{9,1},{17,25},{25,17},{2,10},{10... | collective-permute-start | bytes 663560 | tf_op jit(solution)/shard_map/ppermute | solution.py:80
  378.5 3.6 collective-permute-start.32
  (16 other events, 22.2 us)
Sparse Core Ops, SparseCore 0:
  10.9 72.2 all-gather.2
  86.0 52.1 all-gather.4
  193.1 66.4 reduce-scatter.2
  263.1 81.4 reduce-scatter.4

commit v6 on v4

--- a/solution.py
+++ b/solution.py
@@ -298,13 +298,11 @@
     return value * below, below + value * (bell * 0.3989422804014327)
 
 
-def up_kernel(core_ref, x_ref, own_ref, other_ref, out_ref, slope_ref, inner, chunk=16):
+def up_kernel(core_ref, x_ref, own_ref, other_ref, out_ref, slope_ref):
     def block(weight):
-        inner[...] = dot(x_ref[...], weight)
-        for row in range(0, inner.shape[0], chunk):
-            value, slope = gelu_parts(inner[row : row + chunk])
-            out_ref[row : row + chunk] = value.astype(low)
-            slope_ref[row : row + chunk] = slope.astype(low)
+        value, slope = gelu_parts(dot(x_ref[...], weight))
+        out_ref[...] = value.astype(low)
+        slope_ref[...] = slope.astype(low)
 
     @pl.when(pl.program_id(0) == 0)
     def _():
@@ -315,7 +313,7 @@
         block(other_ref[...])
 
 
-def up(x, own, other, core, columns=768, rows=512):
+def up(x, own, other, core, columns=512, rows=512):
     count, features = x.shape
     half = own.shape[1]
     steps = half // columns
@@ -333,7 +331,6 @@
         ],
         [out, out],
         [shape((count, 2 * half))] * 2,
-        [pltpu.VMEM((rows, columns), wide)],
     )(core, x, own, other)
 
 

time: 398 us -> 395 us (level)
  the two profiles are of different devices: /device:TPU:11 before, /device:TPU:0 now
where the time goes in v6:
time: 395 us; the launch traced here: 388 us
  Pallas kernels  152 us (38%)
  waiting for transfers between devices  114 us (29%)
  starting transfers between devices  42 us (11%)
  other arithmetic  31.1 us (8%)
  local copies, waits for them, and re-layouts  21.7 us (5%)
  between operations  15.5 us (4%)
  matrix products  12 us (3%)
    ppermute x29, waiting for transfers between devices, swap(): return lax.ppermute(value, axis, [(i, i ^ bit) for i in range(size)])  55.8 us
    all_to_all x1, waiting for transfers between devices, spread(): return lax.all_to_all(copies, axis, 0, 0, axis_index_groups=groups)  24.7 us
    pallas_call x1, Pallas kernels, up(): call(up_kernel, 'up', (2, steps, count // rows), [pl.BlockSpec((rows, fea...  22.9 us
    pallas_call x1, Pallas kernels, inner_back(): call(inner_kernel, 'inner_back', (count // rows,), [block, block, tall, b...  22.8 us
    ppermute x29, starting transfers between devices, swap(): return lax.ppermute(value, axis, [(i, i ^ bit) for i in range(size)])  21.8 us
    pallas_call x1, Pallas kernels, attend_back(): call(attend_back_kernel, 'attend_back', (docs, pairs), [column_spec(lengt...  18.9 us
    ppermute x3, waiting for transfers between devices, scatter_end(): lax.ppermute(away, 'fsdp', [(i, (i + 2 * step) % (2 * lines)) for i in ra...  18.1 us
    pallas_call x2, Pallas kernels, weight_columns(): call(columns_kernel, 'weight_columns', (parts, steps), [pl.BlockSpec((cou...  16.8 us
  transfers between devices with their start and end apart: 41, of which 23 were waited for; matrix products, arithmetic and copies ran while one was open for 12% of the time, Pallas kernels for 33%

profile of v6, /device:TPU:0, one launch (start us, length us, event | category | flops | bytes accessed | tf_op | source)
XLA Modules:
  0.0 388.1 jit_solution(658077824399762058)
XLA Ops:
  7.3 1.7 reshape.410
  11.2 7.3 %all-to-all-start = ((bf16[8,112,384]{2,1,0:T(8,128)(2,1)}), bf16[8,112,384]{2,1,0:T(8,128)(2,1)S(1)}, u32[]{:S(2)}, u32[]{:S(2)}) async-start(bf16[8,112,384]{2,1,0:T(8,128)(2,1)} %broadcast_in_dim.39), calls=%async_computation | async-start | bytes 1376256 | tf_op jit(solution)/shard_map/all_to_all | solution.py:75
  21.3 24.7 %all-to-all-done = bf16[8,112,384]{2,1,0:T(8,128)(2,1)S(1)} async-done(((bf16[8,112,384]{2,1,0:T(8,128)(2,1)}), bf16[8,112,384]{2,1,0:T(8,128)(2,1)S(1)}, u32[]{:S(2)}, u32[]{:S(2)}) %all-to-all-start) | async-done | bytes 688160 | tf_op jit(solution)/shard_map/all_to_all | solution.py:75
  47.7 1.4 collective-permute-start.7
  49.1 2.1 collective-permute-start.8
  55.3 1.6 collective-permute-start.2
  59.7 1.5 collective-permute-start.3
  61.3 2.4 collective-permute-done.3
  65.0 3.6 collective-permute-done.7
  69.7 2.9 collective-permute-start.5
  72.6 1.5 collective-permute-start.9
  74.1 6.1 %collective-permute-done.5 = f32[3,768]{1,0:T(4,128)S(1)} collective-permute-done((f32[3,768]{1,0:T(4,128)S(1)}, f32[3,768]{1,0:T(4,128)S(1)}, u32[]{:S(2)}, u32[]{:S(2)}) %collective-permute-start.5) | collective-permute-done | bytes 9248 | tf_op jit(solution)/shard_map/ppermute | solution.py:80
  80.8 3.3 all-gather.3.cloned.1.call-done.own_ref.merge_own_ref
  86.3 2.3 convert_add_fusion
  88.6 1.5 bitcast_convert_fusion.1.x_ref.left_ref
  91.9 1.5 collective-permute-start.11
  94.0 1.4 copy-done.2
  95.5 9.5 %project.1 = bf16[1024,2304]{1,0:T(8,128)(2,1)} custom-call(s32[1]{0:T(128)} %bitcast.core_ref, bf16[1024,768]{1,0:T(8,128)(2,1)} %bitcast_convert_fusion.1.x_ref.left_ref, bf16[768,1536]{1,0:T(8,128)(2,1)} %all-gather.3.cloned.1.call-done.own_ref.merge_own_ref, bf16[768,1536]{1,0:T(8,128)(2,1)} %copy-done.2), custom_call_target="tpu_custom_call" | custom-call | tf_op jit(solution)/shard_map/project/pallas_call | solution.py:188
  105.0 15.9 %attend.1 = (bf16[2,512,768]{2,1,0:T(8,128)(2,1)}, bf16[2,12,512,512]{3,2,1,0:T(8,128)(2,1)}) custom-call(s32[1]{0:T(128)} %bitcast.core_ref, bf16[2,512,2304]{2,1,0:T(8,128)(2,1)} %bitcast.83, bf16[2,512,2304]{2,1,0:T(8,128)(2,1)} %bitcast.84, bf16[2,512,2304]{2,1,0:T(8,128)(2,1)} %bitcast.85, s32[2,1,512]{2,1,0:T(1,128)} %broadcast_in_dim.45.mask_ref), custom_call_target="tpu_custom_call" | custom-call | tf_op jit(solution)/shard_map/attend/pallas_call | solution.py:227
  120.8 2.9 maximum_select_fusion.own_ref.up_own_ref
  125.1 7.1 %merge.1 = (f32[1024,768]{1,0:T(8,128)}, bf16[1024,768]{1,0:T(8,128)(2,1)}) custom-call(s32[1]{0:T(128)} %bitcast.core_ref, bf16[1024,768]{1,0:T(8,128)(2,1)} %bitcast.96, f32[1024,768]{1,0:T(8,128)} %bitcast.93, f32[8,768]{1,0:T(8,128)} %pad.9.vectors_ref, bf16[768,1536]{1,0:T(8,128)(2,1)} %all-gather.3.cloned.1.call-done.own_ref.merge_own_ref, ...), custom_call_target="tpu_custom_call" | custom-call | tf_op jit(solution)/shard_map/merge/pallas_call | solution.py:383
  132.2 22.9 %up.1 = (bf16[1024,3072]{1,0:T(8,128)(2,1)}, bf16[1024,3072]{1,0:T(8,128)(2,1)}) custom-call(s32[1]{0:T(128)} %bitcast.core_ref, bf16[1024,768]{1,0:T(8,128)(2,1)} %get-tuple-element.51.x_ref.left_ref, bf16[768,1536]{1,0:T(8,128)(2,1)} %copy-done.5, bf16[768,1536]{1,0:T(8,128)(2,1)} %collective-permute-done.12.other_ref.up_other_ref), custom_call_target="tpu_custom_call" | custom-call | tf_op jit(solution)/shard_map/up/pallas_call | solution.py:323
  155.3 4.5 %collective-permute-done.13.other_ref.down_other_ref = bf16[3072,384]{1,0:T(8,128)(2,1)S(1)} collective-permute-done((bf16[3072,384]{1,0:T(8,128)(2,1)}, bf16[3072,384]{1,0:T(8,128)(2,1)S(1)}, u32[]{:S(2)}, u32[]{:S(2)}) %collective-permute-start.13) | collective-permute-done | bytes 2359328 | tf_op jit(solution)/shard_map/ppermute | solution.py:80
  159.9 1.4 copy-done.8
  161.3 14.2 %down.1 = (f32[1024,768]{1,0:T(8,128)}, f32[1024,768]{1,0:T(8,128)}, bf16[1024,768]{1,0:T(8,128)(2,1)}, f32[8,768]{1,0:T(8,128)}) custom-call(s32[1]{0:T(128)} %bitcast.core_ref, bf16[1024,3072]{1,0:T(8,128)(2,1)} %get-tuple-element.54.x_ref.left_ref, f32[1024,768]{1,0:T(8,128)} %get-tuple-element.55.sum_ref, bf16[1024,768]{1,0:T(8,128)(2,1)} %bitcast.105, ...), custom_call_target="tpu_custom_call" | custom-call | tf_op jit(solution)/shard_map/down/pallas_call | solution.py:440
  175.5 9.2 %weight_columns.2 = (bf16[3072,384]{1,0:T(8,128)(2,1)}, bf16[3072,384]{1,0:T(8,128)(2,1)}) custom-call(s32[1]{0:T(128)} %bitcast.core_ref, bf16[1024,3072]{1,0:T(8,128)(2,1)} %get-tuple-element.54.x_ref.left_ref, bf16[1,1024,768]{2,1,0:T(8,128)(2,1)} %bitcast.98, bf16[1,1024,768]{2,1,0:T(8,128)(2,1)} %bitcast.99), custom_call_target="tpu_custom_call" | custom-call | tf_op jit(solution)/shard_map/weight_columns/pallas_call | solution.py:599
  184.9 4.5 %collective-permute-done.14 = bf16[3072,384]{1,0:T(8,128)(2,1)S(1)} collective-permute-done((bf16[3072,384]{1,0:T(8,128)(2,1)}, bf16[3072,384]{1,0:T(8,128)(2,1)S(1)}, u32[]{:S(2)}, u32[]{:S(2)}) %collective-permute-start.14) | collective-permute-done | bytes 2359328 | tf_op jit(solution)/shard_map/ppermute | solution.py:80
  189.4 3.6 add_convert_fusion.1
  193.4 22.8 %inner_back.1 = (bf16[1024,3072]{1,0:T(8,128)(2,1)}, f32[1024,768]{1,0:T(8,128)}, bf16[1024,768]{1,0:T(8,128)(2,1)}, bf16[1024,768]{1,0:T(8,128)(2,1)}, f32[8,768]{1,0:T(8,128)}) custom-call(s32[1]{0:T(128)} %bitcast.core_ref, bf16[1024,768]{1,0:T(8,128)(2,1)} %get-tuple-element.62.low_ref, f32[1024,768]{1,0:T(8,128)} %get-tuple-element.63.delta_ref, ...), custom_call_target="tpu_custom_call" | custom-call | tf_op jit(solution)/shard_map/inner_back/pallas_call | solution.py:530
  216.2 10.0 %weight_wide.1 = (bf16[768,1920]{1,0:T(8,128)(2,1)}, bf16[768,1920]{1,0:T(8,128)(2,1)}) custom-call(s32[1]{0:T(128)} %bitcast.core_ref, bf16[1024,768]{1,0:T(8,128)(2,1)} %get-tuple-element.51.x_ref.left_ref, bf16[1024,3072]{1,0:T(8,128)(2,1)} %get-tuple-element.68.right_ref), custom_call_target="tpu_custom_call" | custom-call | tf_op jit(solution)/shard_map/weight_wide/pallas_call | solution.py:628
  226.2 4.3 %weight_into.1 = (bf16[768,1920]{1,0:T(8,128)(2,1)}, bf16[768,1920]{1,0:T(8,128)(2,1)}) custom-call(s32[1]{0:T(128)} %bitcast.core_ref, bf16[1024,768]{1,0:T(8,128)(2,1)} %bitcast.97, bf16[1024,768]{1,0:T(8,128)(2,1)} %get-tuple-element.67.own_ref.other_ref, ...), custom_call_target="tpu_custom_call", output_to_operand_aliasing={{0}: (4, {}), {1}: (5, {})} | custom-call | tf_op jit(solution)/shard_map/weight_into/pallas_call | solution.py:576
  230.8 5.3 %collective-permute-done.15 = bf16[768,1920]{1,0:T(8,128)(2,1)S(1)} collective-permute-done((bf16[768,1920]{1,0:T(8,128)(2,1)}, bf16[768,1920]{1,0:T(8,128)(2,1)S(1)}, u32[]{:S(2)}, u32[]{:S(2)}) %collective-permute-start.15) | collective-permute-done | bytes 2949152 | tf_op jit(solution)/shard_map/ppermute | solution.py:80
  236.1 4.2 %add_convert_fusion = bf16[768,1920]{1,0:T(8,128)(2,1)} fusion(bf16[768,1920]{1,0:T(8,128)(2,1)S(1)} %collective-permute-done.15, bf16[768,1920]{1,0:T(8,128)(2,1)} %get-tuple-element.71), kind=kLoop, calls=%fused_computation | loop fusion | flops 5898240 | bytes 8847360 | tf_op jit(solution)/shard_map/convert_element_type | solution.py:125
  240.3 18.9 %attend_back.1 = bf16[3,2,512,768]{3,2,1,0:T(8,128)(2,1)} custom-call(s32[1]{0:T(128)} %bitcast.core_ref, bf16[2,512,2304]{2,1,0:T(8,128)(2,1)} %bitcast.86, bf16[2,512,2304]{2,1,0:T(8,128)(2,1)} %bitcast.87, bf16[2,512,2304]{2,1,0:T(8,128)(2,1)} %bitcast.88, bf16[2,12,512,512]{3,2,1,0:T(8,128)(2,1)} %get-tuple-element.66.share_ref, ...), custom_call_target="tpu_custom_call" | custom-call | tf_op jit(solution)/shard_map/attend_back/pallas_call | solution.py:273
  259.1 7.6 %weight_columns.3 = (bf16[768,1152]{1,0:T(8,128)(2,1)}, bf16[768,1152]{1,0:T(8,128)(2,1)}) custom-call(s32[1]{0:T(128)} %bitcast.core_ref, bf16[1024,768]{1,0:T(8,128)(2,1)} %bitcast_convert_fusion.1.x_ref.left_ref, bf16[3,1024,768]{2,1,0:T(8,128)(2,1)} %bitcast.89, bf16[3,1024,768]{2,1,0:T(8,128)(2,1)} %bitcast.90), custom_call_target="tpu_custom_call" | custom-call | tf_op jit(solution)/shard_map/weight_columns/pallas_call | solution.py:599
  268.6 2.1 collective-permute-done.16
  270.7 1.2 copy-done.9
  271.9 2.5 add_convert_fusion.2
  275.4 9.8 %joined_back.1 = f32[1024,768]{1,0:T(8,128)} custom-call(s32[1]{0:T(128)} %bitcast.core_ref, f32[1024,768]{1,0:T(8,128)} %get-tuple-element.65.one_ref, bf16[3,1024,768]{2,1,0:T(8,128)(2,1)} %bitcast.91, bf16[3,1024,768]{2,1,0:T(8,128)(2,1)} %bitcast.92, bf16[768,1536]{1,0:T(8,128)(2,1)} %all-gather.3.cloned.1.call-done.own_ref.merge_own_ref, ...), custom_call_target="tpu_custom_call" | custom-call | tf_op jit(solution)/shard_map/joined_back/pallas_call | solution.py:668
  285.2 4.3 %multiply_reduce_fusion = (f32[768]{0:T(1024)S(1)}, f32[768]{0:T(1024)S(1)}, f32[2,128,768]{2,1,0:T(8,128)}) fusion(f32[2,128,768]{2,1,0:T(8,128)S(1)} %copy-done.7, f32[768]{0:T(1024)S(1)} %copy-done.23, f32[768]{0:T(1024)S(1)} %copy-done.25, f32[2,512,768]{2,1,0:T(8,128)} %bitcast.94, s32[2,512]{1,0:T(2,128)S(1)} %copy-done.21), kind=kOutput, calls=%fused_computation.20 | convolution fusion | flops 1209072128 | bytes 4734976 | tf_op jit(solution)/shard_map/drs,drc->dsc/dot_general | solution.py:835
  291.9 2.8 collective-permute-done.18
  294.7 1.5 collective-permute-start.19
  296.2 2.4 collective-permute-done.19
  299.6 2.8 collective-permute-done.20
  302.5 1.5 collective-permute-start.25
  304.0 1.2 collective-permute-start.33
  305.2 1.9 collective-permute-done.21
  307.2 1.4 multiply_convert_fusion
  310.4 1.3 copy-done.4
  311.8 3.2 convolution_add_fusion
  315.0 11.6 %collective-permute-done.25 = bf16[4,96,1152]{2,1,0:T(8,128)(2,1)} collective-permute-done((bf16[4,96,1152]{2,1,0:T(8,128)(2,1)}, bf16[4,96,1152]{2,1,0:T(8,128)(2,1)}, u32[]{:S(2)}, u32[]{:S(2)}) %collective-permute-start.25) | collective-permute-done | bytes 884768 | tf_op jit(solution)/shard_map/ppermute | solution.py:80
  326.6 1.4 fusion
  329.2 2.1 collective-permute-start.27
  331.3 1.8 collective-permute-start.28
  334.1 3.5 all-to-all-start.1
  337.6 5.3 %collective-permute-done.26 = bf16[96,1152]{1,0:T(8,128)(2,1)S(1)} collective-permute-done((bf16[96,1152]{1,0:T(8,128)(2,1)S(1)}, bf16[96,1152]{1,0:T(8,128)(2,1)S(1)}, u32[]{:S(2)}, u32[]{:S(2)}) %collective-permute-start.26) | collective-permute-done | bytes 221216 | tf_op jit(solution)/shard_map/ppermute | solution.py:160
  342.9 12.8 %collective-permute-done.27 = bf16[96,1152]{1,0:T(8,128)(2,1)S(1)} collective-permute-done((bf16[96,1152]{1,0:T(8,128)(2,1)S(1)}, bf16[96,1152]{1,0:T(8,128)(2,1)S(1)}, u32[]{:S(2)}, u32[]{:S(2)}) %collective-permute-start.27) | collective-permute-done | bytes 221216 | tf_op jit(solution)/shard_map/ppermute | solution.py:160
  355.8 1.4 collective-permute-start.29
  359.1 3.6 collective-permute-done.29
  363.4 1.1 fusion.9
  364.7 8.0 %all-to-all-done.1 = bf16[8,96,384]{2,1,0:T(8,128)(2,1)S(1)} async-done(((bf16[8,96,384]{2,1,0:T(8,128)(2,1)}), bf16[8,96,384]{2,1,0:T(8,128)(2,1)S(1)}, u32[]{:S(2)}, u32[]{:S(2)}) %all-to-all-start.1) | async-done | bytes 589856 | tf_op jit(solution)/shard_map/all_to_all | solution.py:140
  372.8 1.5 collective-permute-start.23
  374.5 2.7 collective-permute-done.23
  379.6 1.2 fusion.8
  (220 shorter events, 38.8 us)
Async XLA Ops:
  7.2 12.5 %copy-start = (bf16[384,768]{1,0:T(8,128)(2,1)S(1)}, bf16[384,768]{1,0:T(8,128)(2,1)}, u32[]{:S(2)}) copy-start(bf16[384,768]{1,0:T(8,128)(2,1)} %param.25) | copy-start | bytes 1769476
  7.2 2.8 copy-start.34
  7.2 2.8 copy-start.35
  7.2 2.8 copy-start.36
  7.2 2.8 copy-start.37
  7.2 2.8 copy-start.38
  7.3 3.0 copy-start.28
  7.3 76.8 %all-gather.3.cloned.1.call-start = ((), (), s32[]{:S(2)}) async-start(), calls=%async_computation.4 | async-start | bytes 2654208 | tf_op jit(solution)/shard_map/all_gather | solution.py:113
  10.0 10.4 %copy-start.21 = (s32[2,512]{1,0:T(2,128)S(1)}, s32[2,512]{1,0:T(2,128)}, u32[]{:S(2)}) copy-start(s32[2,512]{1,0:T(2,128)} %param.29) | copy-start | bytes 12292
  10.0 10.6 %copy-start.10 = (bf16[2,512,768]{2,1,0:T(8,128)(2,1)S(1)}, bf16[2,512,768]{2,1,0:T(8,128)(2,1)}, u32[]{:S(2)}) copy-start(bf16[2,512,768]{2,1,0:T(8,128)(2,1)} %param.16) | copy-start | bytes 4718596
  11.2 34.8 %all-to-all-start = ((bf16[8,112,384]{2,1,0:T(8,128)(2,1)}), bf16[8,112,384]{2,1,0:T(8,128)(2,1)S(1)}, u32[]{:S(2)}, u32[]{:S(2)}) async-start(bf16[8,112,384]{2,1,0:T(8,128)(2,1)} %broadcast_in_dim.39), calls=%async_computation | async-start | bytes 1376256 | tf_op jit(solution)/shard_map/all_to_all | solution.py:75
  18.5 136.6 %all-gather.5.cloned.1.call-start = ((), (), s32[]{:S(2)}) async-start(), calls=%async_computation.5 | async-start | bytes 2654208 | tf_op jit(solution)/shard_map/all_gather | solution.py:113
  20.7 25.3 %copy-start.40 = (s32[2]{0:T(128)S(1)}, s32[2]{0:T(128)}, u32[]{:S(2)}) copy-start(s32[2]{0:T(128)} %param.28) | copy-start | bytes 28
  21.3 30.2 %copy-start.15 = (bf16[2,128,768]{2,1,0:T(8,128)(2,1)}, bf16[2,128,768]{2,1,0:T(8,128)(2,1)S(1)}, u32[]{:S(2)}) copy-start(bf16[2,128,768]{2,1,0:T(8,128)(2,1)S(1)} %fusion.1) | copy-start | bytes 1179652
  46.0 5.4 %collective-permute-start = (bf16[8,112,384]{2,1,0:T(8,128)(2,1)S(1)}, bf16[8,112,384]{2,1,0:T(8,128)(2,1)S(1)}, u32[]{:S(2)}, u32[]{:S(2)}) collective-permute-start(bf16[8,112,384]{2,1,0:T(8,128)(2,1)S(1)} %all-to-all-done), channel_id=1, source_target_pairs={{0,8},{8,0},{16,24},{24,16},{1,9},{9,1},{17,25},{25,17},{2,10},{10... | collective-permute-start | bytes 2064392 | tf_op jit(solution)/shard_map/ppermute | solution.py:80
  47.4 5.0 %copy-start.29 = (f32[2,128]{1,0:T(2,128)}, f32[2,128]{1,0:T(2,128)S(1)}, u32[]{:S(2)}) copy-start(f32[2,128]{1,0:T(2,128)S(1)} %compare_convert_fusion) | copy-start | bytes 3076
  47.4 13.9 %collective-permute-start.6 = (bf16[96,768]{1,0:T(8,128)(2,1)S(1)}, bf16[96,768]{1,0:T(8,128)(2,1)S(1)}, u32[]{:S(2)}, u32[]{:S(2)}) collective-permute-start(bf16[96,768]{1,0:T(8,128)(2,1)S(1)} %constant_dynamic-slice_fusion.5), channel_id=1, source_target_pairs={{0,2},{1,3},{2,4},{3,5},{4,6},{5,7},{6,0},{7,1},{8,10},{9,11},{10,... | collective-permute-start | bytes 442376 | tf_op jit(solution)/shard_map/ppermute | solution.py:95
  47.7 20.9 %collective-permute-start.7 = (bf16[96,768]{1,0:T(8,128)(2,1)S(1)}, bf16[96,768]{1,0:T(8,128)(2,1)S(1)}, u32[]{:S(2)}, u32[]{:S(2)}) collective-permute-start(bf16[96,768]{1,0:T(8,128)(2,1)S(1)} %constant_dynamic-slice_fusion.5), channel_id=1, source_target_pairs={{0,4},{1,5},{2,6},{3,7},{4,0},{5,1},{6,2},{7,3},{8,12},{9,13},{10,... | collective-permute-start | bytes 442376 | tf_op jit(solution)/shard_map/ppermute | solution.py:95
  49.1 23.4 %collective-permute-start.8 = (bf16[96,768]{1,0:T(8,128)(2,1)S(1)}, bf16[96,768]{1,0:T(8,128)(2,1)S(1)}, u32[]{:S(2)}, u32[]{:S(2)}) collective-permute-start(bf16[96,768]{1,0:T(8,128)(2,1)S(1)} %constant_dynamic-slice_fusion.5), channel_id=1, source_target_pairs={{0,6},{1,7},{2,0},{3,1},{4,2},{5,3},{6,4},{7,5},{8,14},{9,15},{10,... | collective-permute-start | bytes 442376 | tf_op jit(solution)/shard_map/ppermute | solution.py:95
  53.4 1.2 collective-permute-start.1
  53.6 27.2 %copy-start.19 = (f32[8,6,96]{2,1,0:T(8,128)}, f32[8,6,96]{2,1,0:T(8,128)S(1)}, u32[]{:S(2)}) copy-start(f32[8,6,96]{2,1,0:T(8,128)S(1)} %reshape.426) | copy-start | bytes 55300
  55.3 3.8 collective-permute-start.2
  58.3 245.8 %reduce-scatter.5.cloned.1.call-start = ((), (), s32[]{:S(2)}) async-start(), calls=%async_computation.7 | async-start | bytes 2654208 | tf_op jit(solution)/shard_map/reduce_scatter | solution.py:813
  59.7 4.0 %collective-permute-start.3 = (f32[3,768]{1,0:T(4,128)S(1)}, f32[3,768]{1,0:T(4,128)S(1)}, u32[]{:S(2)}, u32[]{:S(2)}) collective-permute-start(f32[3,768]{1,0:T(4,128)S(1)} %pad_maximum_fusion.5), channel_id=1, source_target_pairs={{0,1},{1,0},{2,3},{3,2},{4,5},{5,4},{6,7},{7,6},{8,9},{9,8},{10,11... | collective-permute-start | bytes 27656 | tf_op jit(solution)/shard_map/ppermute | solution.py:80
  64.4 4.6 %collective-permute-start.4 = (f32[3,768]{1,0:T(4,128)S(1)}, f32[3,768]{1,0:T(4,128)S(1)}, u32[]{:S(2)}, u32[]{:S(2)}) collective-permute-start(f32[3,768]{1,0:T(4,128)S(1)} %pad_maximum_fusion.6), channel_id=1, source_target_pairs={{0,2},{1,3},{2,0},{3,1},{4,6},{5,7},{6,4},{7,5},{8,10},{9,11},{10,... | collective-permute-start | bytes 27656 | tf_op jit(solution)/shard_map/ppermute | solution.py:80
  69.7 10.5 %collective-permute-start.5 = (f32[3,768]{1,0:T(4,128)S(1)}, f32[3,768]{1,0:T(4,128)S(1)}, u32[]{:S(2)}, u32[]{:S(2)}) collective-permute-start(f32[3,768]{1,0:T(4,128)S(1)} %pad_maximum_fusion.7), channel_id=1, source_target_pairs={{0,4},{1,5},{2,6},{3,7},{4,0},{5,1},{6,2},{7,3},{8,12},{9,13},{10,... | collective-permute-start | bytes 27656 | tf_op jit(solution)/shard_map/ppermute | solution.py:80
  72.6 18.2 %collective-permute-start.9 = (bf16[4,96,768]{2,1,0:T(8,128)(2,1)S(1)}, bf16[4,96,768]{2,1,0:T(8,128)(2,1)S(1)}, u32[]{:S(2)}, u32[]{:S(2)}) collective-permute-start(bf16[4,96,768]{2,1,0:T(8,128)(2,1)S(1)} %bitcast_dynamic-update-slice_fusion), channel_id=1, source_target_pairs={{0,1},{1,0},{2,3},{3,2},{4,5},{5,4},{6,7},{7,6},{8,9},{9,8},{10,11... | collective-permute-start | bytes 1769480 | tf_op jit(solution)/shard_map/ppermute | solution.py:80
  84.1 9.9 %collective-permute-start.10 = (bf16[768,1536]{1,0:T(8,128)(2,1)}, bf16[768,1536]{1,0:T(8,128)(2,1)S(1)}, u32[]{:S(2)}, u32[]{:S(2)}) collective-permute-start(bf16[768,1536]{1,0:T(8,128)(2,1)} %all-gather.3.cloned.1.call-done.own_ref.merge_own_ref), channel_id=1, source_target_pairs={{0,8},{8,0},{16,24},{24,16},{1,9},{9,1},{17,25},{25,17},{2,10},{10... | collective-permute-start | bytes 7077896 | tf_op jit(solution)/shard_map/ppermute | solution.py:80
  91.9 28.9 %collective-permute-start.11 = (bf16[768,768]{1,0:T(8,128)(2,1)}, bf16[768,768]{1,0:T(8,128)(2,1)}, u32[]{:S(2)}, u32[]{:S(2)}) collective-permute-start(bf16[768,768]{1,0:T(8,128)(2,1)} %bitcast.18), channel_id=1, source_target_pairs={{0,16},{8,24},{16,0},{24,8},{1,17},{9,25},{17,1},{25,9},{2,18},{10... | collective-permute-start | bytes 3538952 | tf_op jit(solution)/shard_map/ppermute | solution.py:80
  120.8 3.2 copy-start.20
  123.7 8.4 %copy-start.5 = (bf16[768,1536]{1,0:T(8,128)(2,1)}, bf16[768,1536]{1,0:T(8,128)(2,1)S(1)}, u32[]{:S(2)}) copy-start(bf16[768,1536]{1,0:T(8,128)(2,1)S(1)} %maximum_select_fusion.own_ref.up_own_ref) | copy-start | bytes 7077892
  123.8 8.4 %collective-permute-start.12 = (bf16[768,1536]{1,0:T(8,128)(2,1)S(1)}, bf16[768,1536]{1,0:T(8,128)(2,1)}, u32[]{:S(2)}, u32[]{:S(2)}) collective-permute-start(bf16[768,1536]{1,0:T(8,128)(2,1)S(1)} %maximum_select_fusion.own_ref.up_own_ref), channel_id=1, source_target_pairs={{0,8},{8,0},{16,24},{24,16},{1,9},{9,1},{17,25},{25,17},{2,10},{10... | collective-permute-start | bytes 7077896 | tf_op jit(solution)/shard_map/ppermute | solution.py:80
  155.1 4.7 %collective-permute-start.13 = (bf16[3072,384]{1,0:T(8,128)(2,1)}, bf16[3072,384]{1,0:T(8,128)(2,1)S(1)}, u32[]{:S(2)}, u32[]{:S(2)}) collective-permute-start(bf16[3072,384]{1,0:T(8,128)(2,1)} %all-gather.5.cloned.1.call-done.own_ref.down_own_ref), channel_id=1, source_target_pairs={{0,8},{8,0},{16,24},{24,16},{1,9},{9,1},{17,25},{25,17},{2,10},{10... | collective-permute-start | bytes 7077896 | tf_op jit(solution)/shard_map/ppermute | solution.py:80
  184.7 4.7 %collective-permute-start.14 = (bf16[3072,384]{1,0:T(8,128)(2,1)}, bf16[3072,384]{1,0:T(8,128)(2,1)S(1)}, u32[]{:S(2)}, u32[]{:S(2)}) collective-permute-start(bf16[3072,384]{1,0:T(8,128)(2,1)} %get-tuple-element.61), channel_id=1, source_target_pairs={{0,8},{8,0},{16,24},{24,16},{1,9},{9,1},{17,25},{25,17},{2,10},{10... | collective-permute-start | bytes 7077896 | tf_op jit(solution)/shard_map/ppermute | solution.py:80
  193.1 165.3 %reduce-scatter.3.cloned.1.call-start = ((), (), s32[]{:S(2)}) async-start(), calls=%async_computation.6 | async-start | bytes 3317760 | tf_op jit(solution)/shard_map/reduce_scatter | solution.py:823
  230.5 5.6 %collective-permute-start.15 = (bf16[768,1920]{1,0:T(8,128)(2,1)}, bf16[768,1920]{1,0:T(8,128)(2,1)S(1)}, u32[]{:S(2)}, u32[]{:S(2)}) collective-permute-start(bf16[768,1920]{1,0:T(8,128)(2,1)} %get-tuple-element.72), channel_id=1, source_target_pairs={{0,8},{8,0},{16,24},{24,16},{1,9},{9,1},{17,25},{25,17},{2,10},{10... | collective-permute-start | bytes 8847368 | tf_op jit(solution)/shard_map/ppermute | solution.py:80
  266.8 3.9 %collective-permute-start.16 = (bf16[768,1152]{1,0:T(8,128)(2,1)}, bf16[768,1152]{1,0:T(8,128)(2,1)S(1)}, u32[]{:S(2)}, u32[]{:S(2)}) collective-permute-start(bf16[768,1152]{1,0:T(8,128)(2,1)} %get-tuple-element.76), channel_id=1, source_target_pairs={{0,8},{8,0},{16,24},{24,16},{1,9},{9,1},{17,25},{25,17},{2,10},{10... | collective-permute-start | bytes 5308424 | tf_op jit(solution)/shard_map/ppermute | solution.py:80
  275.4 9.8 %copy-start.7 = (f32[2,128,768]{2,1,0:T(8,128)S(1)}, f32[2,128,768]{2,1,0:T(8,128)}, u32[]{:S(2)}) copy-start(f32[2,128,768]{2,1,0:T(8,128)} %copy-done.6) | copy-start | bytes 2359300
  275.4 9.8 %copy-start.23 = (f32[768]{0:T(1024)S(1)}, f32[768]{0:T(1024)}, u32[]{:S(2)}) copy-start(f32[768]{0:T(1024)} %copy-done.22) | copy-start | bytes 9220
  275.4 9.8 %copy-start.25 = (f32[768]{0:T(1024)S(1)}, f32[768]{0:T(1024)}, u32[]{:S(2)}) copy-start(f32[768]{0:T(1024)} %copy-done.24) | copy-start | bytes 9220
  285.1 22.0 %copy-start.26 = (f32[768]{0:T(1024)S(1)}, f32[768]{0:T(1024)}, u32[]{:S(2)}) copy-start(f32[768]{0:T(1024)} %mul.216) | copy-start | bytes 9220
  285.2 22.0 %copy-start.30 = (f32[2,128]{1,0:T(2,128)S(1)}, f32[2,128]{1,0:T(2,128)}, u32[]{:S(2)}) copy-start(f32[2,128]{1,0:T(2,128)} %copy-done.29) | copy-start | bytes 3076
  289.5 19.1 %copy-start.16 = (bf16[2,128,768]{2,1,0:T(8,128)(2,1)S(1)}, bf16[2,128,768]{2,1,0:T(8,128)(2,1)}, u32[]{:S(2)}) copy-start(bf16[2,128,768]{2,1,0:T(8,128)(2,1)} %copy-done.15) | copy-start | bytes 1179652
  289.5 1.3 collective-permute-start.17
  290.8 3.9 %collective-permute-start.18 = (f32[6,768]{1,0:T(8,128)S(1)}, f32[6,768]{1,0:T(8,128)S(1)}, u32[]{:S(2)}, u32[]{:S(2)}) collective-permute-start(f32[6,768]{1,0:T(8,128)S(1)} %fusion.30), channel_id=1, source_target_pairs={{0,16},{8,24},{16,0},{24,8},{1,17},{9,25},{17,1},{25,9},{2,18},{10... | collective-permute-start | bytes 55304 | tf_op jit(solution)/shard_map/ppermute | solution.py:80
  294.7 3.9 collective-permute-start.19
  298.6 3.8 collective-permute-start.20
  302.4 4.7 %collective-permute-start.21 = (f32[6,768]{1,0:T(8,128)S(1)}, f32[6,768]{1,0:T(8,128)S(1)}, u32[]{:S(2)}, u32[]{:S(2)}) collective-permute-start(f32[6,768]{1,0:T(8,128)S(1)} %add.603), channel_id=1, source_target_pairs={{0,4},{1,5},{2,6},{3,7},{4,0},{5,1},{6,2},{7,3},{8,12},{9,13},{10,... | collective-permute-start | bytes 55304 | tf_op jit(solution)/shard_map/ppermute | solution.py:80
  302.5 24.2 %collective-permute-start.25 = (bf16[4,96,1152]{2,1,0:T(8,128)(2,1)}, bf16[4,96,1152]{2,1,0:T(8,128)(2,1)}, u32[]{:S(2)}, u32[]{:S(2)}) collective-permute-start(bf16[4,96,1152]{2,1,0:T(8,128)(2,1)} %dynamic-slice_bitcast_fusion), channel_id=1, source_target_pairs={{0,1},{1,0},{2,3},{3,2},{4,5},{5,4},{6,7},{7,6},{8,9},{9,8},{10,11... | collective-permute-start | bytes 2654216 | tf_op jit(solution)/shard_map/ppermute | solution.py:80
  304.0 53.3 %collective-permute-start.33 = (bf16[384,384]{1,0:T(8,128)(2,1)}, bf16[384,384]{1,0:T(8,128)(2,1)}, u32[]{:S(2)}, u32[]{:S(2)}) collective-permute-start(bf16[384,384]{1,0:T(8,128)(2,1)} %reduce-scatter.5.cloned.1.call-done), channel_id=1, source_target_pairs={{0,16},{8,24},{16,0},{24,8},{1,17},{9,25},{17,1},{25,9},{2,18},{10... | collective-permute-start | bytes 884744 | tf_op jit(solution)/shard_map/ppermute | solution.py:80
  309.2 23.9 %collective-permute-start.22 = (bf16[768,384]{1,0:T(8,128)(2,1)S(1)}, bf16[768,384]{1,0:T(8,128)(2,1)S(1)}, u32[]{:S(2)}, u32[]{:S(2)}) collective-permute-start(bf16[768,384]{1,0:T(8,128)(2,1)S(1)} %constant_dynamic-slice_fusion.1), channel_id=1, source_target_pairs={{0,8},{8,0},{16,24},{24,16},{1,9},{9,1},{17,25},{25,17},{2,10},{10... | collective-permute-start | bytes 1769480 | tf_op jit(solution)/shard_map/ppermute | solution.py:80
  328.1 14.8 %collective-permute-start.26 = (bf16[96,1152]{1,0:T(8,128)(2,1)S(1)}, bf16[96,1152]{1,0:T(8,128)(2,1)S(1)}, u32[]{:S(2)}, u32[]{:S(2)}) collective-permute-start(bf16[96,1152]{1,0:T(8,128)(2,1)S(1)} %get-tuple-element.120), channel_id=1, source_target_pairs={{0,2},{1,3},{2,4},{3,5},{4,6},{5,7},{6,0},{7,1},{8,10},{9,11},{10,... | collective-permute-start | bytes 663560 | tf_op jit(solution)/shard_map/ppermute | solution.py:160
  329.2 26.5 %collective-permute-start.27 = (bf16[96,1152]{1,0:T(8,128)(2,1)S(1)}, bf16[96,1152]{1,0:T(8,128)(2,1)S(1)}, u32[]{:S(2)}, u32[]{:S(2)}) collective-permute-start(bf16[96,1152]{1,0:T(8,128)(2,1)S(1)} %get-tuple-element.122), channel_id=1, source_target_pairs={{0,4},{1,5},{2,6},{3,7},{4,0},{5,1},{6,2},{7,3},{8,12},{9,13},{10,... | collective-permute-start | bytes 663560 | tf_op jit(solution)/shard_map/ppermute | solution.py:160
  331.3 26.0 %copy-start.18 = (bf16[384,384]{1,0:T(8,128)(2,1)S(1)}, bf16[384,384]{1,0:T(8,128)(2,1)}, u32[]{:S(2)}) copy-start(bf16[384,384]{1,0:T(8,128)(2,1)} %reduce-scatter.5.cloned.1.call-done) | copy-start | bytes 884740
  331.3 24.4 %collective-permute-start.28 = (bf16[96,1152]{1,0:T(8,128)(2,1)S(1)}, bf16[96,1152]{1,0:T(8,128)(2,1)S(1)}, u32[]{:S(2)}, u32[]{:S(2)}) collective-permute-start(bf16[96,1152]{1,0:T(8,128)(2,1)S(1)} %get-tuple-element.121), channel_id=1, source_target_pairs={{0,6},{1,7},{2,0},{3,1},{4,2},{5,3},{6,4},{7,5},{8,14},{9,15},{10,... | collective-permute-start | bytes 663560 | tf_op jit(solution)/shard_map/ppermute | solution.py:160
  334.1 38.6 %all-to-all-start.1 = ((bf16[8,96,384]{2,1,0:T(8,128)(2,1)}), bf16[8,96,384]{2,1,0:T(8,128)(2,1)S(1)}, u32[]{:S(2)}, u32[]{:S(2)}) async-start(bf16[8,96,384]{2,1,0:T(8,128)(2,1)} %bitcast.30), calls=%async_computation.1 | async-start | bytes 1179648 | tf_op jit(solution)/shard_map/all_to_all | solution.py:140
  355.8 6.9 %collective-permute-start.29 = (bf16[96,1152]{1,0:T(8,128)(2,1)S(1)}, bf16[96,1152]{1,0:T(8,128)(2,1)S(1)}, u32[]{:S(2)}, u32[]{:S(2)}) collective-permute-start(bf16[96,1152]{1,0:T(8,128)(2,1)S(1)} %fusion.13), channel_id=1, source_target_pairs={{0,16},{8,24},{16,0},{24,8},{1,17},{9,25},{17,1},{25,9},{2,18},{10... | collective-permute-start | bytes 663560 | tf_op jit(solution)/shard_map/ppermute | solution.py:80
  358.3 5.1 %collective-permute-start.34 = (bf16[384,384]{1,0:T(8,128)(2,1)S(1)}, bf16[384,384]{1,0:T(8,128)(2,1)S(1)}, u32[]{:S(2)}, u32[]{:S(2)}) collective-permute-start(bf16[384,384]{1,0:T(8,128)(2,1)S(1)} %add_convert_fusion.6), channel_id=1, source_target_pairs={{0,8},{8,0},{16,24},{24,16},{1,9},{9,1},{17,25},{25,17},{2,10},{10... | collective-permute-start | bytes 884744 | tf_op jit(solution)/shard_map/ppermute | solution.py:80
  358.4 15.9 %collective-permute-start.31 = (bf16[96,1920]{1,0:T(8,128)(2,1)}, bf16[96,1920]{1,0:T(8,128)(2,1)S(1)}, u32[]{:S(2)}, u32[]{:S(2)}) collective-permute-start(bf16[96,1920]{1,0:T(8,128)(2,1)} %reduce-scatter.3.cloned.1.call-done), channel_id=1, source_target_pairs={{0,16},{8,24},{16,0},{24,8},{1,17},{9,25},{17,1},{25,9},{2,18},{10... | collective-permute-start | bytes 1105928 | tf_op jit(solution)/shard_map/ppermute | solution.py:80
  362.8 11.5 %copy-start.17 = (bf16[96,1920]{1,0:T(8,128)(2,1)S(1)}, bf16[96,1920]{1,0:T(8,128)(2,1)}, u32[]{:S(2)}) copy-start(bf16[96,1920]{1,0:T(8,128)(2,1)} %reduce-scatter.3.cloned.1.call-done) | copy-start | bytes 1105924
  362.8 1.8 collective-permute-start.30
  372.8 4.4 %collective-permute-start.23 = (bf16[96,384]{1,0:T(8,128)(2,1)S(1)}, bf16[96,384]{1,0:T(8,128)(2,1)S(1)}, u32[]{:S(2)}, u32[]{:S(2)}) collective-permute-start(bf16[96,384]{1,0:T(8,128)(2,1)S(1)} %reduce_sum.72), channel_id=1, source_target_pairs={{0,16},{8,24},{16,0},{24,8},{1,17},{9,25},{17,1},{25,9},{2,18},{10... | collective-permute-start | bytes 221192 | tf_op jit(solution)/shard_map/ppermute | solution.py:80
  374.4 5.2 %collective-permute-start.32 = (bf16[96,1920]{1,0:T(8,128)(2,1)S(1)}, bf16[96,1920]{1,0:T(8,128)(2,1)S(1)}, u32[]{:S(2)}, u32[]{:S(2)}) collective-permute-start(bf16[96,1920]{1,0:T(8,128)(2,1)S(1)} %add_convert_fusion.5), channel_id=1, source_target_pairs={{0,8},{8,0},{16,24},{24,16},{1,9},{9,1},{17,25},{25,17},{2,10},{10... | collective-permute-start | bytes 1105928 | tf_op jit(solution)/shard_map/ppermute | solution.py:80
  377.2 1.6 collective-permute-start.24
  (18 other events, 26.5 us)
Sparse Core Ops, SparseCore 0:
  10.9 73.2 all-gather.2
  86.9 50.2 all-gather.4
  193.2 66.7 reduce-scatter.4
  267.2 89.8 reduce-scatter.2
